TPU v7x, 128 devices: a whole 4x4x4 slice. The times are simulated.
128 devices in a mesh: isl: 4 (over z_hi, core), fsdp: 32 (over x, z_lo, y).
Axes of the slice: x: 4, y: 4, z: 4 (z_hi: 2, z_lo: 2; z = z_hi * 2 + z_lo), core: 2. Of those that a mesh axis runs over, the one named last changes fastest.
Arguments:
- weights: float32 [3, 7168, 4096], P(None, 'fsdp', 'isl'), may hold values from -6 to 6
- momentum: float32 [3, 7168, 4096], P(None, 'fsdp', 'isl'), may hold values from -0.12 to 0.12
- first_moment: bfloat16 [4, 3, 7168, 4096], P('isl', None, 'fsdp'), may hold values from -0.00029945374 to 0.00029945374
- second_moment: bfloat16 [4, 3, 7168, 4096], P('isl', None, 'fsdp'), may hold values from 9.95351e-09 to 9.953976e-06
- inputs: bfloat16 [2, 1024, 4096], P(None, ('isl', 'fsdp')), may hold values from -6 to 6
- targets: bfloat16 [2, 1024, 4096], P(None, ('isl', 'fsdp')), may hold values from -6 to 6
- overflow_step: int32 [4, 32], P('isl', 'fsdp'), may hold values from 0 to 63
Outputs:
- new_weights: float32 [3, 7168, 4096], P(None, 'fsdp', 'isl')
- new_momentum: float32 [3, 7168, 4096], P(None, 'fsdp', 'isl')
Inputs may be any that keep to these rules, and one draw needn't show every extreme that they name: `overflow_step`: A device reports an overflow at inner step k when its value equals k; values of 2 or more report none.
All inputs are finite; a program needn't handle non-finite values.
Results may differ from a plain program's by a relative error of at most 0.004.
Values may be sent and summed in bfloat16 or wider, within the bound.
No kernel may reach another device: no remote copies, remote signals or barrier semaphores. Data moves between devices by JAX's collectives and lax.ppermute only.
A program may use at most 128 MiB of HBM per device.

v0:
```python
import math

import jax
import jax.numpy as jnp
from jax import lax
from jax.sharding import PartitionSpec as P

D = 4096
FF = 7168


inner_rate = 0.02
beta_first = 0.9
beta_second = 0.95
epsilon = 1e-08
decay_rate = 0.1
outer_rate = 0.7
nesterov_coef = 0.9


def joined_along(parts, dim):
    dims = list(parts.shape[1:])
    dims[dim] *= parts.shape[0]
    return jnp.moveaxis(parts, 0, dim).reshape(dims)


def copy_for_each(shard, axis):
    copies = jnp.broadcast_to(shard, (lax.axis_size(axis), *shard.shape))
    return lax.all_to_all(copies, axis, split_axis=0, concat_axis=0, tiled=True)


def collect(shard, axis, dim):
    return joined_along(copy_for_each(shard, axis), dim)


def taken_together(shard, axis):
    return copy_for_each(shard, axis).sum(axis=0)


def split_up(shard, dim, devices):
    before, after = (shard.shape[:dim], shard.shape[dim + 1 :])
    return jnp.moveaxis(shard.reshape(*before, devices, -1, *after), dim, 0)


def sum_at_owner(shard, axis, dim):
    devices = lax.axis_size(axis)
    parts = lax.all_to_all(split_up(shard, dim, devices), axis, 0, 0, tiled=True)
    return jnp.sum(parts, axis=0)


def silu_parts(preact):
    sigmoid_value = jax.nn.sigmoid(preact)
    return (preact * sigmoid_value, sigmoid_value * (1.0 + preact * (1.0 - sigmoid_value)))


def contract_last(left_side, right_side):
    return lax.dot_general(
        left_side, right_side, (((1,), (1,)), ((), ())), preferred_element_type=jnp.float32
    )


def contract_first(left_side, right_side):
    return lax.dot_general(
        left_side, right_side, (((0,), (0,)), ((), ())), preferred_element_type=jnp.float32
    )


def body(weights, momentum, first_moment, second_moment, inputs, targets, overflow_step):
    island_count = lax.axis_size("isl")
    gathered = collect(weights.astype(jnp.bfloat16), "isl", 2).astype(weights.dtype)
    current = gathered
    moment_one = first_moment[0].astype(jnp.float32)
    moment_two = second_moment[0].astype(jnp.float32)
    inner_count = inputs.shape[0]
    island_tokens = inputs.shape[1] * lax.axis_size("fsdp")
    overflow_marks = (overflow_step.reshape(1) == jnp.arange(inner_count, dtype=jnp.int32)).astype(
        jnp.int32
    )
    overflow_counts = taken_together(overflow_marks, "fsdp")
    all_inputs = lax.all_gather(inputs, "fsdp", axis=1, tiled=True)
    for inner_step in range(inner_count):
        rounded = current.astype(jnp.bfloat16)
        local_inputs = inputs[inner_step]
        local_targets = targets[inner_step]
        every_input = all_inputs[inner_step]
        gate_pre = contract_last(every_input, rounded[0]) / math.sqrt(D)
        up_pre = contract_last(every_input, rounded[1]) / math.sqrt(D)
        activated, slope = silu_parts(gate_pre)
        hidden = (activated * up_pre).astype(jnp.bfloat16)
        partial_value = jnp.dot(hidden, rounded[2], preferred_element_type=jnp.float32)
        summed = sum_at_owner(partial_value, "fsdp", 0)
        outputs = local_inputs.astype(jnp.float32) + summed / math.sqrt(FF)
        own_slopes = ((outputs - local_targets.astype(jnp.float32)) / island_tokens).astype(
            jnp.bfloat16
        )
        slopes = collect(own_slopes, "fsdp", 0)
        hidden_slope = contract_last(slopes, rounded[2]) / math.sqrt(FF)
        gate_slope = (hidden_slope * up_pre * slope).astype(jnp.bfloat16)
        up_slope = (hidden_slope * activated).astype(jnp.bfloat16)
        grad_gate = contract_first(gate_slope, every_input) / math.sqrt(D)
        grad_up = contract_first(up_slope, every_input) / math.sqrt(D)
        grad_down = contract_first(hidden, slopes) / math.sqrt(FF)
        gradient = jnp.stack([grad_gate, grad_up, grad_down])
        overflow_count = overflow_counts[inner_step]
        skipped = overflow_count > 0
        next_one = beta_first * moment_one + (1.0 - beta_first) * gradient
        next_two = beta_second * moment_two + (1.0 - beta_second) * gradient * gradient
        next_weights = current - inner_rate * (
            next_one / (jnp.sqrt(next_two) + epsilon) + decay_rate * current
        )
        current = jnp.where(skipped, current, next_weights)
        moment_one = jnp.where(skipped, moment_one, next_one)
        moment_two = jnp.where(skipped, moment_two, next_two)
    pseudo_term = gathered - current
    pseudo_sum = lax.psum_scatter(
        pseudo_term.astype(jnp.bfloat16), "isl", scatter_dimension=2, tiled=True
    ).astype(jnp.float32)
    outer_delta = pseudo_sum / island_count
    new_momentum = nesterov_coef * momentum + outer_delta
    new_weights = weights - outer_rate * (outer_delta + nesterov_coef * new_momentum)
    return (new_weights, new_momentum)


def solution(mesh):
    in_specs = (
        P(None, "fsdp", "isl"),
        P(None, "fsdp", "isl"),
        P("isl", None, "fsdp", None),
        P("isl", None, "fsdp", None),
        P(None, ("isl", "fsdp"), None),
        P(None, ("isl", "fsdp"), None),
        P("isl", "fsdp"),
    )
    out_specs = (P(None, "fsdp", "isl"), P(None, "fsdp", "isl"))
    return jax.shard_map(body, mesh=mesh, in_specs=in_specs, out_specs=out_specs, check_vma=False)
```

profile of v0, /device:TPU:1, one launch (start us, length us, event | category | flops | bytes accessed | tf_op | source)
XLA Modules:
  0.0 474.0 jit_solution(12137875566399298339)
XLA Ops:
  10.6 96.8 %all_to_all.31 = bf16[4,3,224,1024]{3,2,1,0:T(8,128)(2,1)S(1)} all-to-all(bf16[4,3,224,1024]{3,2,1,0:T(8,128)(2,1)S(1)} %broadcast_in_dim.12), channel_id=1, replica_groups=mesh['isl'=4,'fsdp'=32] {'isl'}, dimensions={0} | all-to-all | bytes 11010048 | tf_op jit(solution)/shard_map/all_to_all | solution.py:29
  107.4 2.9 fusion.66
  114.6 3.1 copy.32
  123.0 26.2 %all-gather.2.cloned.1.call-done = bf16[2,256,4096]{2,1,0:T(8,128)(2,1)} async-done(((bf16[2,8,4096]{2,1,0:T(8,128)(2,1)}), bf16[2,256,4096]{2,1,0:T(8,128)(2,1)}) %all-gather.2.cloned.1.call-update) | async-done | bytes 4194320 | tf_op jit(solution)/shard_map/all_gather | solution.py:80
  149.2 3.1 fusion.34
  152.6 3.1 multiply_convert_fusion.5
  155.8 4.2 fusion.55
  160.0 6.8 %all-to-all-start.2 = ((f32[32,8,4096]{2,1,0:T(8,128)}), f32[32,8,4096]{2,1,0:T(8,128)}, u32[]{:S(2)}, u32[]{:S(2)}) async-start(f32[32,8,4096]{2,1,0:T(8,128)} %fusion.55), calls=%async_computation.2 | async-start | bytes 8388608 | tf_op jit(solution)/shard_map/all_to_all | solution.py:47
  167.5 34.9 %all-to-all-done.2 = f32[32,8,4096]{2,1,0:T(8,128)} async-done(((f32[32,8,4096]{2,1,0:T(8,128)}), f32[32,8,4096]{2,1,0:T(8,128)}, u32[]{:S(2)}, u32[]{:S(2)}) %all-to-all-start.2) | async-done | bytes 4194336 | tf_op jit(solution)/shard_map/all_to_all | solution.py:47
  203.0 9.3 %all-to-all-start.1 = ((s32[32,1,2]{2,1,0:T(1,128)}), s32[32,1,2]{2,1,0:T(1,128)S(1)}, u32[]{:S(2)}, u32[]{:S(2)}) async-start(s32[32,1,2]{2,1,0:T(1,128)} %broadcast_in_dim.13), calls=%async_computation.1 | async-start | bytes 32768 | tf_op jit(solution)/shard_map/all_to_all | solution.py:29
  214.8 5.1 %all-to-all-done.1 = s32[32,1,2]{2,1,0:T(1,128)S(1)} async-done(((s32[32,1,2]{2,1,0:T(1,128)}), s32[32,1,2]{2,1,0:T(1,128)S(1)}, u32[]{:S(2)}, u32[]{:S(2)}) %all-to-all-start.1) | async-done | bytes 288 | tf_op jit(solution)/shard_map/all_to_all | solution.py:29
  221.5 4.9 %all-to-all-start.3 = ((bf16[32,8,4096]{2,1,0:T(8,128)(2,1)}), bf16[32,8,4096]{2,1,0:T(8,128)(2,1)}, u32[]{:S(2)}, u32[]{:S(2)}) async-start(bf16[32,8,4096]{2,1,0:T(8,128)(2,1)} %broadcast_in_dim.14), calls=%async_computation.3 | async-start | bytes 4194304 | tf_op jit(solution)/shard_map/all_to_all | solution.py:29
  229.6 3.9 convert_bitcast_fusion
  233.6 6.5 %copy.39 = f32[4,3,28,8,1024]{4,3,0,2,1:T(8,128)} copy(f32[4,3,28,8,1024]{4,3,2,1,0:T(8,128)S(1)} %convert_bitcast_fusion) | data formatting | bytes 22020096 | tf_op jit(solution)/shard_map/convert_element_type | solution.py:70
  240.1 3.6 all-to-all-done.3
  246.2 4.4 fusion.36
  256.1 11.3 %fusion.65 = bf16[3,224,4096]{2,1,0:T(8,128)(2,1)} fusion(f32[3,224,4096]{2,1,0:T(8,128)S(1)} %bitcast.142, bf16[1,3,224,4096]{3,2,1,0:T(8,128)(2,1)S(1)} %bitcast.148, f32[1,224,4096]{2,1,0:T(8,128)S(1)} %fusion.16, f32[1,224,4096]{2,1,0:T(8,128)S(1)} %fusion.17, f32[1,224,4096]{2,1,0:T(8,128)S(1)} %fusion.18, bf16[1,3,224,4096]{3,2,1,0:T(8,128)(2,1)} %param.9, ...), kind=kLoop, calls=%fused_computation.94 | loop fusion | flops 52297728 | bytes 38535168 | tf_op jit(solution)/shard_map/convert_element_type | solution.py:82
  274.5 32.4 %all_to_all.32 = f32[32,8,4096]{2,1,0:T(8,128)} all-to-all(f32[32,8,4096]{2,1,0:T(8,128)S(1)} %fusion.27), channel_id=1, replica_groups=mesh['isl'=4,'fsdp'=32] {'fsdp'}, dimensions={0} | all-to-all | bytes 8388608 | tf_op jit(solution)/shard_map/all_to_all | solution.py:47
  311.0 4.0 all-to-all-start.5
  315.8 26.2 %all-to-all-done.5 = bf16[32,8,4096]{2,1,0:T(8,128)(2,1)S(1)} async-done(((bf16[32,8,4096]{2,1,0:T(8,128)(2,1)}), bf16[32,8,4096]{2,1,0:T(8,128)(2,1)S(1)}, u32[]{:S(2)}, u32[]{:S(2)}) %all-to-all-start.5) | async-done | bytes 2097184 | tf_op jit(solution)/shard_map/all_to_all | solution.py:29
  347.1 5.0 %fusion.14 = f32[1,224,4096]{2,1,0:T(8,128)} fusion(bf16[2,256,4096]{2,1,0:T(8,128)(2,1)} %all-gather.2.cloned.1.call-done, f32[256,224]{0,1:T(8,128)S(1)} %fusion.43, f32[256,224]{0,1:T(8,128)S(1)} %fusion.40), kind=kOutput, calls=%fused_computation.27 | convolution fusion | flops 471023616 | bytes 6225920 | tf_op jit(solution)/shard_map/dot_general | solution.py:63
  354.8 20.5 %fusion.12 = bf16[3,224,4096]{2,1,0:T(8,128)(2,1)} fusion(f32[3,224,4096]{2,1,0:T(8,128)S(1)} %bitcast.145, f32[1,224,4096]{2,1,0:T(8,128)} %fusion.13, f32[1,224,4096]{2,1,0:T(8,128)} %fusion.14, f32[1,224,4096]{2,1,0:T(8,128)S(1)} %fusion.15, f32[1,224,4096]{2,1,0:T(8,128)S(1)} %copy-done.4, f32[1,224,4096]{2,1,0:T(8,128)S(1)} %copy-done.6, ...), kind=kLoop, calls=%fused_computation.23 | loop fusion | flops 104595456 | bytes 49545216 | tf_op jit(solution)/shard_map/convert_element_type | solution.py:116
  375.4 86.1 %reduce-scatter.2.cloned.1.call-done = bf16[3,224,1024]{2,1,0:T(8,128)(2,1)} async-done(((bf16[3,224,4096]{2,1,0:T(8,128)(2,1)}), bf16[3,224,1024]{2,1,0:T(8,128)(2,1)}) %reduce-scatter.2.cloned.1.call-update) | async-done | bytes 1376272 | tf_op jit(solution)/shard_map/reduce_scatter | solution.py:115
  461.4 5.7 %multiply_subtract_fusion = (f32[3,224,1024]{2,1,0:T(8,128)}, f32[3,224,1024]{2,1,0:T(8,128)}) fusion(f32[3,224,1024]{2,1,0:T(8,128)S(1)} %copy-done.9, bf16[3,224,1024]{2,1,0:T(8,128)(2,1)} %reduce-scatter.2.cloned.1.call-done, f32[3,224,1024]{2,1,0:T(8,128)} %param.8), kind=kLoop, calls=%fused_computation.36 | loop fusion | flops 5505024 | bytes 12386304 | tf_op jit(solution)/shard_map/sub | solution.py:120
  (88 shorter events, 47.6 us)
Async XLA Ops:
  7.2 142.1 %all-gather.2.cloned.1.call-start = ((), (), s32[]{:S(2)}) async-start(), calls=%async_computation.7 | async-start | bytes 4325376 | tf_op jit(solution)/shard_map/all_gather | solution.py:80
  160.0 42.4 %all-to-all-start.2 = ((f32[32,8,4096]{2,1,0:T(8,128)}), f32[32,8,4096]{2,1,0:T(8,128)}, u32[]{:S(2)}, u32[]{:S(2)}) async-start(f32[32,8,4096]{2,1,0:T(8,128)} %fusion.55), calls=%async_computation.2 | async-start | bytes 8388608 | tf_op jit(solution)/shard_map/all_to_all | solution.py:47
  166.8 48.0 %copy-start.13 = (bf16[2,8,4096]{2,1,0:T(8,128)(2,1)S(1)}, bf16[2,8,4096]{2,1,0:T(8,128)(2,1)}, u32[]{:S(2)}) copy-start(bf16[2,8,4096]{2,1,0:T(8,128)(2,1)} %param.11) | copy-start | bytes 393220
  166.8 47.9 %copy-start.16 = (bf16[2,8,4096]{2,1,0:T(8,128)(2,1)S(1)}, bf16[2,8,4096]{2,1,0:T(8,128)(2,1)}, u32[]{:S(2)}) copy-start(bf16[2,8,4096]{2,1,0:T(8,128)(2,1)} %param.12) | copy-start | bytes 393220
  203.0 16.9 %all-to-all-start.1 = ((s32[32,1,2]{2,1,0:T(1,128)}), s32[32,1,2]{2,1,0:T(1,128)S(1)}, u32[]{:S(2)}, u32[]{:S(2)}) async-start(s32[32,1,2]{2,1,0:T(1,128)} %broadcast_in_dim.13), calls=%async_computation.1 | async-start | bytes 32768 | tf_op jit(solution)/shard_map/all_to_all | solution.py:29
  221.5 22.2 %all-to-all-start.3 = ((bf16[32,8,4096]{2,1,0:T(8,128)(2,1)}), bf16[32,8,4096]{2,1,0:T(8,128)(2,1)}, u32[]{:S(2)}, u32[]{:S(2)}) async-start(bf16[32,8,4096]{2,1,0:T(8,128)(2,1)} %broadcast_in_dim.14), calls=%async_computation.3 | async-start | bytes 4194304 | tf_op jit(solution)/shard_map/all_to_all | solution.py:29
  233.5 12.6 %copy-start.10 = (bf16[28,8,4,1024]{3,1,2,0:T(8,128)(2,1)S(1)}, bf16[28,8,4,1024]{3,1,2,0:T(8,128)(2,1)}, u32[]{:S(2)}) copy-start(bf16[28,8,4,1024]{3,1,2,0:T(8,128)(2,1)} %copy.42) | copy-start | bytes 5505028
  243.7 7.0 %copy-start.8 = (bf16[2,256,4096]{2,1,0:T(8,128)(2,1)S(1)}, bf16[2,256,4096]{2,1,0:T(8,128)(2,1)}, u32[]{:S(2)}) copy-start(bf16[2,256,4096]{2,1,0:T(8,128)(2,1)} %all-gather.2.cloned.1.call-done) | copy-start | bytes 12582916
  243.7 8.4 %slice-start = ((s8[11010048]{0:T(1024)(128)(4,1)}), s8[4194304]{0:T(1024)(128)(4,1)S(1)}, s32[]{:S(2)}) async-start(s8[11010048]{0:T(1024)(128)(4,1)} %bitcast.140), calls=%async_computation.9 | async-start | bytes 8388608
  246.1 6.0 %copy-start.3 = (f32[1,224,4096]{2,1,0:T(8,128)}, f32[1,224,4096]{2,1,0:T(8,128)S(1)}, u32[]{:S(2)}) copy-start(f32[1,224,4096]{2,1,0:T(8,128)S(1)} %fusion.16) | copy-start | bytes 11010052
  246.1 5.2 %copy-start.15 = (f32[256,224]{0,1:T(8,128)S(1)}, f32[256,224]{0,1:T(8,128)}, u32[]{:S(2)}) copy-start(f32[256,224]{0,1:T(8,128)} %get-tuple-element.10) | copy-start | bytes 688132
  246.2 5.9 %slice-start.1 = ((s8[11010048]{0:T(1024)(128)(4,1)}), s8[4194304]{0:T(1024)(128)(4,1)S(1)}, s32[]{:S(2)}) async-start(s8[11010048]{0:T(1024)(128)(4,1)} %bitcast.140), calls=%async_computation.10 | async-start | bytes 8388608
  246.2 6.2 %slice-start.6 = ((s8[5505024]{0:T(1024)(128)(4,1)}), s8[4194304]{0:T(1024)(128)(4,1)S(1)}, s32[]{:S(2)}) async-start(s8[5505024]{0:T(1024)(128)(4,1)} %bitcast.147), calls=%async_computation.15 | async-start | bytes 8388608
  250.6 5.5 %slice-start.7 = ((s8[5505024]{0:T(1024)(128)(4,1)}), s8[1310720]{0:T(1024)(128)(4,1)S(1)}, s32[]{:S(2)}) async-start(s8[5505024]{0:T(1024)(128)(4,1)} %bitcast.147), calls=%async_computation.16 | async-start | bytes 2621440
  251.3 16.1 %copy-start.5 = (f32[1,224,4096]{2,1,0:T(8,128)}, f32[1,224,4096]{2,1,0:T(8,128)S(1)}, u32[]{:S(2)}) copy-start(f32[1,224,4096]{2,1,0:T(8,128)S(1)} %fusion.17) | copy-start | bytes 11010052
  252.1 15.3 %copy-start.1 = (f32[1,224,4096]{2,1,0:T(8,128)}, f32[1,224,4096]{2,1,0:T(8,128)S(1)}, u32[]{:S(2)}) copy-start(f32[1,224,4096]{2,1,0:T(8,128)S(1)} %fusion.18) | copy-start | bytes 11010052
  311.0 31.1 %all-to-all-start.5 = ((bf16[32,8,4096]{2,1,0:T(8,128)(2,1)}), bf16[32,8,4096]{2,1,0:T(8,128)(2,1)S(1)}, u32[]{:S(2)}, u32[]{:S(2)}) async-start(bf16[32,8,4096]{2,1,0:T(8,128)(2,1)} %broadcast_in_dim.15), calls=%async_computation.5 | async-start | bytes 4194304 | tf_op jit(solution)/shard_map/all_to_all | solution.py:29
  315.0 146.4 %reduce-scatter.2.cloned.1.call-start = ((), (), s32[]{:S(2)}) async-start(), calls=%async_computation.8 | async-start | bytes 6881280 | tf_op jit(solution)/shard_map/reduce_scatter | solution.py:115
  342.0 12.5 %slice-start.3 = ((s8[11010048]{0:T(1024)(128)(4,1)}), s8[4194304]{0:T(1024)(128)(4,1)S(1)}, s32[]{:S(2)}) async-start(s8[11010048]{0:T(1024)(128)(4,1)} %bitcast.143), calls=%async_computation.12 | async-start | bytes 8388608
  344.5 10.0 %slice-start.4 = ((s8[11010048]{0:T(1024)(128)(4,1)}), s8[4194304]{0:T(1024)(128)(4,1)S(1)}, s32[]{:S(2)}) async-start(s8[11010048]{0:T(1024)(128)(4,1)} %bitcast.143), calls=%async_computation.13 | async-start | bytes 8388608
  344.5 10.0 %copy-start.6 = (f32[1,224,4096]{2,1,0:T(8,128)S(1)}, f32[1,224,4096]{2,1,0:T(8,128)}, u32[]{:S(2)}) copy-start(f32[1,224,4096]{2,1,0:T(8,128)} %copy-done.5) | copy-start | bytes 11010052
  347.1 7.5 %slice-start.5 = ((s8[11010048]{0:T(1024)(128)(4,1)}), s8[2621440]{0:T(1024)(128)(4,1)S(1)}, s32[]{:S(2)}) async-start(s8[11010048]{0:T(1024)(128)(4,1)} %bitcast.143), calls=%async_computation.14 | async-start | bytes 5242880
  347.1 7.5 %copy-start.4 = (f32[1,224,4096]{2,1,0:T(8,128)S(1)}, f32[1,224,4096]{2,1,0:T(8,128)}, u32[]{:S(2)}) copy-start(f32[1,224,4096]{2,1,0:T(8,128)} %copy-done.3) | copy-start | bytes 11010052
  375.3 86.1 %copy-start.9 = (f32[3,224,1024]{2,1,0:T(8,128)S(1)}, f32[3,224,1024]{2,1,0:T(8,128)}, u32[]{:S(2)}) copy-start(f32[3,224,1024]{2,1,0:T(8,128)} %param.7) | copy-start | bytes 8257540
  (8 other events, 28.1 us)
Sparse Core Ops, SparseCore 0:
  9.6 139.5 all-gather.1
  375.5 85.9 reduce-scatter.1
where the time goes:
time: 475 us; the launch traced here: 474 us
  waiting for transfers between devices  183 us (39%)
  blocking collectives  129 us (27%)
  other arithmetic  48.3 us (10%)
  matrix products  38.1 us (8%)
  local copies, waits for them, and re-layouts  33.9 us (7%)
  starting transfers between devices  25.4 us (5%)
  between operations  16.4 us (3%)
    all_to_all x1, blocking collectives, copy_for_each(): return lax.all_to_all(copies, axis, split_axis=0, concat_axis=0, tiled=True)  96.8 us
    reduce_scatter x1, waiting for transfers between devices, body(): lax.psum_scatter(pseudo_term.astype(jnp.bfloat16), 'isl', scatter_dimensi...  86.1 us
    all_to_all x3, waiting for transfers between devices, copy_for_each(): return lax.all_to_all(copies, axis, split_axis=0, concat_axis=0, tiled=True)  34.9 us
    all_to_all x1, waiting for transfers between devices, sum_at_owner(): lax.all_to_all(split_up(shard, dim, devices), axis, 0, 0, tiled=True)  34.9 us
    all_to_all x1, blocking collectives, sum_at_owner(): lax.all_to_all(split_up(shard, dim, devices), axis, 0, 0, tiled=True)  32.4 us
    all_gather x1, waiting for transfers between devices, body(): all_inputs = lax.all_gather(inputs, 'fsdp', axis=1, tiled=True)  26.2 us
    convert_element_type x1, other arithmetic, body(): pseudo_term.astype(jnp.bfloat16)  20.5 us
    all_to_all x3, starting transfers between devices, copy_for_each(): return lax.all_to_all(copies, axis, split_axis=0, concat_axis=0, tiled=True)  18.3 us
  transfers between devices with their start and end apart: 6, of which 6 were waited for; matrix products, arithmetic and copies ran while one was open for 7% of the time, Pallas kernels for 0%

commit v1 on v0

v1 whole, which is shorter than its diff:
```python
import functools
import math

import jax
import jax.numpy as jnp
from jax import lax
from jax.experimental import pallas as pl
from jax.experimental.pallas import tpu as pltpu
from jax.sharding import Mesh
from jax.sharding import PartitionSpec as P


D = 4096
FF = 7168

inner_rate = 0.02
beta_first = 0.9
beta_second = 0.95
epsilon = 1e-08
decay_rate = 0.1
outer_rate = 0.7
nesterov_coef = 0.9


bf16, f32 = jnp.bfloat16, jnp.float32

FSDP = ("x", "y", "zl")
SIZES = {"x": 4, "y": 4, "zl": 2}


def around(own, dim):
    n = SIZES[dim]
    return [own] + [lax.ppermute(own, dim, [(i, (i - s) % n) for i in range(n)]) for s in range(1, n)]


def collect(own, dim):
    n = SIZES[dim]
    blocks = around(own, dim)
    ring = jnp.stack(blocks + blocks[:-1])
    return lax.dynamic_slice_in_dim(ring, (n - lax.axis_index(dim)) % n, n, axis=0)


def contract_last(left, right):
    return lax.dot_general(left, right, (((1,), (1,)), ((), ())), preferred_element_type=f32)


VM = pl.BlockSpec(memory_space=pltpu.VMEM)
SM = pl.BlockSpec(memory_space=pltpu.SMEM)
MIB = 1 << 20


def forward_kernel(n_w, at_ref, *refs):
    pieces, refs = refs[:8], refs[8:]
    w_refs, refs = refs[:n_w], refs[n_w:]
    x_out, gate_out, up_out, hidden_out, p_out = refs[:5]
    turn = refs[-1]
    quarter = x_out.shape[1] // 4
    half = 2 * quarter

    def w(p, r):
        if n_w == 1:
            return w_refs[0][p, r]
        return w_refs[2 * r][p] if p < 2 else w_refs[2 * r + 1][0]

    plane = pieces[0].shape[0]
    block = plane // 4
    for s in range(4):
        row = pl.multiple_of(((at_ref[0] + s) % 4) * plane, plane)
        x_out[pl.ds(row, plane), 0:half] = pieces[s][...]
        for x in range(4):
            row = pl.multiple_of(x * plane + ((at_ref[1] + s) % 4) * block, block)
            x_out[pl.ds(row, block), half:] = pieces[4 + s][x * block : (x + 1) * block, 0:half]
    if n_w > 1:
        for p in range(3):
            for r in range(4):
                refs[5][p, r] = w(p, r)
    gate, up = None, None
    for r in range(4):
        x = x_out[:, r * quarter : (r + 1) * quarter]
        g, u = contract_last(w(0, r), x), contract_last(w(1, r), x)
        gate = g if gate is None else gate + g
        up = u if up is None else up + u
    gate = gate * (1.0 / math.sqrt(D))
    up = up * (1.0 / math.sqrt(D))
    gate_out[...] = gate
    up_out[...] = up
    hidden = (gate * jax.nn.sigmoid(gate)) * up
    hidden_out[...] = hidden.astype(bf16)
    rows = hidden.shape[0]
    turn[...] = jnp.zeros_like(turn)
    turn[0:rows, :] = hidden
    turned = turn[...].T[:, 0:rows].astype(bf16)
    for r in range(4):
        part = jnp.dot(turned, w(2, r), preferred_element_type=f32)
        p_out[:, r * quarter : (r + 1) * quarter] = part.astype(bf16)


def forward(at, pieces, w, rows):
    first = isinstance(w, list)
    tokens, width = 4 * pieces[0].shape[0], 2 * pieces[0].shape[1]
    square = -(-max(rows, tokens) // 128) * 128
    small = jax.ShapeDtypeStruct((rows, tokens), f32)
    wide = jax.ShapeDtypeStruct((tokens, width), bf16)
    outs = [wide, small, small, jax.ShapeDtypeStruct((rows, tokens), bf16), wide]
    if first:
        outs.append(jax.ShapeDtypeStruct((3, 4, rows, width // 4), bf16))
    weights = w if first else [w]
    return pl.pallas_call(
        functools.partial(forward_kernel, len(weights)),
        out_shape=outs,
        in_specs=[SM] + [VM] * (8 + len(weights)),
        out_specs=[VM] * len(outs),
        scratch_shapes=[pltpu.VMEM((square, tokens), f32)],
        compiler_params=pltpu.CompilerParams(vmem_limit_bytes=24 * MIB),
        cost_estimate=pl.CostEstimate(flops=6 * rows * tokens * width, bytes_accessed=8 << 20, transcendentals=0),
        name="forward0" if first else "forward1",
    )(at, *pieces, *weights)


def slopes_kernel(scale, parts_ref, x_ref, y_ref, out_ref):
    width = x_ref.shape[1]
    lanes = min(512, width)
    for low in range(0, width, lanes):
        cols = slice(low, low + lanes)
        total = parts_ref[0, :, cols].astype(f32)
        for k in range(1, parts_ref.shape[0]):
            total = total + parts_ref[k, :, cols].astype(f32)
        outputs = x_ref[:, cols].astype(f32) + total * (1.0 / math.sqrt(FF))
        slopes = ((outputs - y_ref[:, cols].astype(f32)) * scale).astype(bf16)
        for k in range(out_ref.shape[0]):
            out_ref[k, :, cols] = slopes


def own_slopes(parts, x, y):
    n, tok, width = parts.shape
    return pl.pallas_call(
        functools.partial(slopes_kernel, 1.0 / (n * tok)),
        out_shape=jax.ShapeDtypeStruct(parts.shape, bf16),
        in_specs=[VM, VM, VM],
        out_specs=VM,
        compiler_params=pltpu.CompilerParams(vmem_limit_bytes=8 * MIB),
        cost_estimate=pl.CostEstimate(flops=n * tok * width, bytes_accessed=4 * n * tok * width, transcendentals=0),
        name="own_slopes",
    )(parts, x, y)


def slope_kernel(z_ref, w_ref, gate_ref, up_ref, hidden_ref, s_out):
    quarter = w_ref.shape[-1]
    slope = None
    for r in range(4):
        part = contract_last(w_ref[2, r], z_ref[:, r * quarter : (r + 1) * quarter])
        slope = part if slope is None else slope + part
    slope = slope * (1.0 / math.sqrt(FF))
    gate = gate_ref[...]
    sig = jax.nn.sigmoid(gate)
    s_out[0] = (slope * up_ref[...] * (sig * (1.0 + gate * (1.0 - sig)))).astype(bf16)
    s_out[1] = (slope * (gate * sig)).astype(bf16)
    s_out[2] = hidden_ref[...]


def slope_parts(z, w, gate, up, hidden):
    rows, tokens = gate.shape
    width = z.shape[1]
    return pl.pallas_call(
        slope_kernel,
        out_shape=jax.ShapeDtypeStruct((3, rows, tokens), bf16),
        in_specs=[VM] * 5,
        out_specs=VM,
        compiler_params=pltpu.CompilerParams(vmem_limit_bytes=12 * MIB),
        cost_estimate=pl.CostEstimate(flops=2 * rows * tokens * width, bytes_accessed=4 << 20, transcendentals=0),
        name="slope_parts",
    )(z, w, gate, up, hidden)


def adam_step(m, v, c, g, k):
    m = k[0] * m + k[1] * g
    v = k[2] * v + k[3] * (g * g)
    root = v * lax.rsqrt(v)
    c = k[4] * c - k[5] * (m / (root + epsilon))
    return m, v, c


def adam_kernel(steps, ps, r_of, lanes, pos, coef, m_ref, v_ref, w_ref, *refs):
    ins = [refs[3 * s : 3 * s + 3] for s in range(steps)]
    out_ref = refs[3 * steps]
    g_refs = refs[3 * steps + 1 :]
    i = pl.program_id(0)
    r = r_of(i)
    _, rows, quarter = g_refs[0].shape
    across = pl.ds(pl.multiple_of(r * quarter, quarter), quarter)
    for n, p in enumerate(ps):
        for s in range(steps):
            x_ref, z_ref, s_ref = ins[s]
            right = (x_ref if p < 2 else z_ref)[:, across]
            g_refs[s][n] = jnp.dot(s_ref[p], right, preferred_element_type=f32)
    step_rows = 16
    for n, p in enumerate(ps):
        ks = [[coef[12 * s + (6 if p == 2 else 0) + j] for j in range(6)] for s in range(steps)]

        @pl.loop(0, rows // step_rows, unroll=2 if (rows // step_rows) % 2 == 0 else 1)
        def _(k, n=n, p=p, ks=ks):
            at = pl.ds(pl.multiple_of(k * step_rows, step_rows), step_rows)
            for low in range(0, quarter, lanes):
                cols = slice(low, low + lanes)
                m = m_ref[0, n, at, cols].astype(f32)
                v = v_ref[0, n, at, cols].astype(f32)
                start = w_ref[p, r, at, cols].astype(f32)
                c = start
                for s in range(steps):
                    m, v, c = adam_step(m, v, c, g_refs[s][n, at, cols], ks[s])
                out_ref[n, i, at, cols] = (c if steps == 1 else start - c).astype(bf16)


def adam(pos, coef, first_moment, second_moment, w, parts, tiles):
    ps, rs = list(tiles[0]), list(tiles[1])
    steps = len(parts)
    rows, quarter = w.shape[2:]
    tokens = parts[0][0].shape[0]
    np_, nr = len(ps), len(rs)
    stride = rs[1] - rs[0] if nr > 1 else 0
    assert rs == [rs[0] + stride * k for k in range(nr)] and ps == list(range(ps[0], ps[0] + np_)) and ps[0] % np_ == 0

    def r_of(i):
        return rs[0] + stride * i

    moment = pl.BlockSpec((1, np_, rows, quarter), lambda i, pos: (0, ps[0] // np_, 0, r_of(i) ^ pos[0]))
    args = [a for part in parts for a in part]
    return pl.pallas_call(
        functools.partial(adam_kernel, steps, ps, r_of, min(512, quarter)),
        out_shape=jax.ShapeDtypeStruct((np_, nr, rows, quarter), bf16),
        grid_spec=pltpu.PrefetchScalarGridSpec(
            num_scalar_prefetch=1,
            grid=(nr,),
            in_specs=[SM, moment, moment, VM] + [VM] * (3 * steps),
            out_specs=VM,
            scratch_shapes=[pltpu.VMEM((np_, rows, quarter), f32)] * steps,
        ),
        compiler_params=pltpu.CompilerParams(vmem_limit_bytes=32 * MIB),
        cost_estimate=pl.CostEstimate(
            flops=np_ * nr * steps * 2 * rows * tokens * quarter, bytes_accessed=np_ * nr * rows * quarter * 8, transcendentals=0
        ),
    )(pos, coef, first_moment, second_moment, w, *args)


def coefficients(skipped):
    found = []
    for s in range(2):
        for scale in (1.0 / math.sqrt(D), 1.0 / math.sqrt(FF)):
            go = (beta_first, (1.0 - beta_first) * scale, beta_second, (1.0 - beta_second) * scale * scale, 1.0 - inner_rate * decay_rate, inner_rate)
            stay = (1.0, 0.0, 1.0, 0.0, 1.0, 0.0)
            found.append(jnp.where(skipped[s], jnp.array(stay, f32), jnp.array(go, f32)))
    return jnp.concatenate(found)


def round_of(weights, momentum, first_moment, second_moment, inputs, targets, overflow_step):
    _, rows, quarter = weights.shape
    zh, co = lax.axis_index("zh"), lax.axis_index("co")
    mine = 2 * zh + co

    def own_order(array):
        parts = [lax.dynamic_slice_in_dim(array, (mine ^ r) * quarter, quarter, axis=2) for r in range(4)]
        return jnp.concatenate(parts, axis=2)

    def partner(array):
        return lax.ppermute(array, "co", [(0, 1), (1, 0)])

    def across(array):
        return lax.ppermute(array, "zh", [(0, 1), (1, 0)])

    own = [weights[0:2].astype(bf16), weights[2:3].astype(bf16)]
    far = [across(chunk) for chunk in own]
    near = [partner(chunk) for chunk in own]
    both = [partner(chunk) for chunk in far]
    w = own + near + far + both

    inputs, targets = own_order(inputs), own_order(targets)
    steps, tok, width = inputs.shape
    half = width // 2
    marks = (overflow_step.reshape(1, 1) == jnp.arange(128, dtype=jnp.int32).reshape(1, 128)).astype(bf16)
    marks = jnp.broadcast_to(marks, (tok, 128))
    pair = collect(jnp.concatenate([inputs[0], marks, inputs[1]], axis=1), "zl")
    pieces = []
    for k in range(steps):
        low = k * (width + 128)
        first, second = pair[..., low : low + half], pair[..., low + half : low + width + (128 if k == 0 else 0)]
        if k:
            first, second, *middle = lax.optimization_barrier((first, second, *middle))
        middle = [collect(first, "y"), collect(second, "x")]
        flat = [m.reshape(-1, m.shape[-1]) for m in middle]
        pieces.append(around(flat[0], "x") + around(flat[1], "y"))
    marked = functools.reduce(jnp.maximum, [jnp.max(p[:, half : half + steps], axis=0) for p in pieces[0][4:]])
    coef = coefficients([marked[s] > 0 for s in range(steps)])
    pos = mine.reshape(1).astype(jnp.int32)
    at = jnp.stack([lax.axis_index("x"), lax.axis_index("y")]).astype(jnp.int32)

    parts = []
    w_start = None
    for k in range(steps):
        x, gate, up, hidden, sums, *w0 = forward(at, pieces[k], w, rows)
        if k == 0:
            w = w_start = w0[0]
        arrived = lax.all_to_all(sums.reshape(-1, tok, width), FSDP, 0, 0, tiled=True)
        copies = own_slopes(arrived, inputs[k], targets[k])
        z = lax.all_to_all(copies, FSDP, 0, 0, tiled=True).reshape(-1, width)
        parts.append((x, z, slope_parts(z, w, gate, up, hidden)))
        if k == 0:
            w = adam(pos, coef, first_moment, second_moment, w, parts, (range(3), range(4)))
    arrived = []
    for p in (2, 0, 1):
        pair = adam(pos, coef, first_moment, second_moment, w_start, parts, ((p,), (3, 2)))
        joint = (pair[0, 1].astype(f32) + partner(pair[0, 0]).astype(f32)).astype(bf16)
        joint, pos = lax.optimization_barrier((joint, pos))
        arrived.append((p, across(joint)))
    rest = adam(pos, coef, first_moment, second_moment, w_start, parts, (range(3), (1, 0)))
    near_part = partner(rest[:, 0])
    arrived = jnp.stack([a for _, a in sorted(arrived, key=lambda e: e[0])])
    delta = (rest[:, 1].astype(f32) + near_part.astype(f32) + arrived.astype(f32)) / 4
    new_momentum = nesterov_coef * momentum + delta
    new_weights = weights - outer_rate * (delta + nesterov_coef * new_momentum)
    return (new_weights, new_momentum)


def solution(mesh):
    grid = Mesh(mesh.devices.reshape(2, 2, 4, 2, 4), ("zh", "co", "x", "zl", "y"))
    isl, fsdp = ("zh", "co"), ("x", "zl", "y")
    in_specs = (
        P(None, fsdp, isl),
        P(None, fsdp, isl),
        P(isl, None, fsdp, None),
        P(isl, None, fsdp, None),
        P(None, isl + fsdp, None),
        P(None, isl + fsdp, None),
        P(isl, fsdp),
    )
    out_specs = (P(None, fsdp, isl), P(None, fsdp, isl))
    return jax.shard_map(round_of, mesh=grid, in_specs=in_specs, out_specs=out_specs, check_vma=False)
```

time: 475 us -> 361 us (0.76)
  blocking collectives: 129 us -> 52.9 us
  starting transfers between devices: 25.4 us -> 87.1 us
  waiting for transfers between devices: 183 us -> 122 us
  Pallas kernels: 0 us -> 52.6 us
  matrix products: 38.1 us -> 0 us
  other arithmetic: 48.3 us -> 11.2 us
  between operations: 16.4 us -> 3.16 us
    ppermute x0 -> x38, waiting for transfers between devices: none -> 97.6 us  [the longest x25 63.6 us: around(): lax.ppermute(own, dim, [(i, (i - s) % n) for i in range(n)])]
    reduce_scatter x1 -> x0, waiting for transfers between devices: 86.1 us -> none  [body(): lax.psum_scatter(pseudo_term.astype(jnp.bfloat16), 'isl', scatter_dimensi...]
    all_to_all x2, blocking collectives: 129 us -> 52.9 us  [the longest x1 27.5 us: round_of(): z = lax.all_to_all(copies, FSDP, 0, 0, tiled=True).reshape(-1, width)]
    ppermute x0 -> x38, starting transfers between devices: none -> 76.2 us  [the longest x25 38.7 us: around(): lax.ppermute(own, dim, [(i, (i - s) % n) for i in range(n)])]
    pallas_call x0 -> x11, Pallas kernels: none -> 52.6 us  [the longest x5 42.5 us: adam(): pl.pallas_call(functools.partial(adam_kernel, steps, ps, r_of, min(512, q...]
    all_to_all x4 -> x2, waiting for transfers between devices: 69.8 us -> 24.5 us  [the longest x1 15.8 us: round_of(): lax.all_to_all(sums.reshape(-1, tok, width), FSDP, 0, 0, tiled=True)]
    dot_general x14 -> x0, matrix products: 38.1 us -> none  [the longest x6 17.8 us: contract_last(): lax.dot_general(left_side, right_side, (((1,), (1,)), ((), ())), preferre...]
    convert_element_type x6 -> x4, other arithmetic: 33.9 us -> 0.48 us  [the longest x3 0.48 us: round_of(): (pair[0, 1].astype(f32) + partner(pair[0, 0]).astype(f32)).astype(bf16)]
  transfers between devices with their start and end apart: 6 -> 40, of which waited for: 6 -> 21; matrix products, arithmetic and copies ran while one was open for 7% -> 5% of each run, Pallas kernels for 0% -> 5%
where the time goes in v1:
time: 361 us; the launch traced here: 360 us
  waiting for transfers between devices  122 us (34%)
  starting transfers between devices  87.1 us (24%)
  blocking collectives  52.9 us (15%)
  Pallas kernels  52.6 us (15%)
  local copies, waits for them, and re-layouts  30.5 us (8%)
  other arithmetic  11.2 us (3%)
    ppermute x25, waiting for transfers between devices, around(): lax.ppermute(own, dim, [(i, (i - s) % n) for i in range(n)])  63.6 us
    pallas_call x5, Pallas kernels, adam(): pl.pallas_call(functools.partial(adam_kernel, steps, ps, r_of, min(512, q...  42.5 us
    ppermute x25, starting transfers between devices, around(): lax.ppermute(own, dim, [(i, (i - s) % n) for i in range(n)])  38.7 us
    ppermute x5, waiting for transfers between devices, across(): return lax.ppermute(array, 'zh', [(0, 1), (1, 0)])  29.6 us
    ppermute x8, starting transfers between devices, partner(): return lax.ppermute(array, 'co', [(0, 1), (1, 0)])  29.5 us
    all_to_all x1, blocking collectives, round_of(): z = lax.all_to_all(copies, FSDP, 0, 0, tiled=True).reshape(-1, width)  27.5 us
    unnamed x74, local copies, waits for them, and re-layouts  25.6 us
    all_to_all x1, blocking collectives, round_of(): lax.all_to_all(sums.reshape(-1, tok, width), FSDP, 0, 0, tiled=True)  25.4 us
  transfers between devices with their start and end apart: 40, of which 21 were waited for; matrix products, arithmetic and copies ran while one was open for 5% of the time, Pallas kernels for 5%

profile of v1, /device:TPU:1, one launch (start us, length us, event | category | flops | bytes accessed | tf_op | source)
XLA Modules:
  0.0 359.5 jit_solution(341889506245416164)
XLA Ops:
  2.7 4.5 %collective-permute-start.16 = (bf16[1,224,1024]{2,1,0:T(8,128)(2,1)S(1)}, bf16[1,224,1024]{2,1,0:T(8,128)(2,1)}, u32[]{:S(2)}, u32[]{:S(2)}) collective-permute-start(bf16[1,224,1024]{2,1,0:T(8,128)(2,1)S(1)} %slice.109.refs_9_), channel_id=1, source_target_pairs={{0,64},{64,0},{1,65},{65,1},{2,66},{66,2},{3,67},{67,3},{4,68},{68... | collective-permute-start | bytes 1376264 | tf_op jit(solution)/shard_map/ppermute | solution.py:268
  11.2 29.3 %collective-permute-done = bf16[8,8320]{1,0:T(8,128)(2,1)} collective-permute-done((bf16[8,8320]{1,0:T(8,128)(2,1)}, bf16[8,8320]{1,0:T(8,128)(2,1)}, u32[]{:S(2)}, u32[]{:S(2)}) %collective-permute-start) | collective-permute-done | bytes 133152 | tf_op jit(solution)/shard_map/ppermute | solution.py:33
  51.1 4.0 %collective-permute-done.9 = bf16[2,8,2048]{2,1,0:T(8,128)(2,1)S(1)} collective-permute-done((bf16[2,8,2048]{2,1,0:T(8,128)(2,1)S(1)}, bf16[2,8,2048]{2,1,0:T(8,128)(2,1)S(1)}, u32[]{:S(2)}, u32[]{:S(2)}) %collective-permute-start.9) | collective-permute-done | bytes 65568 | tf_op jit(solution)/shard_map/ppermute | solution.py:33
  64.3 4.1 %collective-permute-done.3 = bf16[2,8,2176]{2,1,0:T(8,128)(2,1)S(1)} collective-permute-done((bf16[2,8,2176]{2,1,0:T(8,128)(2,1)S(1)}, bf16[2,8,2176]{2,1,0:T(8,128)(2,1)S(1)}, u32[]{:S(2)}, u32[]{:S(2)}) %collective-permute-start.3) | collective-permute-done | bytes 69664 | tf_op jit(solution)/shard_map/ppermute | solution.py:33
  76.9 4.0 %collective-permute-done.21 = bf16[2,8,2048]{2,1,0:T(8,128)(2,1)S(1)} collective-permute-done((bf16[2,8,2048]{2,1,0:T(8,128)(2,1)S(1)}, bf16[2,8,2048]{2,1,0:T(8,128)(2,1)S(1)}, u32[]{:S(2)}, u32[]{:S(2)}) %collective-permute-start.21) | collective-permute-done | bytes 65568 | tf_op jit(solution)/shard_map/ppermute | solution.py:33
  84.1 11.6 %collective-permute-start.17 = (bf16[2,224,1024]{2,1,0:T(8,128)(2,1)S(1)}, bf16[2,224,1024]{2,1,0:T(8,128)(2,1)S(1)}, u32[]{:S(2)}, u32[]{:S(2)}) collective-permute-start(bf16[2,224,1024]{2,1,0:T(8,128)(2,1)S(1)} %collective-permute-done.15.refs_12_), channel_id=1, source_target_pairs={{0,32},{32,0},{1,33},{33,1},{2,34},{34,2},{3,35},{35,3},{4,36},{36... | collective-permute-start | bytes 2752520 | tf_op jit(solution)/shard_map/ppermute | solution.py:265
  95.9 6.9 %collective-permute-start.18 = (bf16[1,224,1024]{2,1,0:T(8,128)(2,1)}, bf16[1,224,1024]{2,1,0:T(8,128)(2,1)S(1)}, u32[]{:S(2)}, u32[]{:S(2)}) collective-permute-start(bf16[1,224,1024]{2,1,0:T(8,128)(2,1)} %collective-permute-done.16.refs_13_), channel_id=1, source_target_pairs={{0,32},{32,0},{1,33},{33,1},{2,34},{34,2},{3,35},{35,3},{4,36},{36... | collective-permute-start | bytes 1376264 | tf_op jit(solution)/shard_map/ppermute | solution.py:265
  106.3 6.0 %collective-permute-done.5.refs_6_ = bf16[64,2176]{1,0:T(8,128)(2,1)S(1)} collective-permute-done((bf16[64,2176]{1,0:T(8,128)(2,1)S(1)}, bf16[64,2176]{1,0:T(8,128)(2,1)S(1)}, u32[]{:S(2)}, u32[]{:S(2)}) %collective-permute-start.5) | collective-permute-done | bytes 278560 | tf_op jit(solution)/shard_map/ppermute | solution.py:33
  123.5 3.8 %forward0.1 = (bf16[256,4096]{1,0:T(8,128)(2,1)S(1)}, f32[224,256]{1,0:T(8,128)S(1)}, f32[224,256]{1,0:T(8,128)S(1)}, bf16[224,256]{1,0:T(8,128)(2,1)S(1)}, bf16...) custom-call(s32[2]{0:T(128)S(1)} %pad_add_fusion.at_ref, bf16[64,2048]{1,0:T(8,128)(2,1)S(1)} %bitcast.128, ...), custom_call_target="tpu_custom_call" | custom-call | flops 1409286144 | bytes 8388608 | tf_op jit(solution)/shard_map/forward0/pallas_call | solution.py:108
  134.4 5.9 %all-to-all-start = ((bf16[32,8,4096]{2,1,0:T(8,128)(2,1)}), bf16[32,8,4096]{2,1,0:T(8,128)(2,1)S(1)}, u32[]{:S(2)}, u32[]{:S(2)}) async-start(bf16[32,8,4096]{2,1,0:T(8,128)(2,1)} %bitcast.118), calls=%async_computation | async-start | bytes 4194304 | tf_op jit(solution)/shard_map/all_to_all | solution.py:302
  150.9 15.8 %all-to-all-done.parts_ref = bf16[32,8,4096]{2,1,0:T(8,128)(2,1)S(1)} async-done(((bf16[32,8,4096]{2,1,0:T(8,128)(2,1)}), bf16[32,8,4096]{2,1,0:T(8,128)(2,1)S(1)}, u32[]{:S(2)}, u32[]{:S(2)}) %all-to-all-start) | async-done | bytes 2097184 | tf_op jit(solution)/shard_map/all_to_all | solution.py:302
  168.5 4.9 %all-to-all-start.1 = ((bf16[32,8,4096]{2,1,0:T(8,128)(2,1)}), bf16[32,8,4096]{2,1,0:T(8,128)(2,1)S(1)}, u32[]{:S(2)}, u32[]{:S(2)}) async-start(bf16[32,8,4096]{2,1,0:T(8,128)(2,1)} %copy-done.5), calls=%async_computation.1 | async-start | bytes 4194304 | tf_op jit(solution)/shard_map/all_to_all | solution.py:304
  187.7 8.7 %all-to-all-done.1 = bf16[32,8,4096]{2,1,0:T(8,128)(2,1)S(1)} async-done(((bf16[32,8,4096]{2,1,0:T(8,128)(2,1)}), bf16[32,8,4096]{2,1,0:T(8,128)(2,1)S(1)}, u32[]{:S(2)}, u32[]{:S(2)}) %all-to-all-start.1) | async-done | bytes 2097184 | tf_op jit(solution)/shard_map/all_to_all | solution.py:304
  207.1 13.3 %shard_map.158.refs_8_.w_ref = bf16[3,4,224,1024]{3,2,1,0:T(8,128)(2,1)S(1)} custom-call(s32[1]{0:T(128)} %bitcast.pos, f32[24]{0:T(128)S(1)} %pad_maximum_fusion.4.coef, bf16[1,3,224,4096]{3,2,1,0:T(8,128)(2,1)S(1)} %bitcast.106, bf16[1,3,224,4096]{3,2,1,0:T(8,128)(2,1)S(1)} %copy-done.2, bf16[3,4,224,1024]{3,2,1,0:T(8,128)(2,1)} %copy-done, ...), custom_call_target="tpu_custom_call" | custom-call | flops 1409286144 | bytes 22020096 | tf_op jit(solution)/shard_map/pallas_call | solution.py:228
  224.3 25.4 %all_to_all.20.parts_ref = bf16[32,8,4096]{2,1,0:T(8,128)(2,1)S(1)} all-to-all(bf16[32,8,4096]{2,1,0:T(8,128)(2,1)S(1)} %bitcast.119), channel_id=1, replica_groups=mesh['zh'=2,'co'=2,'x'=4,'zl'=2,'y'=4] {'x','y','zl'}, dimensions={0} | all-to-all | bytes 4194304 | tf_op jit(solution)/shard_map/all_to_all | solution.py:302
  250.1 27.5 %all_to_all.21 = bf16[32,8,4096]{2,1,0:T(8,128)(2,1)S(1)} all-to-all(bf16[32,8,4096]{2,1,0:T(8,128)(2,1)S(1)} %own_slopes.3), channel_id=1, replica_groups=mesh['zh'=2,'co'=2,'x'=4,'zl'=2,'y'=4] {'x','y','zl'}, dimensions={0} | all-to-all | bytes 4194304 | tf_op jit(solution)/shard_map/all_to_all | solution.py:304
  278.4 5.9 %shard_map.159 = bf16[1,2,224,1024]{3,2,1,0:T(8,128)(2,1)S(1)} custom-call(s32[1]{0:T(128)} %bitcast.pos, f32[24]{0:T(128)S(1)} %pad_maximum_fusion.4.coef, bf16[1,3,224,4096]{3,2,1,0:T(8,128)(2,1)S(1)} %bitcast.106, bf16[1,3,224,4096]{3,2,1,0:T(8,128)(2,1)S(1)} %copy-done.2, bf16[3,4,224,1024]{3,2,1,0:T(8,128)(2,1)} %copy-done, ...), custom_call_target="tpu_custom_call" | custom-call | flops 469762048 | bytes 3670016 | tf_op jit(solution)/shard_map/pallas_call | solution.py:228
  284.4 8.4 %collective-permute-start.31 = (bf16[224,1024]{1,0:T(8,128)(2,1)S(1)}, bf16[224,1024]{1,0:T(8,128)(2,1)S(1)}, u32[]{:S(2)}, u32[]{:S(2)}) collective-permute-start(bf16[224,1024]{1,0:T(8,128)(2,1)S(1)} %slice_bitcast_fusion.6), channel_id=1, source_target_pairs={{0,32},{32,0},{1,33},{33,1},{2,34},{34,2},{3,35},{35,3},{4,36},{36... | collective-permute-start | bytes 1376264 | tf_op jit(solution)/shard_map/ppermute | solution.py:265
  294.4 5.9 %shard_map.160 = bf16[1,2,224,1024]{3,2,1,0:T(8,128)(2,1)S(1)} custom-call(s32[1]{0:T(128)} %bitcast.pos, f32[24]{0:T(128)S(1)} %pad_maximum_fusion.4.coef, bf16[1,3,224,4096]{3,2,1,0:T(8,128)(2,1)S(1)} %bitcast.106, bf16[1,3,224,4096]{3,2,1,0:T(8,128)(2,1)S(1)} %copy-done.2, bf16[3,4,224,1024]{3,2,1,0:T(8,128)(2,1)} %copy-done, ...), custom_call_target="tpu_custom_call" | custom-call | flops 469762048 | bytes 3670016 | tf_op jit(solution)/shard_map/pallas_call | solution.py:228
  302.4 5.9 %shard_map.161 = bf16[1,2,224,1024]{3,2,1,0:T(8,128)(2,1)S(1)} custom-call(s32[1]{0:T(128)} %bitcast.pos, f32[24]{0:T(128)S(1)} %pad_maximum_fusion.4.coef, bf16[1,3,224,4096]{3,2,1,0:T(8,128)(2,1)S(1)} %bitcast.106, bf16[1,3,224,4096]{3,2,1,0:T(8,128)(2,1)S(1)} %copy-done.2, bf16[3,4,224,1024]{3,2,1,0:T(8,128)(2,1)} %copy-done, ...), custom_call_target="tpu_custom_call" | custom-call | flops 469762048 | bytes 3670016 | tf_op jit(solution)/shard_map/pallas_call | solution.py:228
  310.7 11.5 %shard_map.162 = bf16[3,2,224,1024]{3,2,1,0:T(8,128)(2,1)S(1)} custom-call(s32[1]{0:T(128)} %bitcast.pos, f32[24]{0:T(128)S(1)} %pad_maximum_fusion.4.coef, bf16[1,3,224,4096]{3,2,1,0:T(8,128)(2,1)S(1)} %bitcast.106, bf16[1,3,224,4096]{3,2,1,0:T(8,128)(2,1)S(1)} %copy-done.2, bf16[3,4,224,1024]{3,2,1,0:T(8,128)(2,1)} %copy-done, ...), custom_call_target="tpu_custom_call" | custom-call | flops 1409286144 | bytes 11010048 | tf_op jit(solution)/shard_map/pallas_call | solution.py:228
  326.2 10.0 %collective-permute-done.37 = bf16[224,1024]{1,0:T(8,128)(2,1)S(1)} collective-permute-done((bf16[224,1024]{1,0:T(8,128)(2,1)S(1)}, bf16[224,1024]{1,0:T(8,128)(2,1)S(1)}, u32[]{:S(2)}, u32[]{:S(2)}) %collective-permute-start.37) | collective-permute-done | bytes 458784 | tf_op jit(solution)/shard_map/ppermute | solution.py:268
  336.2 9.8 %collective-permute-done.35 = bf16[224,1024]{1,0:T(8,128)(2,1)S(1)} collective-permute-done((bf16[224,1024]{1,0:T(8,128)(2,1)S(1)}, bf16[224,1024]{1,0:T(8,128)(2,1)S(1)}, u32[]{:S(2)}, u32[]{:S(2)}) %collective-permute-start.35) | collective-permute-done | bytes 458784 | tf_op jit(solution)/shard_map/ppermute | solution.py:268
  346.0 9.8 %collective-permute-done.36 = bf16[224,1024]{1,0:T(8,128)(2,1)S(1)} collective-permute-done((bf16[224,1024]{1,0:T(8,128)(2,1)S(1)}, bf16[224,1024]{1,0:T(8,128)(2,1)S(1)}, u32[]{:S(2)}, u32[]{:S(2)}) %collective-permute-start.36) | collective-permute-done | bytes 458784 | tf_op jit(solution)/shard_map/ppermute | solution.py:268
  (183 shorter events, 113.3 us)
Async XLA Ops:
  2.7 78.2 %collective-permute-start.16 = (bf16[1,224,1024]{2,1,0:T(8,128)(2,1)S(1)}, bf16[1,224,1024]{2,1,0:T(8,128)(2,1)}, u32[]{:S(2)}, u32[]{:S(2)}) collective-permute-start(bf16[1,224,1024]{2,1,0:T(8,128)(2,1)S(1)} %slice.109.refs_9_), channel_id=1, source_target_pairs={{0,64},{64,0},{1,65},{65,1},{2,66},{66,2},{3,67},{67,3},{4,68},{68... | collective-permute-start | bytes 1376264 | tf_op jit(solution)/shard_map/ppermute | solution.py:268
  7.2 88.5 %collective-permute-start.14 = (bf16[1,224,1024]{2,1,0:T(8,128)(2,1)S(1)}, bf16[1,224,1024]{2,1,0:T(8,128)(2,1)}, u32[]{:S(2)}, u32[]{:S(2)}) collective-permute-start(bf16[1,224,1024]{2,1,0:T(8,128)(2,1)S(1)} %slice.109.refs_9_), channel_id=1, source_target_pairs={{0,32},{32,0},{1,33},{33,1},{2,34},{34,2},{3,35},{35,3},{4,36},{36... | collective-permute-start | bytes 1376264 | tf_op jit(solution)/shard_map/ppermute | solution.py:265
  8.2 75.9 %collective-permute-start.15 = (bf16[2,224,1024]{2,1,0:T(8,128)(2,1)S(1)}, bf16[2,224,1024]{2,1,0:T(8,128)(2,1)S(1)}, u32[]{:S(2)}, u32[]{:S(2)}) collective-permute-start(bf16[2,224,1024]{2,1,0:T(8,128)(2,1)S(1)} %slice.108.refs_8_), channel_id=1, source_target_pairs={{0,64},{64,0},{1,65},{65,1},{2,66},{66,2},{3,67},{67,3},{4,68},{68... | collective-permute-start | bytes 2752520 | tf_op jit(solution)/shard_map/ppermute | solution.py:268
  8.3 115.1 %collective-permute-start.13 = (bf16[2,224,1024]{2,1,0:T(8,128)(2,1)S(1)}, bf16[2,224,1024]{2,1,0:T(8,128)(2,1)S(1)}, u32[]{:S(2)}, u32[]{:S(2)}) collective-permute-start(bf16[2,224,1024]{2,1,0:T(8,128)(2,1)S(1)} %slice.108.refs_8_), channel_id=1, source_target_pairs={{0,32},{32,0},{1,33},{33,1},{2,34},{34,2},{3,35},{35,3},{4,36},{36... | collective-permute-start | bytes 2752520 | tf_op jit(solution)/shard_map/ppermute | solution.py:265
  9.9 30.6 %collective-permute-start = (bf16[8,8320]{1,0:T(8,128)(2,1)}, bf16[8,8320]{1,0:T(8,128)(2,1)}, u32[]{:S(2)}, u32[]{:S(2)}) collective-permute-start(bf16[8,8320]{1,0:T(8,128)(2,1)} %pad_maximum_fusion.1), channel_id=1, source_target_pairs={{0,4},{4,0},{1,5},{5,1},{2,6},{6,2},{3,7},{7,3},{8,12},{12,8},{9,1... | collective-permute-start | bytes 399368 | tf_op jit(solution)/shard_map/ppermute | solution.py:33
  80.9 14.9 %collective-permute-start.12 = (bf16[64,2048]{1,0:T(8,128)(2,1)S(1)}, bf16[64,2048]{1,0:T(8,128)(2,1)S(1)}, u32[]{:S(2)}, u32[]{:S(2)}) collective-permute-start(bf16[64,2048]{1,0:T(8,128)(2,1)S(1)} %bitcast.125), channel_id=1, source_target_pairs={{0,8},{8,16},{16,24},{24,0},{1,9},{9,17},{17,25},{25,1},{2,10},{10... | collective-permute-start | bytes 786440 | tf_op jit(solution)/shard_map/ppermute | solution.py:33
  80.9 15.0 %collective-permute-start.11 = (bf16[64,2048]{1,0:T(8,128)(2,1)S(1)}, bf16[64,2048]{1,0:T(8,128)(2,1)S(1)}, u32[]{:S(2)}, u32[]{:S(2)}) collective-permute-start(bf16[64,2048]{1,0:T(8,128)(2,1)S(1)} %bitcast.126), channel_id=1, source_target_pairs={{0,16},{8,24},{16,0},{24,8},{1,17},{9,25},{17,1},{25,9},{2,18},{10... | collective-permute-start | bytes 786440 | tf_op jit(solution)/shard_map/ppermute | solution.py:33
  84.1 39.3 %collective-permute-start.17 = (bf16[2,224,1024]{2,1,0:T(8,128)(2,1)S(1)}, bf16[2,224,1024]{2,1,0:T(8,128)(2,1)S(1)}, u32[]{:S(2)}, u32[]{:S(2)}) collective-permute-start(bf16[2,224,1024]{2,1,0:T(8,128)(2,1)S(1)} %collective-permute-done.15.refs_12_), channel_id=1, source_target_pairs={{0,32},{32,0},{1,33},{33,1},{2,34},{34,2},{3,35},{35,3},{4,36},{36... | collective-permute-start | bytes 2752520 | tf_op jit(solution)/shard_map/ppermute | solution.py:265
  95.9 24.2 %collective-permute-start.18 = (bf16[1,224,1024]{2,1,0:T(8,128)(2,1)}, bf16[1,224,1024]{2,1,0:T(8,128)(2,1)S(1)}, u32[]{:S(2)}, u32[]{:S(2)}) collective-permute-start(bf16[1,224,1024]{2,1,0:T(8,128)(2,1)} %collective-permute-done.16.refs_13_), channel_id=1, source_target_pairs={{0,32},{32,0},{1,33},{33,1},{2,34},{34,2},{3,35},{35,3},{4,36},{36... | collective-permute-start | bytes 1376264 | tf_op jit(solution)/shard_map/ppermute | solution.py:265
  112.3 36.5 %collective-permute-start.27 = (bf16[2,8,2048]{2,1,0:T(8,128)(2,1)S(1)}, bf16[2,8,2048]{2,1,0:T(8,128)(2,1)}, u32[]{:S(2)}, u32[]{:S(2)}) collective-permute-start(bf16[2,8,2048]{2,1,0:T(8,128)(2,1)S(1)} %get-tuple-element.28), channel_id=1, source_target_pairs={{0,8},{8,16},{16,24},{24,0},{1,9},{9,17},{17,25},{25,1},{2,10},{10... | collective-permute-start | bytes 196616 | tf_op jit(solution)/shard_map/ppermute | solution.py:33
  118.4 28.9 %collective-permute-start.26 = (bf16[2,8,2048]{2,1,0:T(8,128)(2,1)S(1)}, bf16[2,8,2048]{2,1,0:T(8,128)(2,1)}, u32[]{:S(2)}, u32[]{:S(2)}) collective-permute-start(bf16[2,8,2048]{2,1,0:T(8,128)(2,1)S(1)} %get-tuple-element.28), channel_id=1, source_target_pairs={{0,16},{8,24},{16,0},{24,8},{1,17},{9,25},{17,1},{25,9},{2,18},{10... | collective-permute-start | bytes 196616 | tf_op jit(solution)/shard_map/ppermute | solution.py:33
  120.1 24.6 %collective-permute-start.25 = (bf16[2,8,2048]{2,1,0:T(8,128)(2,1)S(1)}, bf16[2,8,2048]{2,1,0:T(8,128)(2,1)}, u32[]{:S(2)}, u32[]{:S(2)}) collective-permute-start(bf16[2,8,2048]{2,1,0:T(8,128)(2,1)S(1)} %get-tuple-element.28), channel_id=1, source_target_pairs={{0,24},{8,0},{16,8},{24,16},{1,25},{9,1},{17,9},{25,17},{2,26},{10... | collective-permute-start | bytes 196616 | tf_op jit(solution)/shard_map/ppermute | solution.py:33
  134.4 32.4 %all-to-all-start = ((bf16[32,8,4096]{2,1,0:T(8,128)(2,1)}), bf16[32,8,4096]{2,1,0:T(8,128)(2,1)S(1)}, u32[]{:S(2)}, u32[]{:S(2)}) async-start(bf16[32,8,4096]{2,1,0:T(8,128)(2,1)} %bitcast.118), calls=%async_computation | async-start | bytes 4194304 | tf_op jit(solution)/shard_map/all_to_all | solution.py:302
  141.1 45.3 %collective-permute-start.24 = (bf16[64,2048]{1,0:T(8,128)(2,1)}, bf16[64,2048]{1,0:T(8,128)(2,1)}, u32[]{:S(2)}, u32[]{:S(2)}) collective-permute-start(bf16[64,2048]{1,0:T(8,128)(2,1)} %bitcast.27.refs_0_), channel_id=1, source_target_pairs={{0,8},{8,16},{16,24},{24,0},{1,9},{9,17},{17,25},{25,1},{2,10},{10... | collective-permute-start | bytes 786440 | tf_op jit(solution)/shard_map/ppermute | solution.py:33
  142.3 78.1 %collective-permute-start.23 = (bf16[64,2048]{1,0:T(8,128)(2,1)}, bf16[64,2048]{1,0:T(8,128)(2,1)}, u32[]{:S(2)}, u32[]{:S(2)}) collective-permute-start(bf16[64,2048]{1,0:T(8,128)(2,1)} %bitcast.27.refs_0_), channel_id=1, source_target_pairs={{0,16},{8,24},{16,0},{24,8},{1,17},{9,25},{17,1},{25,9},{2,18},{10... | collective-permute-start | bytes 786440 | tf_op jit(solution)/shard_map/ppermute | solution.py:33
  144.7 75.7 %collective-permute-start.22 = (bf16[64,2048]{1,0:T(8,128)(2,1)}, bf16[64,2048]{1,0:T(8,128)(2,1)}, u32[]{:S(2)}, u32[]{:S(2)}) collective-permute-start(bf16[64,2048]{1,0:T(8,128)(2,1)} %bitcast.27.refs_0_), channel_id=1, source_target_pairs={{0,24},{8,0},{16,8},{24,16},{1,25},{9,1},{17,9},{25,17},{2,26},{10... | collective-permute-start | bytes 786440 | tf_op jit(solution)/shard_map/ppermute | solution.py:33
  168.5 27.8 %all-to-all-start.1 = ((bf16[32,8,4096]{2,1,0:T(8,128)(2,1)}), bf16[32,8,4096]{2,1,0:T(8,128)(2,1)S(1)}, u32[]{:S(2)}, u32[]{:S(2)}) async-start(bf16[32,8,4096]{2,1,0:T(8,128)(2,1)} %copy-done.5), calls=%async_computation.1 | async-start | bytes 4194304 | tf_op jit(solution)/shard_map/all_to_all | solution.py:304
  178.0 42.4 %collective-permute-start.30 = (bf16[64,2048]{1,0:T(8,128)(2,1)}, bf16[64,2048]{1,0:T(8,128)(2,1)}, u32[]{:S(2)}, u32[]{:S(2)}) collective-permute-start(bf16[64,2048]{1,0:T(8,128)(2,1)} %bitcast.32.refs_4_), channel_id=1, source_target_pairs={{0,1},{1,2},{2,3},{3,0},{4,5},{5,6},{6,7},{7,4},{8,9},{9,10},{10,1... | collective-permute-start | bytes 786440 | tf_op jit(solution)/shard_map/ppermute | solution.py:33
  179.2 41.2 %collective-permute-start.29 = (bf16[64,2048]{1,0:T(8,128)(2,1)}, bf16[64,2048]{1,0:T(8,128)(2,1)}, u32[]{:S(2)}, u32[]{:S(2)}) collective-permute-start(bf16[64,2048]{1,0:T(8,128)(2,1)} %bitcast.32.refs_4_), channel_id=1, source_target_pairs={{0,2},{1,3},{2,0},{3,1},{4,6},{5,7},{6,4},{7,5},{8,10},{9,11},{10,... | collective-permute-start | bytes 786440 | tf_op jit(solution)/shard_map/ppermute | solution.py:33
  186.4 34.0 %collective-permute-start.28 = (bf16[64,2048]{1,0:T(8,128)(2,1)}, bf16[64,2048]{1,0:T(8,128)(2,1)}, u32[]{:S(2)}, u32[]{:S(2)}) collective-permute-start(bf16[64,2048]{1,0:T(8,128)(2,1)} %bitcast.32.refs_4_), channel_id=1, source_target_pairs={{0,3},{1,0},{2,1},{3,2},{4,7},{5,4},{6,5},{7,6},{8,11},{9,8},{10,9... | collective-permute-start | bytes 786440 | tf_op jit(solution)/shard_map/ppermute | solution.py:33
  322.3 33.6 %collective-permute-start.34 = (bf16[3,224,1024]{2,1,0:T(8,128)(2,1)S(1)}, bf16[3,224,1024]{2,1,0:T(8,128)(2,1)S(1)}, u32[]{:S(2)}, u32[]{:S(2)}) collective-permute-start(bf16[3,224,1024]{2,1,0:T(8,128)(2,1)S(1)} %slice_bitcast_fusion), channel_id=1, source_target_pairs={{0,32},{32,0},{1,33},{33,1},{2,34},{34,2},{3,35},{35,3},{4,36},{36... | collective-permute-start | bytes 4128776 | tf_op jit(solution)/shard_map/ppermute | solution.py:265
  322.7 13.4 %collective-permute-start.37 = (bf16[224,1024]{1,0:T(8,128)(2,1)S(1)}, bf16[224,1024]{1,0:T(8,128)(2,1)S(1)}, u32[]{:S(2)}, u32[]{:S(2)}) collective-permute-start(bf16[224,1024]{1,0:T(8,128)(2,1)S(1)} %fusion.4), channel_id=1, source_target_pairs={{0,64},{64,0},{1,65},{65,1},{2,66},{66,2},{3,67},{67,3},{4,68},{68... | collective-permute-start | bytes 1376264 | tf_op jit(solution)/shard_map/ppermute | solution.py:268
  323.2 22.8 %collective-permute-start.35 = (bf16[224,1024]{1,0:T(8,128)(2,1)S(1)}, bf16[224,1024]{1,0:T(8,128)(2,1)S(1)}, u32[]{:S(2)}, u32[]{:S(2)}) collective-permute-start(bf16[224,1024]{1,0:T(8,128)(2,1)S(1)} %fusion.3), channel_id=1, source_target_pairs={{0,64},{64,0},{1,65},{65,1},{2,66},{66,2},{3,67},{67,3},{4,68},{68... | collective-permute-start | bytes 1376264 | tf_op jit(solution)/shard_map/ppermute | solution.py:268
  325.7 30.1 %collective-permute-start.36 = (bf16[224,1024]{1,0:T(8,128)(2,1)S(1)}, bf16[224,1024]{1,0:T(8,128)(2,1)S(1)}, u32[]{:S(2)}, u32[]{:S(2)}) collective-permute-start(bf16[224,1024]{1,0:T(8,128)(2,1)S(1)} %fusion.2), channel_id=1, source_target_pairs={{0,64},{64,0},{1,65},{65,1},{2,66},{66,2},{3,67},{67,3},{4,68},{68... | collective-permute-start | bytes 1376264 | tf_op jit(solution)/shard_map/ppermute | solution.py:268
  (41 other events, 336.4 us)

commit v2 on v1

--- a/solution.py
+++ b/solution.py
@@ -47,9 +47,10 @@
 VM = pl.BlockSpec(memory_space=pltpu.VMEM)
 SM = pl.BlockSpec(memory_space=pltpu.SMEM)
 MIB = 1 << 20
-
-
-def forward_kernel(n_w, at_ref, *refs):
+FORWARD_MIB, ADAM_MIB, SMALL_MIB = 6, 13, 4
+
+
+def forward_kernel(step, n_w, at_ref, *refs):
     pieces, refs = refs[:8], refs[8:]
     w_refs, refs = refs[:n_w], refs[n_w:]
     x_out, gate_out, up_out, hidden_out, p_out = refs[:5]
@@ -64,12 +65,13 @@
 
     plane = pieces[0].shape[0]
     block = plane // 4
+    cols = slice(step * half, (step + 1) * half)
     for s in range(4):
         row = pl.multiple_of(((at_ref[0] + s) % 4) * plane, plane)
-        x_out[pl.ds(row, plane), 0:half] = pieces[s][...]
+        x_out[pl.ds(row, plane), 0:half] = pieces[s][:, cols]
         for x in range(4):
             row = pl.multiple_of(x * plane + ((at_ref[1] + s) % 4) * block, block)
-            x_out[pl.ds(row, block), half:] = pieces[4 + s][x * block : (x + 1) * block, 0:half]
+            x_out[pl.ds(row, block), half:] = pieces[4 + s][x * block : (x + 1) * block, cols]
     if n_w > 1:
         for p in range(3):
             for r in range(4):
@@ -95,23 +97,23 @@
         p_out[:, r * quarter : (r + 1) * quarter] = part.astype(bf16)
 
 
-def forward(at, pieces, w, rows):
+def forward(at, step, pieces, w, rows):
     first = isinstance(w, list)
-    tokens, width = 4 * pieces[0].shape[0], 2 * pieces[0].shape[1]
+    tokens, width = 4 * pieces[0].shape[0], pieces[0].shape[1]
     square = -(-max(rows, tokens) // 128) * 128
-    small = jax.ShapeDtypeStruct((rows, tokens), f32)
+    small = pltpu.VMEM((rows, tokens), f32)
     wide = jax.ShapeDtypeStruct((tokens, width), bf16)
-    outs = [wide, small, small, jax.ShapeDtypeStruct((rows, tokens), bf16), wide]
+    outs = [pltpu.VMEM((tokens, width), bf16), small, small, pltpu.VMEM((rows, tokens), bf16), wide]
     if first:
-        outs.append(jax.ShapeDtypeStruct((3, 4, rows, width // 4), bf16))
+        outs.append(pltpu.VMEM((3, 4, rows, width // 4), bf16))
     weights = w if first else [w]
     return pl.pallas_call(
-        functools.partial(forward_kernel, len(weights)),
+        functools.partial(forward_kernel, step, len(weights)),
         out_shape=outs,
         in_specs=[SM] + [VM] * (8 + len(weights)),
         out_specs=[VM] * len(outs),
         scratch_shapes=[pltpu.VMEM((square, tokens), f32)],
-        compiler_params=pltpu.CompilerParams(vmem_limit_bytes=24 * MIB),
+        compiler_params=pltpu.CompilerParams(vmem_limit_bytes=FORWARD_MIB * MIB),
         cost_estimate=pl.CostEstimate(flops=6 * rows * tokens * width, bytes_accessed=8 << 20, transcendentals=0),
         name="forward0" if first else "forward1",
     )(at, *pieces, *weights)
@@ -138,7 +140,7 @@
         out_shape=jax.ShapeDtypeStruct(parts.shape, bf16),
         in_specs=[VM, VM, VM],
         out_specs=VM,
-        compiler_params=pltpu.CompilerParams(vmem_limit_bytes=8 * MIB),
+        compiler_params=pltpu.CompilerParams(vmem_limit_bytes=SMALL_MIB * MIB),
         cost_estimate=pl.CostEstimate(flops=n * tok * width, bytes_accessed=4 * n * tok * width, transcendentals=0),
         name="own_slopes",
     )(parts, x, y)
@@ -163,10 +165,10 @@
     width = z.shape[1]
     return pl.pallas_call(
         slope_kernel,
-        out_shape=jax.ShapeDtypeStruct((3, rows, tokens), bf16),
+        out_shape=pltpu.VMEM((3, rows, tokens), bf16),
         in_specs=[VM] * 5,
         out_specs=VM,
-        compiler_params=pltpu.CompilerParams(vmem_limit_bytes=12 * MIB),
+        compiler_params=pltpu.CompilerParams(vmem_limit_bytes=SMALL_MIB * MIB),
         cost_estimate=pl.CostEstimate(flops=2 * rows * tokens * width, bytes_accessed=4 << 20, transcendentals=0),
         name="slope_parts",
     )(z, w, gate, up, hidden)
@@ -227,7 +229,7 @@
     args = [a for part in parts for a in part]
     return pl.pallas_call(
         functools.partial(adam_kernel, steps, ps, r_of, min(512, quarter)),
-        out_shape=jax.ShapeDtypeStruct((np_, nr, rows, quarter), bf16),
+        out_shape=pltpu.VMEM((np_, nr, rows, quarter), bf16),
         grid_spec=pltpu.PrefetchScalarGridSpec(
             num_scalar_prefetch=1,
             grid=(nr,),
@@ -235,7 +237,7 @@
             out_specs=VM,
             scratch_shapes=[pltpu.VMEM((np_, rows, quarter), f32)] * steps,
         ),
-        compiler_params=pltpu.CompilerParams(vmem_limit_bytes=32 * MIB),
+        compiler_params=pltpu.CompilerParams(vmem_limit_bytes=ADAM_MIB * MIB),
         cost_estimate=pl.CostEstimate(
             flops=np_ * nr * steps * 2 * rows * tokens * quarter, bytes_accessed=np_ * nr * rows * quarter * 8, transcendentals=0
         ),
@@ -267,40 +269,43 @@
     def across(array):
         return lax.ppermute(array, "zh", [(0, 1), (1, 0)])
 
+    steps, tok, width = inputs.shape
+    half = width // 2
+    pair = collect(inputs, "zl")
+    told = jnp.max(jnp.stack([(e == jnp.arange(128, dtype=jnp.int32)).astype(bf16) for e in around(overflow_step, "zl")]), axis=0)
     own = [weights[0:2].astype(bf16), weights[2:3].astype(bf16)]
-    far = [across(chunk) for chunk in own]
+    far = []
+    for chunk in own:
+        far.append(across(chunk))
     near = [partner(chunk) for chunk in own]
     both = [partner(chunk) for chunk in far]
     w = own + near + far + both
 
-    inputs, targets = own_order(inputs), own_order(targets)
-    steps, tok, width = inputs.shape
-    half = width // 2
-    marks = (overflow_step.reshape(1, 1) == jnp.arange(128, dtype=jnp.int32).reshape(1, 128)).astype(bf16)
-    marks = jnp.broadcast_to(marks, (tok, 128))
-    pair = collect(jnp.concatenate([inputs[0], marks, inputs[1]], axis=1), "zl")
-    pieces = []
-    for k in range(steps):
-        low = k * (width + 128)
-        first, second = pair[..., low : low + half], pair[..., low + half : low + width + (128 if k == 0 else 0)]
-        if k:
-            first, second, *middle = lax.optimization_barrier((first, second, *middle))
-        middle = [collect(first, "y"), collect(second, "x")]
-        flat = [m.reshape(-1, m.shape[-1]) for m in middle]
-        pieces.append(around(flat[0], "x") + around(flat[1], "y"))
-    marked = functools.reduce(jnp.maximum, [jnp.max(p[:, half : half + steps], axis=0) for p in pieces[0][4:]])
+    inputs, targets, pair = own_order(inputs), own_order(targets), own_order(pair.reshape(2 * steps, tok, width))
+    pair = pair.reshape(2, steps, tok, width)
+    marks = jnp.broadcast_to(told.reshape(1, 1, 128), (2, tok, 128))
+    low = jnp.concatenate([pair[:, k, :, :half] for k in range(steps)], axis=2)
+    high = jnp.concatenate([pair[:, k, :, half:] for k in range(steps)] + [marks], axis=2)
+    flat = [m.reshape(-1, m.shape[-1]) for m in (collect(low, "y"), collect(high, "x"))]
+    pieces = around(flat[0], "x") + around(flat[1], "y")
+    begin = steps * half
+    marked = functools.reduce(jnp.maximum, [jnp.max(p[:, begin : begin + steps], axis=0) for p in pieces[4:]])
     coef = coefficients([marked[s] > 0 for s in range(steps)])
     pos = mine.reshape(1).astype(jnp.int32)
+    first_moment = pltpu.with_memory_space_constraint(first_moment, pltpu.HBM)
+    second_moment = pltpu.with_memory_space_constraint(second_moment, pltpu.HBM)
     at = jnp.stack([lax.axis_index("x"), lax.axis_index("y")]).astype(jnp.int32)
 
+    xs, ys = [inputs[k] for k in range(steps)], [targets[k] for k in range(steps)]
     parts = []
     w_start = None
     for k in range(steps):
-        x, gate, up, hidden, sums, *w0 = forward(at, pieces[k], w, rows)
+        x, gate, up, hidden, sums, *w0 = forward(at, k, pieces, w, rows)
         if k == 0:
             w = w_start = w0[0]
+            sums, coef, xs, ys = lax.optimization_barrier((sums, coef, xs, ys))
         arrived = lax.all_to_all(sums.reshape(-1, tok, width), FSDP, 0, 0, tiled=True)
-        copies = own_slopes(arrived, inputs[k], targets[k])
+        copies = own_slopes(arrived, xs[k], ys[k])
         z = lax.all_to_all(copies, FSDP, 0, 0, tiled=True).reshape(-1, width)
         parts.append((x, z, slope_parts(z, w, gate, up, hidden)))
         if k == 0:

time: 361 us -> 303 us (0.84)
  blocking collectives: 52.9 us -> 127 us
  waiting for transfers between devices: 122 us -> 70.9 us
  starting transfers between devices: 87.1 us -> 48.9 us
  local copies, waits for them, and re-layouts: 30.5 us -> 1.34 us
  Pallas kernels: 52.6 us -> 44.3 us
  other arithmetic: 11.2 us -> 7.23 us
    all_to_all x1 -> x2, blocking collectives: 25.4 us -> 64.3 us  [round_of(): lax.all_to_all(sums.reshape(-1, tok, width), FSDP, 0, 0, tiled=True)]
    all_to_all x1 -> x2, blocking collectives: 27.5 us -> 62.3 us  [round_of(): z = lax.all_to_all(copies, FSDP, 0, 0, tiled=True).reshape(-1, width)]
    unnamed x74 -> x23, local copies, waits for them, and re-layouts: 25.6 us -> 0.17 us
    ppermute x25 -> x14, waiting for transfers between devices: 63.6 us -> 39.1 us  [around(): lax.ppermute(own, dim, [(i, (i - s) % n) for i in range(n)])]
    all_to_all x2 -> x0, waiting for transfers between devices: 24.5 us -> none  [the longest x1 15.8 us: round_of(): lax.all_to_all(sums.reshape(-1, tok, width), FSDP, 0, 0, tiled=True)]
    ppermute x25 -> x14, starting transfers between devices: 38.7 us -> 21.4 us  [around(): lax.ppermute(own, dim, [(i, (i - s) % n) for i in range(n)])]
    ppermute x8, starting transfers between devices: 29.5 us -> 17.7 us  [partner(): return lax.ppermute(array, 'co', [(0, 1), (1, 0)])]
    all_to_all x2 -> x0, starting transfers between devices: 10.8 us -> none  [the longest x1 5.94 us: round_of(): lax.all_to_all(sums.reshape(-1, tok, width), FSDP, 0, 0, tiled=True)]
  transfers between devices with their start and end apart: 40 -> 27, of which waited for: 21 -> 14; matrix products, arithmetic and copies ran while one was open for 5% -> 1% of each run, Pallas kernels for 5% -> 0%
where the time goes in v2:
time: 303 us; the launch traced here: 302 us
  blocking collectives  127 us (42%)
  waiting for transfers between devices  70.9 us (23%)
  starting transfers between devices  48.9 us (16%)
  Pallas kernels  44.3 us (15%)
  other arithmetic  7.23 us (2%)
  between operations  3.16 us (1%)
    all_to_all x2, blocking collectives, round_of(): lax.all_to_all(sums.reshape(-1, tok, width), FSDP, 0, 0, tiled=True)  64.3 us
    all_to_all x2, blocking collectives, round_of(): z = lax.all_to_all(copies, FSDP, 0, 0, tiled=True).reshape(-1, width)  62.3 us
    ppermute x14, waiting for transfers between devices, around(): lax.ppermute(own, dim, [(i, (i - s) % n) for i in range(n)])  39.1 us
    pallas_call x5, Pallas kernels, adam(): pl.pallas_call(functools.partial(adam_kernel, steps, ps, r_of, min(512, q...  35.9 us
    ppermute x5, waiting for transfers between devices, across(): return lax.ppermute(array, 'zh', [(0, 1), (1, 0)])  27.5 us
    ppermute x14, starting transfers between devices, around(): lax.ppermute(own, dim, [(i, (i - s) % n) for i in range(n)])  21.4 us
    ppermute x8, starting transfers between devices, partner(): return lax.ppermute(array, 'co', [(0, 1), (1, 0)])  17.7 us
    ppermute x5, starting transfers between devices, across(): return lax.ppermute(array, 'zh', [(0, 1), (1, 0)])  9.76 us
  transfers between devices with their start and end apart: 27, of which 14 were waited for; matrix products, arithmetic and copies ran while one was open for 1% of the time, Pallas kernels for 0%

profile of v2, /device:TPU:1, one launch (start us, length us, event | category | flops | bytes accessed | tf_op | source)
XLA Modules:
  0.0 302.4 jit_solution(5199874946887546176)
XLA Ops:
  5.3 3.4 %collective-permute-start.17 = (bf16[1,224,1024]{2,1,0:T(8,128)(2,1)S(1)}, bf16[1,224,1024]{2,1,0:T(8,128)(2,1)S(1)}, u32[]{:S(2)}, u32[]{:S(2)}) collective-permute-start(bf16[1,224,1024]{2,1,0:T(8,128)(2,1)S(1)} %slice.103.refs_9_), channel_id=1, source_target_pairs={{0,64},{64,0},{1,65},{65,1},{2,66},{66,2},{3,67},{67,3},{4,68},{68... | collective-permute-start | bytes 1376264 | tf_op jit(solution)/shard_map/ppermute | solution.py:270
  15.2 3.7 %collective-permute-done.1 = bf16[2,8,4096]{2,1,0:T(8,128)(2,1)S(1)} collective-permute-done((bf16[2,8,4096]{2,1,0:T(8,128)(2,1)S(1)}, bf16[2,8,4096]{2,1,0:T(8,128)(2,1)S(1)}, u32[]{:S(2)}, u32[]{:S(2)}) %collective-permute-start.1) | collective-permute-done | bytes 131104 | tf_op jit(solution)/shard_map/ppermute | solution.py:33
  33.1 9.1 %collective-permute-done.13.refs_7_ = bf16[64,4224]{1,0:T(8,128)(2,1)S(1)} collective-permute-done((bf16[64,4224]{1,0:T(8,128)(2,1)S(1)}, bf16[64,4224]{1,0:T(8,128)(2,1)S(1)}, u32[]{:S(2)}, u32[]{:S(2)}) %collective-permute-start.13) | collective-permute-done | bytes 540704 | tf_op jit(solution)/shard_map/ppermute | solution.py:33
  42.2 4.1 %collective-permute-start.15 = (bf16[1,224,1024]{2,1,0:T(8,128)(2,1)S(1)}, bf16[1,224,1024]{2,1,0:T(8,128)(2,1)S(1)}, u32[]{:S(2)}, u32[]{:S(2)}) collective-permute-start(bf16[1,224,1024]{2,1,0:T(8,128)(2,1)S(1)} %slice.103.refs_9_), channel_id=1, source_target_pairs={{0,32},{32,0},{1,33},{33,1},{2,34},{34,2},{3,35},{35,3},{4,36},{36... | collective-permute-start | bytes 1376264 | tf_op jit(solution)/shard_map/ppermute | solution.py:267
  46.3 8.5 %collective-permute-done.12.refs_6_ = bf16[64,4224]{1,0:T(8,128)(2,1)S(1)} collective-permute-done((bf16[64,4224]{1,0:T(8,128)(2,1)S(1)}, bf16[64,4224]{1,0:T(8,128)(2,1)S(1)}, u32[]{:S(2)}, u32[]{:S(2)}) %collective-permute-start.12) | collective-permute-done | bytes 540704 | tf_op jit(solution)/shard_map/ppermute | solution.py:33
  55.7 3.3 %collective-permute-start.14 = (bf16[2,224,1024]{2,1,0:T(8,128)(2,1)S(1)}, bf16[2,224,1024]{2,1,0:T(8,128)(2,1)S(1)}, u32[]{:S(2)}, u32[]{:S(2)}) collective-permute-start(bf16[2,224,1024]{2,1,0:T(8,128)(2,1)S(1)} %slice.102.refs_8_), channel_id=1, source_target_pairs={{0,32},{32,0},{1,33},{33,1},{2,34},{34,2},{3,35},{35,3},{4,36},{36... | collective-permute-start | bytes 2752520 | tf_op jit(solution)/shard_map/ppermute | solution.py:267
  62.3 4.3 %collective-permute-done.6.refs_3_ = bf16[64,4096]{1,0:T(8,128)(2,1)S(1)} collective-permute-done((bf16[64,4096]{1,0:T(8,128)(2,1)S(1)}, bf16[64,4096]{1,0:T(8,128)(2,1)S(1)}, u32[]{:S(2)}, u32[]{:S(2)}) %collective-permute-start.6) | collective-permute-done | bytes 524320 | tf_op jit(solution)/shard_map/ppermute | solution.py:33
  66.6 5.9 %collective-permute-start.19 = (bf16[1,224,1024]{2,1,0:T(8,128)(2,1)S(1)}, bf16[1,224,1024]{2,1,0:T(8,128)(2,1)S(1)}, u32[]{:S(2)}, u32[]{:S(2)}) collective-permute-start(bf16[1,224,1024]{2,1,0:T(8,128)(2,1)S(1)} %collective-permute-done.17.refs_13_), channel_id=1, source_target_pairs={{0,32},{32,0},{1,33},{33,1},{2,34},{34,2},{3,35},{35,3},{4,36},{36... | collective-permute-start | bytes 1376264 | tf_op jit(solution)/shard_map/ppermute | solution.py:267
  74.6 4.4 %collective-permute-done.5.refs_2_ = bf16[64,4096]{1,0:T(8,128)(2,1)S(1)} collective-permute-done((bf16[64,4096]{1,0:T(8,128)(2,1)S(1)}, bf16[64,4096]{1,0:T(8,128)(2,1)S(1)}, u32[]{:S(2)}, u32[]{:S(2)}) %collective-permute-start.5) | collective-permute-done | bytes 524320 | tf_op jit(solution)/shard_map/ppermute | solution.py:33
  79.0 5.6 %collective-permute-done.4.refs_1_ = bf16[64,4096]{1,0:T(8,128)(2,1)S(1)} collective-permute-done((bf16[64,4096]{1,0:T(8,128)(2,1)S(1)}, bf16[64,4096]{1,0:T(8,128)(2,1)S(1)}, u32[]{:S(2)}, u32[]{:S(2)}) %collective-permute-start.4) | collective-permute-done | bytes 524320 | tf_op jit(solution)/shard_map/ppermute | solution.py:33
  87.8 33.1 %all_to_all.20.parts_ref = bf16[32,8,4096]{2,1,0:T(8,128)(2,1)S(1)} all-to-all(bf16[32,8,4096]{2,1,0:T(8,128)(2,1)S(1)} %bitcast.118), channel_id=1, replica_groups=mesh['zh'=2,'co'=2,'x'=4,'zl'=2,'y'=4] {'x','y','zl'}, dimensions={0} | all-to-all | bytes 4194304 | tf_op jit(solution)/shard_map/all_to_all | solution.py:307
  121.3 31.0 %all_to_all.21 = bf16[32,8,4096]{2,1,0:T(8,128)(2,1)S(1)} all-to-all(bf16[32,8,4096]{2,1,0:T(8,128)(2,1)S(1)} %own_slopes.2), channel_id=1, replica_groups=mesh['zh'=2,'co'=2,'x'=4,'zl'=2,'y'=4] {'x','y','zl'}, dimensions={0} | all-to-all | bytes 4194304 | tf_op jit(solution)/shard_map/all_to_all | solution.py:309
  153.1 12.1 %shard_map.158.refs_8_.w_ref = bf16[3,4,224,1024]{3,2,1,0:T(8,128)(2,1)S(1)} custom-call(s32[1]{0:T(128)} %bitcast.pos, f32[24]{0:T(128)S(1)} %pad_maximum_fusion.5.coef, bf16[1,3,224,4096]{3,2,1,0:T(8,128)(2,1)} %m_ref.9, bf16[1,3,224,4096]{3,2,1,0:T(8,128)(2,1)} %v_ref.9, bf16[3,4,224,1024]{3,2,1,0:T(8,128)(2,1)S(1)} %get-tuple-element.27.w_ref, ...), custom_call_target="tpu_custom_call" | custom-call | flops 1409286144 | bytes 22020096 | tf_op jit(solution)/shard_map/pallas_call | solution.py:230
  168.1 31.2 %all_to_all.22.parts_ref = bf16[32,8,4096]{2,1,0:T(8,128)(2,1)S(1)} all-to-all(bf16[32,8,4096]{2,1,0:T(8,128)(2,1)S(1)} %bitcast.119), channel_id=1, replica_groups=mesh['zh'=2,'co'=2,'x'=4,'zl'=2,'y'=4] {'x','y','zl'}, dimensions={0} | all-to-all | bytes 4194304 | tf_op jit(solution)/shard_map/all_to_all | solution.py:307
  199.7 31.3 %all_to_all.23 = bf16[32,8,4096]{2,1,0:T(8,128)(2,1)S(1)} all-to-all(bf16[32,8,4096]{2,1,0:T(8,128)(2,1)S(1)} %own_slopes.3), channel_id=1, replica_groups=mesh['zh'=2,'co'=2,'x'=4,'zl'=2,'y'=4] {'x','y','zl'}, dimensions={0} | all-to-all | bytes 4194304 | tf_op jit(solution)/shard_map/all_to_all | solution.py:309
  231.8 4.4 %shard_map.159 = bf16[1,2,224,1024]{3,2,1,0:T(8,128)(2,1)S(1)} custom-call(s32[1]{0:T(128)} %bitcast.pos, f32[24]{0:T(128)S(1)} %pad_maximum_fusion.5.coef, bf16[1,3,224,4096]{3,2,1,0:T(8,128)(2,1)} %m_ref.9, bf16[1,3,224,4096]{3,2,1,0:T(8,128)(2,1)} %v_ref.9, bf16[3,4,224,1024]{3,2,1,0:T(8,128)(2,1)S(1)} %get-tuple-element.27.w_ref, ...), custom_call_target="tpu_custom_call" | custom-call | flops 469762048 | bytes 3670016 | tf_op jit(solution)/shard_map/pallas_call | solution.py:230
  240.8 4.4 %shard_map.160 = bf16[1,2,224,1024]{3,2,1,0:T(8,128)(2,1)S(1)} custom-call(s32[1]{0:T(128)} %bitcast.pos, f32[24]{0:T(128)S(1)} %pad_maximum_fusion.5.coef, bf16[1,3,224,4096]{3,2,1,0:T(8,128)(2,1)} %m_ref.9, bf16[1,3,224,4096]{3,2,1,0:T(8,128)(2,1)} %v_ref.9, bf16[3,4,224,1024]{3,2,1,0:T(8,128)(2,1)S(1)} %get-tuple-element.27.w_ref, ...), custom_call_target="tpu_custom_call" | custom-call | flops 469762048 | bytes 3670016 | tf_op jit(solution)/shard_map/pallas_call | solution.py:230
  247.4 4.4 %shard_map.161 = bf16[1,2,224,1024]{3,2,1,0:T(8,128)(2,1)S(1)} custom-call(s32[1]{0:T(128)} %bitcast.pos, f32[24]{0:T(128)S(1)} %pad_maximum_fusion.5.coef, bf16[1,3,224,4096]{3,2,1,0:T(8,128)(2,1)} %m_ref.9, bf16[1,3,224,4096]{3,2,1,0:T(8,128)(2,1)} %v_ref.9, bf16[3,4,224,1024]{3,2,1,0:T(8,128)(2,1)S(1)} %get-tuple-element.27.w_ref, ...), custom_call_target="tpu_custom_call" | custom-call | flops 469762048 | bytes 3670016 | tf_op jit(solution)/shard_map/pallas_call | solution.py:230
  254.0 10.5 %shard_map.162 = bf16[3,2,224,1024]{3,2,1,0:T(8,128)(2,1)S(1)} custom-call(s32[1]{0:T(128)} %bitcast.pos, f32[24]{0:T(128)S(1)} %pad_maximum_fusion.5.coef, bf16[1,3,224,4096]{3,2,1,0:T(8,128)(2,1)} %m_ref.9, bf16[1,3,224,4096]{3,2,1,0:T(8,128)(2,1)} %v_ref.9, bf16[3,4,224,1024]{3,2,1,0:T(8,128)(2,1)S(1)} %get-tuple-element.27.w_ref, ...), custom_call_target="tpu_custom_call" | custom-call | flops 1409286144 | bytes 11010048 | tf_op jit(solution)/shard_map/pallas_call | solution.py:230
  265.0 3.3 %collective-permute-start.26 = (bf16[224,1024]{1,0:T(8,128)(2,1)S(1)}, bf16[224,1024]{1,0:T(8,128)(2,1)S(1)}, u32[]{:S(2)}, u32[]{:S(2)}) collective-permute-start(bf16[224,1024]{1,0:T(8,128)(2,1)S(1)} %fusion.4), channel_id=1, source_target_pairs={{0,64},{64,0},{1,65},{65,1},{2,66},{66,2},{3,67},{67,3},{4,68},{68... | collective-permute-start | bytes 1376264 | tf_op jit(solution)/shard_map/ppermute | solution.py:270
  271.3 7.8 %collective-permute-done.26 = bf16[224,1024]{1,0:T(8,128)(2,1)S(1)} collective-permute-done((bf16[224,1024]{1,0:T(8,128)(2,1)S(1)}, bf16[224,1024]{1,0:T(8,128)(2,1)S(1)}, u32[]{:S(2)}, u32[]{:S(2)}) %collective-permute-start.26) | collective-permute-done | bytes 458784 | tf_op jit(solution)/shard_map/ppermute | solution.py:270
  279.0 9.8 %collective-permute-done.24 = bf16[224,1024]{1,0:T(8,128)(2,1)S(1)} collective-permute-done((bf16[224,1024]{1,0:T(8,128)(2,1)S(1)}, bf16[224,1024]{1,0:T(8,128)(2,1)S(1)}, u32[]{:S(2)}, u32[]{:S(2)}) %collective-permute-start.24) | collective-permute-done | bytes 458784 | tf_op jit(solution)/shard_map/ppermute | solution.py:270
  288.9 9.8 %collective-permute-done.25 = bf16[224,1024]{1,0:T(8,128)(2,1)S(1)} collective-permute-done((bf16[224,1024]{1,0:T(8,128)(2,1)S(1)}, bf16[224,1024]{1,0:T(8,128)(2,1)S(1)}, u32[]{:S(2)}, u32[]{:S(2)}) %collective-permute-start.25) | collective-permute-done | bytes 458784 | tf_op jit(solution)/shard_map/ppermute | solution.py:270
  298.7 3.7 %multiply_subtract_fusion = (f32[3,224,1024]{2,1,0:T(8,128)}, f32[3,224,1024]{2,1,0:T(8,128)}) fusion(f32[3,224,1024]{2,1,0:T(8,128)S(1)} %copy-done, bf16[3,224,1024]{2,1,0:T(8,128)(2,1)S(1)} %collective-permute-done.23, bf16[3,2,224,1024]{3,2,1,0:T(8,128)(2,1)S(1)} %shard_map.162, bf16[1,224,1024]{2,1,0:T(8,128)(2,1)S(1)} %bitcast.123, ...), kind=kLoop, calls=%fused_computation.3 | loop fusion | flops 9633792 | bytes 15138816 | tf_op jit(solution)/shard_map/sub | solution.py:324
  (107 shorter events, 50.0 us)
Async XLA Ops:
  0.6 9.1 %collective-permute-start.7 = (s32[1,1]{1,0:T(1,128)}, s32[1,1]{1,0:T(1,128)}, u32[]{:S(2)}, u32[]{:S(2)}) collective-permute-start(s32[1,1]{1,0:T(1,128)} %param.21), channel_id=1, source_target_pairs={{0,4},{4,0},{1,5},{5,1},{2,6},{6,2},{3,7},{7,3},{8,12},{12,8},{9,1... | collective-permute-start | bytes 20 | tf_op jit(solution)/shard_map/ppermute | solution.py:33
  3.2 7.2 %collective-permute-start = (bf16[2,8,4096]{2,1,0:T(8,128)(2,1)}, bf16[2,8,4096]{2,1,0:T(8,128)(2,1)S(1)}, u32[]{:S(2)}, u32[]{:S(2)}) collective-permute-start(bf16[2,8,4096]{2,1,0:T(8,128)(2,1)} %param.19), channel_id=1, source_target_pairs={{0,4},{4,0},{1,5},{5,1},{2,6},{6,2},{3,7},{7,3},{8,12},{12,8},{9,1... | collective-permute-start | bytes 393224 | tf_op jit(solution)/shard_map/ppermute | solution.py:33
  5.3 53.9 %collective-permute-start.17 = (bf16[1,224,1024]{2,1,0:T(8,128)(2,1)S(1)}, bf16[1,224,1024]{2,1,0:T(8,128)(2,1)S(1)}, u32[]{:S(2)}, u32[]{:S(2)}) collective-permute-start(bf16[1,224,1024]{2,1,0:T(8,128)(2,1)S(1)} %slice.103.refs_9_), channel_id=1, source_target_pairs={{0,64},{64,0},{1,65},{65,1},{2,66},{66,2},{3,67},{67,3},{4,68},{68... | collective-permute-start | bytes 1376264 | tf_op jit(solution)/shard_map/ppermute | solution.py:270
  8.8 50.2 %collective-permute-start.16 = (bf16[2,224,1024]{2,1,0:T(8,128)(2,1)S(1)}, bf16[2,224,1024]{2,1,0:T(8,128)(2,1)S(1)}, u32[]{:S(2)}, u32[]{:S(2)}) collective-permute-start(bf16[2,224,1024]{2,1,0:T(8,128)(2,1)S(1)} %slice.102.refs_8_), channel_id=1, source_target_pairs={{0,64},{64,0},{1,65},{65,1},{2,66},{66,2},{3,67},{67,3},{4,68},{68... | collective-permute-start | bytes 2752520 | tf_op jit(solution)/shard_map/ppermute | solution.py:270
  10.6 9.5 %collective-permute-start.2 = (bf16[2,8,4096]{2,1,0:T(8,128)(2,1)S(1)}, bf16[2,8,4096]{2,1,0:T(8,128)(2,1)S(1)}, u32[]{:S(2)}, u32[]{:S(2)}) collective-permute-start(bf16[2,8,4096]{2,1,0:T(8,128)(2,1)S(1)} %pad_maximum_fusion.2), channel_id=1, source_target_pairs={{0,2},{1,3},{2,0},{3,1},{4,6},{5,7},{6,4},{7,5},{8,10},{9,11},{10,... | collective-permute-start | bytes 393224 | tf_op jit(solution)/shard_map/ppermute | solution.py:33
  13.6 5.3 %collective-permute-start.1 = (bf16[2,8,4096]{2,1,0:T(8,128)(2,1)S(1)}, bf16[2,8,4096]{2,1,0:T(8,128)(2,1)S(1)}, u32[]{:S(2)}, u32[]{:S(2)}) collective-permute-start(bf16[2,8,4096]{2,1,0:T(8,128)(2,1)S(1)} %pad_maximum_fusion.2), channel_id=1, source_target_pairs={{0,3},{1,0},{2,1},{3,2},{4,7},{5,4},{6,5},{7,6},{8,11},{9,8},{10,9... | collective-permute-start | bytes 393224 | tf_op jit(solution)/shard_map/ppermute | solution.py:33
  14.4 8.3 %collective-permute-start.3 = (bf16[2,8,4096]{2,1,0:T(8,128)(2,1)S(1)}, bf16[2,8,4096]{2,1,0:T(8,128)(2,1)S(1)}, u32[]{:S(2)}, u32[]{:S(2)}) collective-permute-start(bf16[2,8,4096]{2,1,0:T(8,128)(2,1)S(1)} %pad_maximum_fusion.2), channel_id=1, source_target_pairs={{0,1},{1,2},{2,3},{3,0},{4,5},{5,6},{6,7},{7,4},{8,9},{9,10},{10,1... | collective-permute-start | bytes 393224 | tf_op jit(solution)/shard_map/ppermute | solution.py:33
  18.9 8.4 %collective-permute-start.10 = (bf16[2,8,4224]{2,1,0:T(8,128)(2,1)S(1)}, bf16[2,8,4224]{2,1,0:T(8,128)(2,1)S(1)}, u32[]{:S(2)}, u32[]{:S(2)}) collective-permute-start(bf16[2,8,4224]{2,1,0:T(8,128)(2,1)S(1)} %get-tuple-element.51), channel_id=1, source_target_pairs={{0,8},{8,16},{16,24},{24,0},{1,9},{9,17},{17,25},{25,1},{2,10},{10... | collective-permute-start | bytes 405512 | tf_op jit(solution)/shard_map/ppermute | solution.py:33
  20.1 7.1 %collective-permute-start.9 = (bf16[2,8,4224]{2,1,0:T(8,128)(2,1)S(1)}, bf16[2,8,4224]{2,1,0:T(8,128)(2,1)S(1)}, u32[]{:S(2)}, u32[]{:S(2)}) collective-permute-start(bf16[2,8,4224]{2,1,0:T(8,128)(2,1)S(1)} %get-tuple-element.51), channel_id=1, source_target_pairs={{0,16},{8,24},{16,0},{24,8},{1,17},{9,25},{17,1},{25,9},{2,18},{10... | collective-permute-start | bytes 405512 | tf_op jit(solution)/shard_map/ppermute | solution.py:33
  22.7 4.5 %collective-permute-start.8 = (bf16[2,8,4224]{2,1,0:T(8,128)(2,1)S(1)}, bf16[2,8,4224]{2,1,0:T(8,128)(2,1)S(1)}, u32[]{:S(2)}, u32[]{:S(2)}) collective-permute-start(bf16[2,8,4224]{2,1,0:T(8,128)(2,1)S(1)} %get-tuple-element.51), channel_id=1, source_target_pairs={{0,24},{8,0},{16,8},{24,16},{1,25},{9,1},{17,9},{25,17},{2,26},{10... | collective-permute-start | bytes 405512 | tf_op jit(solution)/shard_map/ppermute | solution.py:33
  27.4 14.8 %collective-permute-start.13 = (bf16[64,4224]{1,0:T(8,128)(2,1)S(1)}, bf16[64,4224]{1,0:T(8,128)(2,1)S(1)}, u32[]{:S(2)}, u32[]{:S(2)}) collective-permute-start(bf16[64,4224]{1,0:T(8,128)(2,1)S(1)} %bitcast.107), channel_id=1, source_target_pairs={{0,1},{1,2},{2,3},{3,0},{4,5},{5,6},{6,7},{7,4},{8,9},{9,10},{10,1... | collective-permute-start | bytes 1622024 | tf_op jit(solution)/shard_map/ppermute | solution.py:33
  30.4 24.4 %collective-permute-start.12 = (bf16[64,4224]{1,0:T(8,128)(2,1)S(1)}, bf16[64,4224]{1,0:T(8,128)(2,1)S(1)}, u32[]{:S(2)}, u32[]{:S(2)}) collective-permute-start(bf16[64,4224]{1,0:T(8,128)(2,1)S(1)} %bitcast.108), channel_id=1, source_target_pairs={{0,2},{1,3},{2,0},{3,1},{4,6},{5,7},{6,4},{7,5},{8,10},{9,11},{10,... | collective-permute-start | bytes 1622024 | tf_op jit(solution)/shard_map/ppermute | solution.py:33
  32.9 22.8 %collective-permute-start.11 = (bf16[64,4224]{1,0:T(8,128)(2,1)S(1)}, bf16[64,4224]{1,0:T(8,128)(2,1)S(1)}, u32[]{:S(2)}, u32[]{:S(2)}) collective-permute-start(bf16[64,4224]{1,0:T(8,128)(2,1)S(1)} %bitcast.109), channel_id=1, source_target_pairs={{0,3},{1,0},{2,1},{3,2},{4,7},{5,4},{6,5},{7,6},{8,11},{9,8},{10,9... | collective-permute-start | bytes 1622024 | tf_op jit(solution)/shard_map/ppermute | solution.py:33
  42.2 19.9 %collective-permute-start.15 = (bf16[1,224,1024]{2,1,0:T(8,128)(2,1)S(1)}, bf16[1,224,1024]{2,1,0:T(8,128)(2,1)S(1)}, u32[]{:S(2)}, u32[]{:S(2)}) collective-permute-start(bf16[1,224,1024]{2,1,0:T(8,128)(2,1)S(1)} %slice.103.refs_9_), channel_id=1, source_target_pairs={{0,32},{32,0},{1,33},{33,1},{2,34},{34,2},{3,35},{35,3},{4,36},{36... | collective-permute-start | bytes 1376264 | tf_op jit(solution)/shard_map/ppermute | solution.py:267
  54.8 11.8 %collective-permute-start.6 = (bf16[64,4096]{1,0:T(8,128)(2,1)S(1)}, bf16[64,4096]{1,0:T(8,128)(2,1)S(1)}, u32[]{:S(2)}, u32[]{:S(2)}) collective-permute-start(bf16[64,4096]{1,0:T(8,128)(2,1)S(1)} %bitcast.113), channel_id=1, source_target_pairs={{0,8},{8,16},{16,24},{24,0},{1,9},{9,17},{17,25},{25,1},{2,10},{10... | collective-permute-start | bytes 1572872 | tf_op jit(solution)/shard_map/ppermute | solution.py:33
  55.7 28.9 %collective-permute-start.14 = (bf16[2,224,1024]{2,1,0:T(8,128)(2,1)S(1)}, bf16[2,224,1024]{2,1,0:T(8,128)(2,1)S(1)}, u32[]{:S(2)}, u32[]{:S(2)}) collective-permute-start(bf16[2,224,1024]{2,1,0:T(8,128)(2,1)S(1)} %slice.102.refs_8_), channel_id=1, source_target_pairs={{0,32},{32,0},{1,33},{33,1},{2,34},{34,2},{3,35},{35,3},{4,36},{36... | collective-permute-start | bytes 2752520 | tf_op jit(solution)/shard_map/ppermute | solution.py:267
  59.0 25.6 %collective-permute-start.18 = (bf16[2,224,1024]{2,1,0:T(8,128)(2,1)S(1)}, bf16[2,224,1024]{2,1,0:T(8,128)(2,1)S(1)}, u32[]{:S(2)}, u32[]{:S(2)}) collective-permute-start(bf16[2,224,1024]{2,1,0:T(8,128)(2,1)S(1)} %collective-permute-done.16.refs_12_), channel_id=1, source_target_pairs={{0,32},{32,0},{1,33},{33,1},{2,34},{34,2},{3,35},{35,3},{4,36},{36... | collective-permute-start | bytes 2752520 | tf_op jit(solution)/shard_map/ppermute | solution.py:267
  59.2 19.8 %collective-permute-start.5 = (bf16[64,4096]{1,0:T(8,128)(2,1)S(1)}, bf16[64,4096]{1,0:T(8,128)(2,1)S(1)}, u32[]{:S(2)}, u32[]{:S(2)}) collective-permute-start(bf16[64,4096]{1,0:T(8,128)(2,1)S(1)} %bitcast.114), channel_id=1, source_target_pairs={{0,16},{8,24},{16,0},{24,8},{1,17},{9,25},{17,1},{25,9},{2,18},{10... | collective-permute-start | bytes 1572872 | tf_op jit(solution)/shard_map/ppermute | solution.py:33
  62.1 22.5 %collective-permute-start.4 = (bf16[64,4096]{1,0:T(8,128)(2,1)S(1)}, bf16[64,4096]{1,0:T(8,128)(2,1)S(1)}, u32[]{:S(2)}, u32[]{:S(2)}) collective-permute-start(bf16[64,4096]{1,0:T(8,128)(2,1)S(1)} %bitcast.115), channel_id=1, source_target_pairs={{0,24},{8,0},{16,8},{24,16},{1,25},{9,1},{17,9},{25,17},{2,26},{10... | collective-permute-start | bytes 1572872 | tf_op jit(solution)/shard_map/ppermute | solution.py:33
  66.6 18.0 %collective-permute-start.19 = (bf16[1,224,1024]{2,1,0:T(8,128)(2,1)S(1)}, bf16[1,224,1024]{2,1,0:T(8,128)(2,1)S(1)}, u32[]{:S(2)}, u32[]{:S(2)}) collective-permute-start(bf16[1,224,1024]{2,1,0:T(8,128)(2,1)S(1)} %collective-permute-done.17.refs_13_), channel_id=1, source_target_pairs={{0,32},{32,0},{1,33},{33,1},{2,34},{34,2},{3,35},{35,3},{4,36},{36... | collective-permute-start | bytes 1376264 | tf_op jit(solution)/shard_map/ppermute | solution.py:267
  264.6 34.2 %collective-permute-start.23 = (bf16[3,224,1024]{2,1,0:T(8,128)(2,1)S(1)}, bf16[3,224,1024]{2,1,0:T(8,128)(2,1)S(1)}, u32[]{:S(2)}, u32[]{:S(2)}) collective-permute-start(bf16[3,224,1024]{2,1,0:T(8,128)(2,1)S(1)} %slice_bitcast_fusion), channel_id=1, source_target_pairs={{0,32},{32,0},{1,33},{33,1},{2,34},{34,2},{3,35},{35,3},{4,36},{36... | collective-permute-start | bytes 4128776 | tf_op jit(solution)/shard_map/ppermute | solution.py:267
  265.0 14.0 %collective-permute-start.26 = (bf16[224,1024]{1,0:T(8,128)(2,1)S(1)}, bf16[224,1024]{1,0:T(8,128)(2,1)S(1)}, u32[]{:S(2)}, u32[]{:S(2)}) collective-permute-start(bf16[224,1024]{1,0:T(8,128)(2,1)S(1)} %fusion.4), channel_id=1, source_target_pairs={{0,64},{64,0},{1,65},{65,1},{2,66},{66,2},{3,67},{67,3},{4,68},{68... | collective-permute-start | bytes 1376264 | tf_op jit(solution)/shard_map/ppermute | solution.py:270
  268.3 20.6 %collective-permute-start.24 = (bf16[224,1024]{1,0:T(8,128)(2,1)S(1)}, bf16[224,1024]{1,0:T(8,128)(2,1)S(1)}, u32[]{:S(2)}, u32[]{:S(2)}) collective-permute-start(bf16[224,1024]{1,0:T(8,128)(2,1)S(1)} %fusion.3), channel_id=1, source_target_pairs={{0,64},{64,0},{1,65},{65,1},{2,66},{66,2},{3,67},{67,3},{4,68},{68... | collective-permute-start | bytes 1376264 | tf_op jit(solution)/shard_map/ppermute | solution.py:270
  268.3 30.4 %collective-permute-start.25 = (bf16[224,1024]{1,0:T(8,128)(2,1)S(1)}, bf16[224,1024]{1,0:T(8,128)(2,1)S(1)}, u32[]{:S(2)}, u32[]{:S(2)}) collective-permute-start(bf16[224,1024]{1,0:T(8,128)(2,1)S(1)} %fusion.2), channel_id=1, source_target_pairs={{0,64},{64,0},{1,65},{65,1},{2,66},{66,2},{3,67},{67,3},{4,68},{68... | collective-permute-start | bytes 1376264 | tf_op jit(solution)/shard_map/ppermute | solution.py:270
  (10 other events, 281.9 us)

commit v3 on v2

--- a/solution.py
+++ b/solution.py
@@ -50,13 +50,12 @@
 FORWARD_MIB, ADAM_MIB, SMALL_MIB = 6, 13, 4
 
 
-def forward_kernel(step, n_w, at_ref, *refs):
+def forward_kernel(n_w, at_ref, *refs):
     pieces, refs = refs[:8], refs[8:]
     w_refs, refs = refs[:n_w], refs[n_w:]
     x_out, gate_out, up_out, hidden_out, p_out = refs[:5]
     turn = refs[-1]
     quarter = x_out.shape[1] // 4
-    half = 2 * quarter
 
     def w(p, r):
         if n_w == 1:
@@ -65,13 +64,17 @@
 
     plane = pieces[0].shape[0]
     block = plane // 4
-    cols = slice(step * half, (step + 1) * half)
-    for s in range(4):
-        row = pl.multiple_of(((at_ref[0] + s) % 4) * plane, plane)
-        x_out[pl.ds(row, plane), 0:half] = pieces[s][:, cols]
-        for x in range(4):
-            row = pl.multiple_of(x * plane + ((at_ref[1] + s) % 4) * block, block)
-            x_out[pl.ds(row, block), half:] = pieces[4 + s][x * block : (x + 1) * block, cols]
+    for a in range(4):
+        source = slice(a % 2 * quarter, (a % 2 + 1) * quarter)
+        cols = pl.ds(pl.multiple_of((at_ref[2] ^ a) * quarter, quarter), quarter)
+        for s in range(4):
+            if a < 2:
+                row = pl.multiple_of(((at_ref[0] + s) % 4) * plane, plane)
+                x_out[pl.ds(row, plane), cols] = pieces[s][:, source]
+                continue
+            for x in range(4):
+                row = pl.multiple_of(x * plane + ((at_ref[1] + s) % 4) * block, block)
+                x_out[pl.ds(row, block), cols] = pieces[4 + s][x * block : (x + 1) * block, source]
     if n_w > 1:
         for p in range(3):
             for r in range(4):
@@ -97,9 +100,9 @@
         p_out[:, r * quarter : (r + 1) * quarter] = part.astype(bf16)
 
 
-def forward(at, step, pieces, w, rows):
+def forward(at, pieces, w, rows):
     first = isinstance(w, list)
-    tokens, width = 4 * pieces[0].shape[0], pieces[0].shape[1]
+    tokens, width = 4 * pieces[0].shape[0], 2 * pieces[0].shape[1]
     square = -(-max(rows, tokens) // 128) * 128
     small = pltpu.VMEM((rows, tokens), f32)
     wide = jax.ShapeDtypeStruct((tokens, width), bf16)
@@ -108,7 +111,7 @@
         outs.append(pltpu.VMEM((3, 4, rows, width // 4), bf16))
     weights = w if first else [w]
     return pl.pallas_call(
-        functools.partial(forward_kernel, step, len(weights)),
+        functools.partial(forward_kernel, len(weights)),
         out_shape=outs,
         in_specs=[SM] + [VM] * (8 + len(weights)),
         out_specs=[VM] * len(outs),
@@ -244,6 +247,38 @@
     )(pos, coef, first_moment, second_moment, w, *args)
 
 
+def settle_kernel(w_ref, m_ref, own_ref, near_ref, far_ref, *refs):
+    w_out, m_out = refs[-2:]
+    total = own_ref[0, 0].astype(f32) + near_ref[0].astype(f32) + far_ref[...].astype(f32)
+    delta = total * 0.25
+    new_momentum = nesterov_coef * m_ref[0] + delta
+    m_out[0] = new_momentum
+    w_out[0] = w_ref[0] - outer_rate * (delta + nesterov_coef * new_momentum)
+
+
+def settle(p, weights, momentum, own, near, far, before):
+    _, rows, quarter = weights.shape
+    half = rows // 2
+    block = pl.BlockSpec((1, half, quarter), lambda i: (p, i, 0))
+    shape = jax.ShapeDtypeStruct(weights.shape, f32)
+    return pl.pallas_call(
+        settle_kernel,
+        grid=(2,),
+        out_shape=[shape, shape],
+        in_specs=[
+            block,
+            block,
+            pl.BlockSpec((1, 1, half, quarter), lambda i: (p, 1, i, 0)),
+            block,
+            pl.BlockSpec((half, quarter), lambda i: (i, 0)),
+        ]
+        + [pl.BlockSpec(memory_space=pl.ANY)] * len(before),
+        out_specs=[block, block],
+        input_output_aliases={5 + k: k for k in range(len(before))},
+        compiler_params=pltpu.CompilerParams(vmem_limit_bytes=12 * MIB),
+    )(weights, momentum, own, near, far, *before)
+
+
 def coefficients(skipped):
     found = []
     for s in range(2):
@@ -281,26 +316,27 @@
     both = [partner(chunk) for chunk in far]
     w = own + near + far + both
 
-    inputs, targets, pair = own_order(inputs), own_order(targets), own_order(pair.reshape(2 * steps, tok, width))
-    pair = pair.reshape(2, steps, tok, width)
     marks = jnp.broadcast_to(told.reshape(1, 1, 128), (2, tok, 128))
     low = jnp.concatenate([pair[:, k, :, :half] for k in range(steps)], axis=2)
-    high = jnp.concatenate([pair[:, k, :, half:] for k in range(steps)] + [marks], axis=2)
+    high = jnp.concatenate([pair[:, 0, :, half:], marks] + [pair[:, k, :, half:] for k in range(1, steps)], axis=2)
     flat = [m.reshape(-1, m.shape[-1]) for m in (collect(low, "y"), collect(high, "x"))]
-    pieces = around(flat[0], "x") + around(flat[1], "y")
-    begin = steps * half
-    marked = functools.reduce(jnp.maximum, [jnp.max(p[:, begin : begin + steps], axis=0) for p in pieces[4:]])
+    pieces = []
+    for k in range(steps):
+        start, stop = (k * half + (128 if k else 0), (k + 1) * half + 128)
+        pieces.append(around(flat[0][:, k * half : (k + 1) * half], "x") + around(flat[1][:, start:stop], "y"))
+    inputs, targets = own_order(inputs), own_order(targets)
+    marked = functools.reduce(jnp.maximum, [jnp.max(p[:, half : half + steps], axis=0) for p in pieces[0][4:]])
     coef = coefficients([marked[s] > 0 for s in range(steps)])
     pos = mine.reshape(1).astype(jnp.int32)
     first_moment = pltpu.with_memory_space_constraint(first_moment, pltpu.HBM)
     second_moment = pltpu.with_memory_space_constraint(second_moment, pltpu.HBM)
-    at = jnp.stack([lax.axis_index("x"), lax.axis_index("y")]).astype(jnp.int32)
+    at = jnp.stack([lax.axis_index("x"), lax.axis_index("y"), mine]).astype(jnp.int32)
 
     xs, ys = [inputs[k] for k in range(steps)], [targets[k] for k in range(steps)]
     parts = []
     w_start = None
     for k in range(steps):
-        x, gate, up, hidden, sums, *w0 = forward(at, k, pieces, w, rows)
+        x, gate, up, hidden, sums, *w0 = forward(at, pieces[k], w, rows)
         if k == 0:
             w = w_start = w0[0]
             sums, coef, xs, ys = lax.optimization_barrier((sums, coef, xs, ys))
@@ -318,11 +354,10 @@
         arrived.append((p, across(joint)))
     rest = adam(pos, coef, first_moment, second_moment, w_start, parts, (range(3), (1, 0)))
     near_part = partner(rest[:, 0])
-    arrived = jnp.stack([a for _, a in sorted(arrived, key=lambda e: e[0])])
-    delta = (rest[:, 1].astype(f32) + near_part.astype(f32) + arrived.astype(f32)) / 4
-    new_momentum = nesterov_coef * momentum + delta
-    new_weights = weights - outer_rate * (delta + nesterov_coef * new_momentum)
-    return (new_weights, new_momentum)
+    result = ()
+    for p, far_part in arrived:
+        result = settle(p, weights, momentum, rest, near_part, far_part, result)
+    return tuple(result)
 
 
 def solution(mesh):

time: 303 us -> 300 us (0.990)
  blocking collectives: 127 us -> 94.3 us
  local copies, waits for them, and re-layouts: 1.34 us -> 15.6 us
  starting transfers between devices: 48.9 us -> 60.6 us
  Pallas kernels: 44.3 us -> 49.1 us
    all_to_all x2 -> x1, blocking collectives: 62.3 us -> 31.2 us  [round_of(): z = lax.all_to_all(copies, FSDP, 0, 0, tiled=True).reshape(-1, width)]
    ppermute x14 -> x20, starting transfers between devices: 21.4 us -> 34.3 us  [around(): lax.ppermute(own, dim, [(i, (i - s) % n) for i in range(n)])]
    unnamed x23 -> x57, local copies, waits for them, and re-layouts: 0.17 us -> 12 us
    ppermute x8, starting transfers between devices: 17.7 us -> 12.1 us  [partner(): return lax.ppermute(array, 'co', [(0, 1), (1, 0)])]
    pallas_call x2 -> x5, Pallas kernels: 6.03 us -> 10.9 us  [the longest x2 6.85 us: forward(): pl.pallas_call(functools.partial(forward_kernel, len(weights)), out_shape...]
    all_to_all x0 -> x1, starting transfers between devices: none -> 4.46 us  [round_of(): z = lax.all_to_all(copies, FSDP, 0, 0, tiled=True).reshape(-1, width)]
    ppermute x14 -> x20, waiting for transfers between devices: 39.1 us -> 43.1 us  [around(): lax.ppermute(own, dim, [(i, (i - s) % n) for i in range(n)])]
    sub x1 -> x0, other arithmetic: 3.67 us -> none  [round_of(): new_weights = weights - outer_rate * (delta + nesterov_coef * new_momentum)]
  transfers between devices with their start and end apart: 27 -> 34, of which waited for: 14 -> 14; matrix products, arithmetic and copies ran while one was open for 1% -> 3% of each run, Pallas kernels for 0% -> 5%
where the time goes in v3:
time: 300 us; the launch traced here: 299 us
  blocking collectives  94.3 us (31%)
  waiting for transfers between devices  72.1 us (24%)
  starting transfers between devices  60.6 us (20%)
  Pallas kernels  49.1 us (16%)
  local copies, waits for them, and re-layouts  15.6 us (5%)
  other arithmetic  4.52 us (2%)
  between operations  3.24 us (1%)
    all_to_all x2, blocking collectives, round_of(): lax.all_to_all(sums.reshape(-1, tok, width), FSDP, 0, 0, tiled=True)  63 us
    ppermute x20, waiting for transfers between devices, around(): lax.ppermute(own, dim, [(i, (i - s) % n) for i in range(n)])  43.1 us
    pallas_call x5, Pallas kernels, adam(): pl.pallas_call(functools.partial(adam_kernel, steps, ps, r_of, min(512, q...  35.8 us
    ppermute x20, starting transfers between devices, around(): lax.ppermute(own, dim, [(i, (i - s) % n) for i in range(n)])  34.3 us
    all_to_all x1, blocking collectives, round_of(): z = lax.all_to_all(copies, FSDP, 0, 0, tiled=True).reshape(-1, width)  31.2 us
    ppermute x5, waiting for transfers between devices, across(): return lax.ppermute(array, 'zh', [(0, 1), (1, 0)])  24.7 us
    ppermute x8, starting transfers between devices, partner(): return lax.ppermute(array, 'co', [(0, 1), (1, 0)])  12.1 us
    unnamed x57, local copies, waits for them, and re-layouts  12 us
  transfers between devices with their start and end apart: 34, of which 14 were waited for; matrix products, arithmetic and copies ran while one was open for 3% of the time, Pallas kernels for 5%

profile of v3, /device:TPU:1, one launch (start us, length us, event | category | flops | bytes accessed | tf_op | source)
XLA Modules:
  0.0 299.5 jit_solution(16540956256498207986)
XLA Ops:
  5.3 3.4 %collective-permute-start.17 = (bf16[1,224,1024]{2,1,0:T(8,128)(2,1)S(1)}, bf16[1,224,1024]{2,1,0:T(8,128)(2,1)S(1)}, u32[]{:S(2)}, u32[]{:S(2)}) collective-permute-start(bf16[1,224,1024]{2,1,0:T(8,128)(2,1)S(1)} %slice.118.refs_9_), channel_id=1, source_target_pairs={{0,64},{64,0},{1,65},{65,1},{2,66},{66,2},{3,67},{67,3},{4,68},{68... | collective-permute-start | bytes 1376264 | tf_op jit(solution)/shard_map/ppermute | solution.py:305
  16.1 3.8 %collective-permute-done.1 = bf16[2,8,4096]{2,1,0:T(8,128)(2,1)S(1)} collective-permute-done((bf16[2,8,4096]{2,1,0:T(8,128)(2,1)S(1)}, bf16[2,8,4096]{2,1,0:T(8,128)(2,1)S(1)}, u32[]{:S(2)}, u32[]{:S(2)}) %collective-permute-start.1) | collective-permute-done | bytes 131104 | tf_op jit(solution)/shard_map/ppermute | solution.py:33
  25.0 3.1 %collective-permute-done.8 = bf16[2,8,4224]{2,1,0:T(8,128)(2,1)S(1)} collective-permute-done((bf16[2,8,4224]{2,1,0:T(8,128)(2,1)S(1)}, bf16[2,8,4224]{2,1,0:T(8,128)(2,1)S(1)}, u32[]{:S(2)}, u32[]{:S(2)}) %collective-permute-start.8) | collective-permute-done | bytes 135200 | tf_op jit(solution)/shard_map/ppermute | solution.py:33
  37.6 4.1 %collective-permute-start.14 = (bf16[2,224,1024]{2,1,0:T(8,128)(2,1)S(1)}, bf16[2,224,1024]{2,1,0:T(8,128)(2,1)S(1)}, u32[]{:S(2)}, u32[]{:S(2)}) collective-permute-start(bf16[2,224,1024]{2,1,0:T(8,128)(2,1)S(1)} %slice.117.refs_8_), channel_id=1, source_target_pairs={{0,32},{32,0},{1,33},{33,1},{2,34},{34,2},{3,35},{35,3},{4,36},{36... | collective-permute-start | bytes 2752520 | tf_op jit(solution)/shard_map/ppermute | solution.py:302
  53.6 3.1 %collective-permute-done.6.refs_3_ = bf16[64,2048]{1,0:T(8,128)(2,1)S(1)} collective-permute-done((bf16[64,2048]{1,0:T(8,128)(2,1)S(1)}, bf16[64,2048]{1,0:T(8,128)(2,1)S(1)}, u32[]{:S(2)}, u32[]{:S(2)}) %collective-permute-start.6) | collective-permute-done | bytes 262176 | tf_op jit(solution)/shard_map/ppermute | solution.py:33
  58.0 5.2 %collective-permute-done.5.refs_2_ = bf16[64,2048]{1,0:T(8,128)(2,1)S(1)} collective-permute-done((bf16[64,2048]{1,0:T(8,128)(2,1)S(1)}, bf16[64,2048]{1,0:T(8,128)(2,1)S(1)}, u32[]{:S(2)}, u32[]{:S(2)}) %collective-permute-start.5) | collective-permute-done | bytes 262176 | tf_op jit(solution)/shard_map/ppermute | solution.py:33
  65.0 3.2 %forward0.1 = (bf16[256,4096]{1,0:T(8,128)(2,1)S(1)}, f32[224,256]{1,0:T(8,128)S(1)}, f32[224,256]{1,0:T(8,128)S(1)}, bf16[224,256]{1,0:T(8,128)(2,1)S(1)}, bf16...) custom-call(s32[3]{0:T(128)S(1)} %pad_add_fusion.at_ref, ...), custom_call_target="tpu_custom_call" | custom-call | flops 1409286144 | bytes 8388608 | tf_op jit(solution)/shard_map/forward0/pallas_call | solution.py:113
  70.6 33.1 %all_to_all.20.parts_ref = bf16[32,8,4096]{2,1,0:T(8,128)(2,1)S(1)} all-to-all(bf16[32,8,4096]{2,1,0:T(8,128)(2,1)S(1)} %bitcast.96), channel_id=1, replica_groups=mesh['zh'=2,'co'=2,'x'=4,'zl'=2,'y'=4] {'x','y','zl'}, dimensions={0} | all-to-all | bytes 4194304 | tf_op jit(solution)/shard_map/all_to_all | solution.py:343
  105.4 4.5 %all-to-all-start.1 = ((bf16[32,8,4096]{2,1,0:T(8,128)(2,1)}), bf16[32,8,4096]{2,1,0:T(8,128)(2,1)S(1)}, u32[]{:S(2)}, u32[]{:S(2)}) async-start(bf16[32,8,4096]{2,1,0:T(8,128)(2,1)} %copy-done.6), calls=%async_computation.1 | async-start | bytes 4194304 | tf_op jit(solution)/shard_map/all_to_all | solution.py:345
  120.1 20.4 %collective-permute-done.22.refs_3_ = bf16[64,2048]{1,0:T(8,128)(2,1)S(1)} collective-permute-done((bf16[64,2048]{1,0:T(8,128)(2,1)}, bf16[64,2048]{1,0:T(8,128)(2,1)S(1)}, u32[]{:S(2)}, u32[]{:S(2)}) %collective-permute-start.22) | collective-permute-done | bytes 262176 | tf_op jit(solution)/shard_map/ppermute | solution.py:33
  141.2 3.2 %collective-permute-start.23 = (bf16[64,2048]{1,0:T(8,128)(2,1)}, bf16[64,2048]{1,0:T(8,128)(2,1)}, u32[]{:S(2)}, u32[]{:S(2)}) collective-permute-start(bf16[64,2048]{1,0:T(8,128)(2,1)} %slice.128.refs_4_), channel_id=1, source_target_pairs={{0,3},{1,0},{2,1},{3,2},{4,7},{5,4},{6,5},{7,6},{8,11},{9,8},{10,9... | collective-permute-start | bytes 786440 | tf_op jit(solution)/shard_map/ppermute | solution.py:33
  152.5 12.1 %shard_map.158.refs_8_.w_ref = bf16[3,4,224,1024]{3,2,1,0:T(8,128)(2,1)S(1)} custom-call(s32[1]{0:T(128)} %bitcast.pos, f32[24]{0:T(128)S(1)} %pad_maximum_fusion.4.coef, bf16[1,3,224,4096]{3,2,1,0:T(8,128)(2,1)} %m_ref.12, bf16[1,3,224,4096]{3,2,1,0:T(8,128)(2,1)} %v_ref.9, bf16[3,4,224,1024]{3,2,1,0:T(8,128)(2,1)S(1)} %bitcast.84, ...), custom_call_target="tpu_custom_call" | custom-call | flops 1409286144 | bytes 22020096 | tf_op jit(solution)/shard_map/pallas_call | solution.py:233
  164.7 3.6 %forward1.1 = (bf16[256,4096]{1,0:T(8,128)(2,1)S(1)}, f32[224,256]{1,0:T(8,128)S(1)}, f32[224,256]{1,0:T(8,128)S(1)}, bf16[224,256]{1,0:T(8,128)(2,1)S(1)}, bf16[256,4096]{1,0:T(8,128)(2,1)S(1)}) custom-call(s32[3]{0:T(128)S(1)} %pad_add_fusion.at_ref, bf16[64,2048]{1,0:T(8,128)(2,1)S(1)} %copy-done.7, bf16[64,2048]{1,0:T(8,128)(2,1)} %collective-permute-done.20.refs_1_, ...), custom_call_target="tpu_custom_call" | custom-call | flops 1409286144 | bytes 8388608 | tf_op jit(solution)/shard_map/forward1/pallas_call | solution.py:113
  168.3 29.9 %all_to_all.21.parts_ref = bf16[32,8,4096]{2,1,0:T(8,128)(2,1)S(1)} all-to-all(bf16[32,8,4096]{2,1,0:T(8,128)(2,1)S(1)} %bitcast.97), channel_id=1, replica_groups=mesh['zh'=2,'co'=2,'x'=4,'zl'=2,'y'=4] {'x','y','zl'}, dimensions={0} | all-to-all | bytes 4194304 | tf_op jit(solution)/shard_map/all_to_all | solution.py:343
  198.7 31.2 %all_to_all.22 = bf16[32,8,4096]{2,1,0:T(8,128)(2,1)S(1)} all-to-all(bf16[32,8,4096]{2,1,0:T(8,128)(2,1)S(1)} %own_slopes.3), channel_id=1, replica_groups=mesh['zh'=2,'co'=2,'x'=4,'zl'=2,'y'=4] {'x','y','zl'}, dimensions={0} | all-to-all | bytes 4194304 | tf_op jit(solution)/shard_map/all_to_all | solution.py:345
  230.8 4.4 %shard_map.159 = bf16[1,2,224,1024]{3,2,1,0:T(8,128)(2,1)S(1)} custom-call(s32[1]{0:T(128)} %bitcast.pos, f32[24]{0:T(128)S(1)} %pad_maximum_fusion.4.coef, bf16[1,3,224,4096]{3,2,1,0:T(8,128)(2,1)} %m_ref.12, bf16[1,3,224,4096]{3,2,1,0:T(8,128)(2,1)} %v_ref.9, bf16[3,4,224,1024]{3,2,1,0:T(8,128)(2,1)S(1)} %bitcast.84, bf16[256,4096]{1,0:T(8,128)(2,1)S(1)} %copy-done.3, ...), custom_call_target="tpu_custom_call" | custom-call | flops 469762048 | bytes 3670016 | tf_op jit(solution)/shard_map/pallas_call | solution.py:233
  235.2 3.5 %collective-permute-start.26 = (bf16[224,1024]{1,0:T(8,128)(2,1)S(1)}, bf16[224,1024]{1,0:T(8,128)(2,1)S(1)}, u32[]{:S(2)}, u32[]{:S(2)}) collective-permute-start(bf16[224,1024]{1,0:T(8,128)(2,1)S(1)} %slice_bitcast_fusion.5), channel_id=1, source_target_pairs={{0,32},{32,0},{1,33},{33,1},{2,34},{34,2},{3,35},{35,3},{4,36},{36... | collective-permute-start | bytes 1376264 | tf_op jit(solution)/shard_map/ppermute | solution.py:302
  240.3 4.4 %shard_map.160 = bf16[1,2,224,1024]{3,2,1,0:T(8,128)(2,1)S(1)} custom-call(s32[1]{0:T(128)} %bitcast.pos, f32[24]{0:T(128)S(1)} %pad_maximum_fusion.4.coef, bf16[1,3,224,4096]{3,2,1,0:T(8,128)(2,1)} %m_ref.12, bf16[1,3,224,4096]{3,2,1,0:T(8,128)(2,1)} %v_ref.9, bf16[3,4,224,1024]{3,2,1,0:T(8,128)(2,1)S(1)} %bitcast.84, bf16[256,4096]{1,0:T(8,128)(2,1)S(1)} %copy-done.3, ...), custom_call_target="tpu_custom_call" | custom-call | flops 469762048 | bytes 3670016 | tf_op jit(solution)/shard_map/pallas_call | solution.py:233
  246.9 4.4 %shard_map.161 = bf16[1,2,224,1024]{3,2,1,0:T(8,128)(2,1)S(1)} custom-call(s32[1]{0:T(128)} %bitcast.pos, f32[24]{0:T(128)S(1)} %pad_maximum_fusion.4.coef, bf16[1,3,224,4096]{3,2,1,0:T(8,128)(2,1)} %m_ref.12, bf16[1,3,224,4096]{3,2,1,0:T(8,128)(2,1)} %v_ref.9, bf16[3,4,224,1024]{3,2,1,0:T(8,128)(2,1)S(1)} %bitcast.84, bf16[256,4096]{1,0:T(8,128)(2,1)S(1)} %copy-done.3, ...), custom_call_target="tpu_custom_call" | custom-call | flops 469762048 | bytes 3670016 | tf_op jit(solution)/shard_map/pallas_call | solution.py:233
  253.4 10.5 %shard_map.162.own_ref = bf16[3,2,224,1024]{3,2,1,0:T(8,128)(2,1)S(1)} custom-call(s32[1]{0:T(128)} %bitcast.pos, f32[24]{0:T(128)S(1)} %pad_maximum_fusion.4.coef, bf16[1,3,224,4096]{3,2,1,0:T(8,128)(2,1)} %m_ref.12, bf16[1,3,224,4096]{3,2,1,0:T(8,128)(2,1)} %v_ref.9, bf16[3,4,224,1024]{3,2,1,0:T(8,128)(2,1)S(1)} %bitcast.84, ...), custom_call_target="tpu_custom_call" | custom-call | flops 1409286144 | bytes 11010048 | tf_op jit(solution)/shard_map/pallas_call | solution.py:233
  264.5 3.2 %collective-permute-start.32 = (bf16[224,1024]{1,0:T(8,128)(2,1)S(1)}, bf16[224,1024]{1,0:T(8,128)(2,1)S(1)}, u32[]{:S(2)}, u32[]{:S(2)}) collective-permute-start(bf16[224,1024]{1,0:T(8,128)(2,1)S(1)} %fusion.2), channel_id=1, source_target_pairs={{0,64},{64,0},{1,65},{65,1},{2,66},{66,2},{3,67},{67,3},{4,68},{68... | collective-permute-start | bytes 1376264 | tf_op jit(solution)/shard_map/ppermute | solution.py:305
  270.7 7.8 %collective-permute-done.32.far_ref = bf16[224,1024]{1,0:T(8,128)(2,1)S(1)} collective-permute-done((bf16[224,1024]{1,0:T(8,128)(2,1)S(1)}, bf16[224,1024]{1,0:T(8,128)(2,1)S(1)}, u32[]{:S(2)}, u32[]{:S(2)}) %collective-permute-start.32) | collective-permute-done | bytes 458784 | tf_op jit(solution)/shard_map/ppermute | solution.py:305
  279.9 8.4 %collective-permute-done.31.far_ref = bf16[224,1024]{1,0:T(8,128)(2,1)S(1)} collective-permute-done((bf16[224,1024]{1,0:T(8,128)(2,1)S(1)}, bf16[224,1024]{1,0:T(8,128)(2,1)S(1)}, u32[]{:S(2)}, u32[]{:S(2)}) %collective-permute-start.31) | collective-permute-done | bytes 458784 | tf_op jit(solution)/shard_map/ppermute | solution.py:305
  289.6 8.5 %collective-permute-done.30.far_ref = bf16[224,1024]{1,0:T(8,128)(2,1)S(1)} collective-permute-done((bf16[224,1024]{1,0:T(8,128)(2,1)S(1)}, bf16[224,1024]{1,0:T(8,128)(2,1)S(1)}, u32[]{:S(2)}, u32[]{:S(2)}) %collective-permute-start.30) | collective-permute-done | bytes 458784 | tf_op jit(solution)/shard_map/ppermute | solution.py:305
  (158 shorter events, 77.2 us)
Async XLA Ops:
  0.6 9.1 %collective-permute-start.7 = (s32[1,1]{1,0:T(1,128)}, s32[1,1]{1,0:T(1,128)}, u32[]{:S(2)}, u32[]{:S(2)}) collective-permute-start(s32[1,1]{1,0:T(1,128)} %param.21), channel_id=1, source_target_pairs={{0,4},{4,0},{1,5},{5,1},{2,6},{6,2},{3,7},{7,3},{8,12},{12,8},{9,1... | collective-permute-start | bytes 20 | tf_op jit(solution)/shard_map/ppermute | solution.py:33
  5.3 42.2 %collective-permute-start.17 = (bf16[1,224,1024]{2,1,0:T(8,128)(2,1)S(1)}, bf16[1,224,1024]{2,1,0:T(8,128)(2,1)S(1)}, u32[]{:S(2)}, u32[]{:S(2)}) collective-permute-start(bf16[1,224,1024]{2,1,0:T(8,128)(2,1)S(1)} %slice.118.refs_9_), channel_id=1, source_target_pairs={{0,64},{64,0},{1,65},{65,1},{2,66},{66,2},{3,67},{67,3},{4,68},{68... | collective-permute-start | bytes 1376264 | tf_op jit(solution)/shard_map/ppermute | solution.py:305
  8.8 32.9 %collective-permute-start.16 = (bf16[2,224,1024]{2,1,0:T(8,128)(2,1)S(1)}, bf16[2,224,1024]{2,1,0:T(8,128)(2,1)S(1)}, u32[]{:S(2)}, u32[]{:S(2)}) collective-permute-start(bf16[2,224,1024]{2,1,0:T(8,128)(2,1)S(1)} %slice.117.refs_8_), channel_id=1, source_target_pairs={{0,64},{64,0},{1,65},{65,1},{2,66},{66,2},{3,67},{67,3},{4,68},{68... | collective-permute-start | bytes 2752520 | tf_op jit(solution)/shard_map/ppermute | solution.py:305
  11.6 9.5 %collective-permute-start.2 = (bf16[2,8,4096]{2,1,0:T(8,128)(2,1)S(1)}, bf16[2,8,4096]{2,1,0:T(8,128)(2,1)S(1)}, u32[]{:S(2)}, u32[]{:S(2)}) collective-permute-start(bf16[2,8,4096]{2,1,0:T(8,128)(2,1)S(1)} %pad_maximum_fusion.1), channel_id=1, source_target_pairs={{0,2},{1,3},{2,0},{3,1},{4,6},{5,7},{6,4},{7,5},{8,10},{9,11},{10,... | collective-permute-start | bytes 393224 | tf_op jit(solution)/shard_map/ppermute | solution.py:33
  19.9 8.4 %collective-permute-start.10 = (bf16[2,8,4224]{2,1,0:T(8,128)(2,1)S(1)}, bf16[2,8,4224]{2,1,0:T(8,128)(2,1)S(1)}, u32[]{:S(2)}, u32[]{:S(2)}) collective-permute-start(bf16[2,8,4224]{2,1,0:T(8,128)(2,1)S(1)} %get-tuple-element.57), channel_id=1, source_target_pairs={{0,8},{8,16},{16,24},{24,0},{1,9},{9,17},{17,25},{25,1},{2,10},{10... | collective-permute-start | bytes 405512 | tf_op jit(solution)/shard_map/ppermute | solution.py:33
  28.4 9.2 %collective-permute-start.13 = (bf16[64,2176]{1,0:T(8,128)(2,1)S(1)}, bf16[64,2176]{1,0:T(8,128)(2,1)S(1)}, u32[]{:S(2)}, u32[]{:S(2)}) collective-permute-start(bf16[64,2176]{1,0:T(8,128)(2,1)S(1)} %slice.116.refs_4_), channel_id=1, source_target_pairs={{0,1},{1,2},{2,3},{3,0},{4,5},{5,6},{6,7},{7,4},{8,9},{9,10},{10,1... | collective-permute-start | bytes 835592 | tf_op jit(solution)/shard_map/ppermute | solution.py:33
  31.4 13.1 %collective-permute-start.12 = (bf16[64,2176]{1,0:T(8,128)(2,1)S(1)}, bf16[64,2176]{1,0:T(8,128)(2,1)S(1)}, u32[]{:S(2)}, u32[]{:S(2)}) collective-permute-start(bf16[64,2176]{1,0:T(8,128)(2,1)S(1)} %slice.116.refs_4_), channel_id=1, source_target_pairs={{0,2},{1,3},{2,0},{3,1},{4,6},{5,7},{6,4},{7,5},{8,10},{9,11},{10,... | collective-permute-start | bytes 835592 | tf_op jit(solution)/shard_map/ppermute | solution.py:33
  34.7 13.7 %collective-permute-start.11 = (bf16[64,2176]{1,0:T(8,128)(2,1)S(1)}, bf16[64,2176]{1,0:T(8,128)(2,1)S(1)}, u32[]{:S(2)}, u32[]{:S(2)}) collective-permute-start(bf16[64,2176]{1,0:T(8,128)(2,1)S(1)} %slice.116.refs_4_), channel_id=1, source_target_pairs={{0,3},{1,0},{2,1},{3,2},{4,7},{5,4},{6,5},{7,6},{8,11},{9,8},{10,9... | collective-permute-start | bytes 835592 | tf_op jit(solution)/shard_map/ppermute | solution.py:33
  37.6 27.4 %collective-permute-start.14 = (bf16[2,224,1024]{2,1,0:T(8,128)(2,1)S(1)}, bf16[2,224,1024]{2,1,0:T(8,128)(2,1)S(1)}, u32[]{:S(2)}, u32[]{:S(2)}) collective-permute-start(bf16[2,224,1024]{2,1,0:T(8,128)(2,1)S(1)} %slice.117.refs_8_), channel_id=1, source_target_pairs={{0,32},{32,0},{1,33},{33,1},{2,34},{34,2},{3,35},{35,3},{4,36},{36... | collective-permute-start | bytes 2752520 | tf_op jit(solution)/shard_map/ppermute | solution.py:302
  41.7 23.3 %collective-permute-start.18 = (bf16[2,224,1024]{2,1,0:T(8,128)(2,1)S(1)}, bf16[2,224,1024]{2,1,0:T(8,128)(2,1)S(1)}, u32[]{:S(2)}, u32[]{:S(2)}) collective-permute-start(bf16[2,224,1024]{2,1,0:T(8,128)(2,1)S(1)} %collective-permute-done.16.refs_12_), channel_id=1, source_target_pairs={{0,32},{32,0},{1,33},{33,1},{2,34},{34,2},{3,35},{35,3},{4,36},{36... | collective-permute-start | bytes 2752520 | tf_op jit(solution)/shard_map/ppermute | solution.py:302
  47.5 9.1 %collective-permute-start.6 = (bf16[64,2048]{1,0:T(8,128)(2,1)S(1)}, bf16[64,2048]{1,0:T(8,128)(2,1)S(1)}, u32[]{:S(2)}, u32[]{:S(2)}) collective-permute-start(bf16[64,2048]{1,0:T(8,128)(2,1)S(1)} %get-tuple-element.59.refs_0_), channel_id=1, source_target_pairs={{0,8},{8,16},{16,24},{24,0},{1,9},{9,17},{17,25},{25,1},{2,10},{10... | collective-permute-start | bytes 786440 | tf_op jit(solution)/shard_map/ppermute | solution.py:33
  48.4 16.5 %collective-permute-start.19 = (bf16[1,224,1024]{2,1,0:T(8,128)(2,1)S(1)}, bf16[1,224,1024]{2,1,0:T(8,128)(2,1)S(1)}, u32[]{:S(2)}, u32[]{:S(2)}) collective-permute-start(bf16[1,224,1024]{2,1,0:T(8,128)(2,1)S(1)} %collective-permute-done.17.refs_13_), channel_id=1, source_target_pairs={{0,32},{32,0},{1,33},{33,1},{2,34},{34,2},{3,35},{35,3},{4,36},{36... | collective-permute-start | bytes 1376264 | tf_op jit(solution)/shard_map/ppermute | solution.py:302
  50.6 12.6 %collective-permute-start.5 = (bf16[64,2048]{1,0:T(8,128)(2,1)S(1)}, bf16[64,2048]{1,0:T(8,128)(2,1)S(1)}, u32[]{:S(2)}, u32[]{:S(2)}) collective-permute-start(bf16[64,2048]{1,0:T(8,128)(2,1)S(1)} %get-tuple-element.59.refs_0_), channel_id=1, source_target_pairs={{0,16},{8,24},{16,0},{24,8},{1,17},{9,25},{17,1},{25,9},{2,18},{10... | collective-permute-start | bytes 786440 | tf_op jit(solution)/shard_map/ppermute | solution.py:33
  105.4 38.9 %all-to-all-start.1 = ((bf16[32,8,4096]{2,1,0:T(8,128)(2,1)}), bf16[32,8,4096]{2,1,0:T(8,128)(2,1)S(1)}, u32[]{:S(2)}, u32[]{:S(2)}) async-start(bf16[32,8,4096]{2,1,0:T(8,128)(2,1)} %copy-done.6), calls=%async_computation.1 | async-start | bytes 4194304 | tf_op jit(solution)/shard_map/all_to_all | solution.py:345
  109.9 30.5 %collective-permute-start.22 = (bf16[64,2048]{1,0:T(8,128)(2,1)}, bf16[64,2048]{1,0:T(8,128)(2,1)S(1)}, u32[]{:S(2)}, u32[]{:S(2)}) collective-permute-start(bf16[64,2048]{1,0:T(8,128)(2,1)} %get-tuple-element.58.refs_0_), channel_id=1, source_target_pairs={{0,8},{8,16},{16,24},{24,0},{1,9},{9,17},{17,25},{25,1},{2,10},{10... | collective-permute-start | bytes 786440 | tf_op jit(solution)/shard_map/ppermute | solution.py:33
  111.2 53.4 %collective-permute-start.21 = (bf16[64,2048]{1,0:T(8,128)(2,1)}, bf16[64,2048]{1,0:T(8,128)(2,1)}, u32[]{:S(2)}, u32[]{:S(2)}) collective-permute-start(bf16[64,2048]{1,0:T(8,128)(2,1)} %get-tuple-element.58.refs_0_), channel_id=1, source_target_pairs={{0,16},{8,24},{16,0},{24,8},{1,17},{9,25},{17,1},{25,9},{2,18},{10... | collective-permute-start | bytes 786440 | tf_op jit(solution)/shard_map/ppermute | solution.py:33
  113.7 51.0 %collective-permute-start.20 = (bf16[64,2048]{1,0:T(8,128)(2,1)}, bf16[64,2048]{1,0:T(8,128)(2,1)}, u32[]{:S(2)}, u32[]{:S(2)}) collective-permute-start(bf16[64,2048]{1,0:T(8,128)(2,1)} %get-tuple-element.58.refs_0_), channel_id=1, source_target_pairs={{0,24},{8,0},{16,8},{24,16},{1,25},{9,1},{17,9},{25,17},{2,26},{10... | collective-permute-start | bytes 786440 | tf_op jit(solution)/shard_map/ppermute | solution.py:33
  116.5 48.2 %collective-permute-start.25 = (bf16[64,2048]{1,0:T(8,128)(2,1)}, bf16[64,2048]{1,0:T(8,128)(2,1)}, u32[]{:S(2)}, u32[]{:S(2)}) collective-permute-start(bf16[64,2048]{1,0:T(8,128)(2,1)} %slice.128.refs_4_), channel_id=1, source_target_pairs={{0,1},{1,2},{2,3},{3,0},{4,5},{5,6},{6,7},{7,4},{8,9},{9,10},{10,1... | collective-permute-start | bytes 786440 | tf_op jit(solution)/shard_map/ppermute | solution.py:33
  117.7 47.0 %collective-permute-start.24 = (bf16[64,2048]{1,0:T(8,128)(2,1)}, bf16[64,2048]{1,0:T(8,128)(2,1)}, u32[]{:S(2)}, u32[]{:S(2)}) collective-permute-start(bf16[64,2048]{1,0:T(8,128)(2,1)} %slice.128.refs_4_), channel_id=1, source_target_pairs={{0,2},{1,3},{2,0},{3,1},{4,6},{5,7},{6,4},{7,5},{8,10},{9,11},{10,... | collective-permute-start | bytes 786440 | tf_op jit(solution)/shard_map/ppermute | solution.py:33
  141.2 23.5 %collective-permute-start.23 = (bf16[64,2048]{1,0:T(8,128)(2,1)}, bf16[64,2048]{1,0:T(8,128)(2,1)}, u32[]{:S(2)}, u32[]{:S(2)}) collective-permute-start(bf16[64,2048]{1,0:T(8,128)(2,1)} %slice.128.refs_4_), channel_id=1, source_target_pairs={{0,3},{1,0},{2,1},{3,2},{4,7},{5,4},{6,5},{7,6},{8,11},{9,8},{10,9... | collective-permute-start | bytes 786440 | tf_op jit(solution)/shard_map/ppermute | solution.py:33
  264.0 14.5 %collective-permute-start.29 = (bf16[3,224,1024]{2,1,0:T(8,128)(2,1)S(1)}, bf16[3,224,1024]{2,1,0:T(8,128)(2,1)S(1)}, u32[]{:S(2)}, u32[]{:S(2)}) collective-permute-start(bf16[3,224,1024]{2,1,0:T(8,128)(2,1)S(1)} %slice_bitcast_fusion), channel_id=1, source_target_pairs={{0,32},{32,0},{1,33},{33,1},{2,34},{34,2},{3,35},{35,3},{4,36},{36... | collective-permute-start | bytes 4128776 | tf_op jit(solution)/shard_map/ppermute | solution.py:302
  264.5 14.0 %collective-permute-start.32 = (bf16[224,1024]{1,0:T(8,128)(2,1)S(1)}, bf16[224,1024]{1,0:T(8,128)(2,1)S(1)}, u32[]{:S(2)}, u32[]{:S(2)}) collective-permute-start(bf16[224,1024]{1,0:T(8,128)(2,1)S(1)} %fusion.2), channel_id=1, source_target_pairs={{0,64},{64,0},{1,65},{65,1},{2,66},{66,2},{3,67},{67,3},{4,68},{68... | collective-permute-start | bytes 1376264 | tf_op jit(solution)/shard_map/ppermute | solution.py:305
  267.7 20.6 %collective-permute-start.31 = (bf16[224,1024]{1,0:T(8,128)(2,1)S(1)}, bf16[224,1024]{1,0:T(8,128)(2,1)S(1)}, u32[]{:S(2)}, u32[]{:S(2)}) collective-permute-start(bf16[224,1024]{1,0:T(8,128)(2,1)S(1)} %fusion.1), channel_id=1, source_target_pairs={{0,64},{64,0},{1,65},{65,1},{2,66},{66,2},{3,67},{67,3},{4,68},{68... | collective-permute-start | bytes 1376264 | tf_op jit(solution)/shard_map/ppermute | solution.py:305
  267.7 30.4 %collective-permute-start.30 = (bf16[224,1024]{1,0:T(8,128)(2,1)S(1)}, bf16[224,1024]{1,0:T(8,128)(2,1)S(1)}, u32[]{:S(2)}, u32[]{:S(2)}) collective-permute-start(bf16[224,1024]{1,0:T(8,128)(2,1)S(1)} %fusion), channel_id=1, source_target_pairs={{0,64},{64,0},{1,65},{65,1},{2,66},{66,2},{3,67},{67,3},{4,68},{68... | collective-permute-start | bytes 1376264 | tf_op jit(solution)/shard_map/ppermute | solution.py:305
  (34 other events, 447.3 us)

commit v4 on v3

--- a/solution.py
+++ b/solution.py
@@ -268,7 +268,7 @@
         in_specs=[
             block,
             block,
-            pl.BlockSpec((1, 1, half, quarter), lambda i: (p, 1, i, 0)),
+            pl.BlockSpec((1, 1, half, quarter), lambda i: (p, 0, i, 0)),
             block,
             pl.BlockSpec((half, quarter), lambda i: (i, 0)),
         ]
@@ -312,9 +312,9 @@
     far = []
     for chunk in own:
         far.append(across(chunk))
-    near = [partner(chunk) for chunk in own]
-    both = [partner(chunk) for chunk in far]
-    w = own + near + far + both
+    near = []
+    for chunk in own:
+        near.append(partner(chunk))
 
     marks = jnp.broadcast_to(told.reshape(1, 1, 128), (2, tok, 128))
     low = jnp.concatenate([pair[:, k, :, :half] for k in range(steps)], axis=2)
@@ -324,6 +324,7 @@
     for k in range(steps):
         start, stop = (k * half + (128 if k else 0), (k + 1) * half + 128)
         pieces.append(around(flat[0][:, k * half : (k + 1) * half], "x") + around(flat[1][:, start:stop], "y"))
+    inputs, targets, far[1] = lax.optimization_barrier((inputs, targets, far[1]))
     inputs, targets = own_order(inputs), own_order(targets)
     marked = functools.reduce(jnp.maximum, [jnp.max(p[:, half : half + steps], axis=0) for p in pieces[0][4:]])
     coef = coefficients([marked[s] > 0 for s in range(steps)])
@@ -332,6 +333,8 @@
     second_moment = pltpu.with_memory_space_constraint(second_moment, pltpu.HBM)
     at = jnp.stack([lax.axis_index("x"), lax.axis_index("y"), mine]).astype(jnp.int32)
 
+    both = [partner(chunk) for chunk in far]
+    w = own + near + far + both
     xs, ys = [inputs[k] for k in range(steps)], [targets[k] for k in range(steps)]
     parts = []
     w_start = None
@@ -347,13 +350,21 @@
         if k == 0:
             w = adam(pos, coef, first_moment, second_moment, w, parts, (range(3), range(4)))
     arrived = []
+    state = (first_moment, second_moment, w_start, parts)
     for p in (2, 0, 1):
-        pair = adam(pos, coef, first_moment, second_moment, w_start, parts, ((p,), (3, 2)))
-        joint = (pair[0, 1].astype(f32) + partner(pair[0, 0]).astype(f32)).astype(bf16)
+        if p == 2:
+            out = adam(pos, coef, *state, ((p,), (3,)))[0, 0]
+            handed = partner(out)
+            kept = adam(pos, coef, *state, ((p,), (2,)))[0, 0]
+        else:
+            pair = adam(pos, coef, *state, ((p,), (3, 2)))
+            handed, kept = partner(pair[0, 0]), pair[0, 1]
+        joint = (kept.astype(f32) + handed.astype(f32)).astype(bf16)
         joint, pos = lax.optimization_barrier((joint, pos))
         arrived.append((p, across(joint)))
-    rest = adam(pos, coef, first_moment, second_moment, w_start, parts, (range(3), (1, 0)))
-    near_part = partner(rest[:, 0])
+    beside = adam(pos, coef, *state, (range(3), (1,)))
+    near_part = partner(beside[:, 0])
+    rest = adam(pos, coef, *state, (range(3), (0,)))
     result = ()
     for p, far_part in arrived:
         result = settle(p, weights, momentum, rest, near_part, far_part, result)

time: 300 us -> 313 us (1.043)
  waiting for transfers between devices: 72.1 us -> 81.4 us
    ppermute x20, waiting for transfers between devices: 43.1 us -> 57.3 us  [around(): lax.ppermute(own, dim, [(i, (i - s) % n) for i in range(n)])]
    ppermute x5, waiting for transfers between devices: 24.7 us -> 20.6 us  [across(): return lax.ppermute(array, 'zh', [(0, 1), (1, 0)])]
    pallas_call x5 -> x7, Pallas kernels: 35.8 us -> 38.5 us  [adam(): pl.pallas_call(functools.partial(adam_kernel, steps, ps, r_of, min(512, q...]
    unnamed x57 -> x61, local copies, waits for them, and re-layouts: 12 us -> 12.7 us
  transfers between devices with their start and end apart: 34 -> 34, of which waited for: 14 -> 16; matrix products, arithmetic and copies ran while one was open for 3% -> 2% of each run, Pallas kernels for 5% -> 8%
where the time goes in v4:
time: 313 us
  blocking collectives  95.4 us (30%)
  waiting for transfers between devices  81.4 us (26%)
  starting transfers between devices  60.2 us (19%)
  Pallas kernels  51.8 us (17%)
  local copies, waits for them, and re-layouts  16 us (5%)
  other arithmetic  4.58 us (1%)
  between operations  3.19 us (1%)
    all_to_all x2, blocking collectives, round_of(): lax.all_to_all(sums.reshape(-1, tok, width), FSDP, 0, 0, tiled=True)  64.1 us
    ppermute x20, waiting for transfers between devices, around(): lax.ppermute(own, dim, [(i, (i - s) % n) for i in range(n)])  57.3 us
    pallas_call x7, Pallas kernels, adam(): pl.pallas_call(functools.partial(adam_kernel, steps, ps, r_of, min(512, q...  38.5 us
    ppermute x20, starting transfers between devices, around(): lax.ppermute(own, dim, [(i, (i - s) % n) for i in range(n)])  32.7 us
    all_to_all x1, blocking collectives, round_of(): z = lax.all_to_all(copies, FSDP, 0, 0, tiled=True).reshape(-1, width)  31.2 us
    ppermute x5, waiting for transfers between devices, across(): return lax.ppermute(array, 'zh', [(0, 1), (1, 0)])  20.6 us
    ppermute x8, starting transfers between devices, partner(): return lax.ppermute(array, 'co', [(0, 1), (1, 0)])  14.8 us
    unnamed x61, local copies, waits for them, and re-layouts  12.7 us
  transfers between devices with their start and end apart: 34, of which 16 were waited for; matrix products, arithmetic and copies ran while one was open for 2% of the time, Pallas kernels for 8%

profile of v4, /device:TPU:1, one launch (start us, length us, event | category | flops | bytes accessed | tf_op | source)
XLA Modules:
  0.0 312.5 jit_solution(8993885520476397260)
XLA Ops:
  2.7 4.5 %collective-permute-start.17 = (bf16[1,224,1024]{2,1,0:T(8,128)(2,1)S(1)}, bf16[1,224,1024]{2,1,0:T(8,128)(2,1)S(1)}, u32[]{:S(2)}, u32[]{:S(2)}) collective-permute-start(bf16[1,224,1024]{2,1,0:T(8,128)(2,1)S(1)} %slice.106.refs_9_), channel_id=1, source_target_pairs={{0,64},{64,0},{1,65},{65,1},{2,66},{66,2},{3,67},{67,3},{4,68},{68... | collective-permute-start | bytes 1376264 | tf_op jit(solution)/shard_map/ppermute | solution.py:305
  10.7 7.2 %collective-permute-done.7 = s32[1,1]{1,0:T(1,128)} collective-permute-done((s32[1,1]{1,0:T(1,128)}, s32[1,1]{1,0:T(1,128)}, u32[]{:S(2)}, u32[]{:S(2)}) %collective-permute-start.7) | collective-permute-done | bytes 36 | tf_op jit(solution)/shard_map/ppermute | solution.py:33
  26.4 3.6 %collective-permute-done.1 = bf16[2,8,4096]{2,1,0:T(8,128)(2,1)S(1)} collective-permute-done((bf16[2,8,4096]{2,1,0:T(8,128)(2,1)S(1)}, bf16[2,8,4096]{2,1,0:T(8,128)(2,1)S(1)}, u32[]{:S(2)}, u32[]{:S(2)}) %collective-permute-start.1) | collective-permute-done | bytes 131104 | tf_op jit(solution)/shard_map/ppermute | solution.py:33
  48.4 6.7 %collective-permute-done.13.refs_7_ = bf16[64,2176]{1,0:T(8,128)(2,1)S(1)} collective-permute-done((bf16[64,2176]{1,0:T(8,128)(2,1)S(1)}, bf16[64,2176]{1,0:T(8,128)(2,1)S(1)}, u32[]{:S(2)}, u32[]{:S(2)}) %collective-permute-start.13) | collective-permute-done | bytes 278560 | tf_op jit(solution)/shard_map/ppermute | solution.py:33
  55.1 9.0 %collective-permute-start.14 = (bf16[2,224,1024]{2,1,0:T(8,128)(2,1)S(1)}, bf16[2,224,1024]{2,1,0:T(8,128)(2,1)S(1)}, u32[]{:S(2)}, u32[]{:S(2)}) collective-permute-start(bf16[2,224,1024]{2,1,0:T(8,128)(2,1)S(1)} %slice.105.refs_8_), channel_id=1, source_target_pairs={{0,32},{32,0},{1,33},{33,1},{2,34},{34,2},{3,35},{35,3},{4,36},{36... | collective-permute-start | bytes 2752520 | tf_op jit(solution)/shard_map/ppermute | solution.py:302
  67.7 3.9 %collective-permute-start.5 = (bf16[64,2048]{1,0:T(8,128)(2,1)S(1)}, bf16[64,2048]{1,0:T(8,128)(2,1)S(1)}, u32[]{:S(2)}, u32[]{:S(2)}) collective-permute-start(bf16[64,2048]{1,0:T(8,128)(2,1)S(1)} %get-tuple-element.65.refs_0_), channel_id=1, source_target_pairs={{0,16},{8,24},{16,0},{24,8},{1,17},{9,25},{17,1},{25,9},{2,18},{10... | collective-permute-start | bytes 786440 | tf_op jit(solution)/shard_map/ppermute | solution.py:33
  75.0 5.2 %collective-permute-done.5.refs_2_ = bf16[64,2048]{1,0:T(8,128)(2,1)S(1)} collective-permute-done((bf16[64,2048]{1,0:T(8,128)(2,1)S(1)}, bf16[64,2048]{1,0:T(8,128)(2,1)S(1)}, u32[]{:S(2)}, u32[]{:S(2)}) %collective-permute-start.5) | collective-permute-done | bytes 262176 | tf_op jit(solution)/shard_map/ppermute | solution.py:33
  82.9 3.2 %forward0.1 = (bf16[256,4096]{1,0:T(8,128)(2,1)S(1)}, f32[224,256]{1,0:T(8,128)S(1)}, f32[224,256]{1,0:T(8,128)S(1)}, bf16[224,256]{1,0:T(8,128)(2,1)S(1)}, bf16...) custom-call(s32[3]{0:T(128)S(1)} %pad_add_fusion.at_ref, ...), custom_call_target="tpu_custom_call" | custom-call | flops 1409286144 | bytes 8388608 | tf_op jit(solution)/shard_map/forward0/pallas_call | solution.py:113
  88.6 34.1 %all_to_all.20.parts_ref = bf16[32,8,4096]{2,1,0:T(8,128)(2,1)S(1)} all-to-all(bf16[32,8,4096]{2,1,0:T(8,128)(2,1)S(1)} %bitcast.94), channel_id=1, replica_groups=mesh['zh'=2,'co'=2,'x'=4,'zl'=2,'y'=4] {'x','y','zl'}, dimensions={0} | all-to-all | bytes 4194304 | tf_op jit(solution)/shard_map/all_to_all | solution.py:346
  124.5 4.5 %all-to-all-start.1 = ((bf16[32,8,4096]{2,1,0:T(8,128)(2,1)}), bf16[32,8,4096]{2,1,0:T(8,128)(2,1)S(1)}, u32[]{:S(2)}, u32[]{:S(2)}) async-start(bf16[32,8,4096]{2,1,0:T(8,128)(2,1)} %copy-done.6), calls=%async_computation.1 | async-start | bytes 4194304 | tf_op jit(solution)/shard_map/all_to_all | solution.py:348
  139.1 20.4 %collective-permute-done.22.refs_3_ = bf16[64,2048]{1,0:T(8,128)(2,1)S(1)} collective-permute-done((bf16[64,2048]{1,0:T(8,128)(2,1)}, bf16[64,2048]{1,0:T(8,128)(2,1)S(1)}, u32[]{:S(2)}, u32[]{:S(2)}) %collective-permute-start.22) | collective-permute-done | bytes 262176 | tf_op jit(solution)/shard_map/ppermute | solution.py:33
  160.2 3.2 %collective-permute-start.23 = (bf16[64,2048]{1,0:T(8,128)(2,1)}, bf16[64,2048]{1,0:T(8,128)(2,1)}, u32[]{:S(2)}, u32[]{:S(2)}) collective-permute-start(bf16[64,2048]{1,0:T(8,128)(2,1)} %slice.116.refs_4_), channel_id=1, source_target_pairs={{0,3},{1,0},{2,1},{3,2},{4,7},{5,4},{6,5},{7,6},{8,11},{9,8},{10,9... | collective-permute-start | bytes 786440 | tf_op jit(solution)/shard_map/ppermute | solution.py:33
  171.6 12.1 %shard_map.158.refs_8_.w_ref = bf16[3,4,224,1024]{3,2,1,0:T(8,128)(2,1)S(1)} custom-call(s32[1]{0:T(128)} %bitcast.pos, f32[24]{0:T(128)S(1)} %pad_maximum_fusion.4.coef, bf16[1,3,224,4096]{3,2,1,0:T(8,128)(2,1)} %m_ref.16, bf16[1,3,224,4096]{3,2,1,0:T(8,128)(2,1)} %v_ref.13, bf16[3,4,224,1024]{3,2,1,0:T(8,128)(2,1)S(1)} %bitcast.78, ...), custom_call_target="tpu_custom_call" | custom-call | flops 1409286144 | bytes 22020096 | tf_op jit(solution)/shard_map/pallas_call | solution.py:233
  183.7 3.6 %forward1.1 = (bf16[256,4096]{1,0:T(8,128)(2,1)S(1)}, f32[224,256]{1,0:T(8,128)S(1)}, f32[224,256]{1,0:T(8,128)S(1)}, bf16[224,256]{1,0:T(8,128)(2,1)S(1)}, bf16[256,4096]{1,0:T(8,128)(2,1)S(1)}) custom-call(s32[3]{0:T(128)S(1)} %pad_add_fusion.at_ref, bf16[64,2048]{1,0:T(8,128)(2,1)S(1)} %copy-done.7, bf16[64,2048]{1,0:T(8,128)(2,1)} %collective-permute-done.20.refs_1_, ...), custom_call_target="tpu_custom_call" | custom-call | flops 1409286144 | bytes 8388608 | tf_op jit(solution)/shard_map/forward1/pallas_call | solution.py:113
  187.4 30.0 %all_to_all.21.parts_ref = bf16[32,8,4096]{2,1,0:T(8,128)(2,1)S(1)} all-to-all(bf16[32,8,4096]{2,1,0:T(8,128)(2,1)S(1)} %bitcast.95), channel_id=1, replica_groups=mesh['zh'=2,'co'=2,'x'=4,'zl'=2,'y'=4] {'x','y','zl'}, dimensions={0} | all-to-all | bytes 4194304 | tf_op jit(solution)/shard_map/all_to_all | solution.py:346
  217.8 31.2 %all_to_all.22 = bf16[32,8,4096]{2,1,0:T(8,128)(2,1)S(1)} all-to-all(bf16[32,8,4096]{2,1,0:T(8,128)(2,1)S(1)} %own_slopes.3), channel_id=1, replica_groups=mesh['zh'=2,'co'=2,'x'=4,'zl'=2,'y'=4] {'x','y','zl'}, dimensions={0} | all-to-all | bytes 4194304 | tf_op jit(solution)/shard_map/all_to_all | solution.py:348
  252.5 3.5 %collective-permute-start.26 = (bf16[224,1024]{1,0:T(8,128)(2,1)S(1)}, bf16[224,1024]{1,0:T(8,128)(2,1)S(1)}, u32[]{:S(2)}, u32[]{:S(2)}) collective-permute-start(bf16[224,1024]{1,0:T(8,128)(2,1)S(1)} %bitcast.97), channel_id=1, source_target_pairs={{0,32},{32,0},{1,33},{33,1},{2,34},{34,2},{3,35},{35,3},{4,36},{36... | collective-permute-start | bytes 1376264 | tf_op jit(solution)/shard_map/ppermute | solution.py:302
  258.9 4.4 %shard_map.161 = bf16[1,2,224,1024]{3,2,1,0:T(8,128)(2,1)S(1)} custom-call(s32[1]{0:T(128)} %bitcast.pos, f32[24]{0:T(128)S(1)} %pad_maximum_fusion.4.coef, bf16[1,3,224,4096]{3,2,1,0:T(8,128)(2,1)} %m_ref.16, bf16[1,3,224,4096]{3,2,1,0:T(8,128)(2,1)} %v_ref.13, bf16[3,4,224,1024]{3,2,1,0:T(8,128)(2,1)S(1)} %bitcast.78, bf16[256,4096]{1,0:T(8,128)(2,1)S(1)} %copy-done.3, ...), custom_call_target="tpu_custom_call" | custom-call | flops 469762048 | bytes 3670016 | tf_op jit(solution)/shard_map/pallas_call | solution.py:233
  265.5 4.4 %shard_map.162 = bf16[1,2,224,1024]{3,2,1,0:T(8,128)(2,1)S(1)} custom-call(s32[1]{0:T(128)} %bitcast.pos, f32[24]{0:T(128)S(1)} %pad_maximum_fusion.4.coef, bf16[1,3,224,4096]{3,2,1,0:T(8,128)(2,1)} %m_ref.16, bf16[1,3,224,4096]{3,2,1,0:T(8,128)(2,1)} %v_ref.13, bf16[3,4,224,1024]{3,2,1,0:T(8,128)(2,1)S(1)} %bitcast.78, bf16[256,4096]{1,0:T(8,128)(2,1)S(1)} %copy-done.3, ...), custom_call_target="tpu_custom_call" | custom-call | flops 469762048 | bytes 3670016 | tf_op jit(solution)/shard_map/pallas_call | solution.py:233
  272.0 6.1 %shard_map.164 = bf16[3,1,224,1024]{3,2,1,0:T(8,128)(2,1)S(1)} custom-call(s32[1]{0:T(128)} %bitcast.pos, f32[24]{0:T(128)S(1)} %pad_maximum_fusion.4.coef, bf16[1,3,224,4096]{3,2,1,0:T(8,128)(2,1)} %m_ref.16, bf16[1,3,224,4096]{3,2,1,0:T(8,128)(2,1)} %v_ref.13, bf16[3,4,224,1024]{3,2,1,0:T(8,128)(2,1)S(1)} %bitcast.78, bf16[256,4096]{1,0:T(8,128)(2,1)S(1)} %copy-done.3, ...), custom_call_target="tpu_custom_call" | custom-call | flops 704643072 | bytes 5505024 | tf_op jit(solution)/shard_map/pallas_call | solution.py:233
  281.8 6.1 %shard_map.163.own_ref = bf16[3,1,224,1024]{3,2,1,0:T(8,128)(2,1)S(1)} custom-call(s32[1]{0:T(128)} %bitcast.pos, f32[24]{0:T(128)S(1)} %pad_maximum_fusion.4.coef, bf16[1,3,224,4096]{3,2,1,0:T(8,128)(2,1)} %m_ref.16, bf16[1,3,224,4096]{3,2,1,0:T(8,128)(2,1)} %v_ref.13, bf16[3,4,224,1024]{3,2,1,0:T(8,128)(2,1)S(1)} %bitcast.78, ...), custom_call_target="tpu_custom_call" | custom-call | flops 704643072 | bytes 5505024 | tf_op jit(solution)/shard_map/pallas_call | solution.py:233
  287.8 3.7 %collective-permute-done.32.far_ref = bf16[224,1024]{1,0:T(8,128)(2,1)S(1)} collective-permute-done((bf16[224,1024]{1,0:T(8,128)(2,1)S(1)}, bf16[224,1024]{1,0:T(8,128)(2,1)S(1)}, u32[]{:S(2)}, u32[]{:S(2)}) %collective-permute-start.32) | collective-permute-done | bytes 458784 | tf_op jit(solution)/shard_map/ppermute | solution.py:305
  292.9 8.4 %collective-permute-done.31.far_ref = bf16[224,1024]{1,0:T(8,128)(2,1)S(1)} collective-permute-done((bf16[224,1024]{1,0:T(8,128)(2,1)S(1)}, bf16[224,1024]{1,0:T(8,128)(2,1)S(1)}, u32[]{:S(2)}, u32[]{:S(2)}) %collective-permute-start.31) | collective-permute-done | bytes 458784 | tf_op jit(solution)/shard_map/ppermute | solution.py:305
  302.7 8.5 %collective-permute-done.30.far_ref = bf16[224,1024]{1,0:T(8,128)(2,1)S(1)} collective-permute-done((bf16[224,1024]{1,0:T(8,128)(2,1)S(1)}, bf16[224,1024]{1,0:T(8,128)(2,1)S(1)}, u32[]{:S(2)}, u32[]{:S(2)}) %collective-permute-start.30) | collective-permute-done | bytes 458784 | tf_op jit(solution)/shard_map/ppermute | solution.py:305
  (162 shorter events, 81.8 us)
Async XLA Ops:
  2.7 45.2 %collective-permute-start.17 = (bf16[1,224,1024]{2,1,0:T(8,128)(2,1)S(1)}, bf16[1,224,1024]{2,1,0:T(8,128)(2,1)S(1)}, u32[]{:S(2)}, u32[]{:S(2)}) collective-permute-start(bf16[1,224,1024]{2,1,0:T(8,128)(2,1)S(1)} %slice.106.refs_9_), channel_id=1, source_target_pairs={{0,64},{64,0},{1,65},{65,1},{2,66},{66,2},{3,67},{67,3},{4,68},{68... | collective-permute-start | bytes 1376264 | tf_op jit(solution)/shard_map/ppermute | solution.py:305
  7.2 60.5 %collective-permute-start.15 = (bf16[1,224,1024]{2,1,0:T(8,128)(2,1)S(1)}, bf16[1,224,1024]{2,1,0:T(8,128)(2,1)S(1)}, u32[]{:S(2)}, u32[]{:S(2)}) collective-permute-start(bf16[1,224,1024]{2,1,0:T(8,128)(2,1)S(1)} %slice.106.refs_9_), channel_id=1, source_target_pairs={{0,32},{32,0},{1,33},{33,1},{2,34},{34,2},{3,35},{35,3},{4,36},{36... | collective-permute-start | bytes 1376264 | tf_op jit(solution)/shard_map/ppermute | solution.py:302
  8.2 9.7 %collective-permute-start.7 = (s32[1,1]{1,0:T(1,128)}, s32[1,1]{1,0:T(1,128)}, u32[]{:S(2)}, u32[]{:S(2)}) collective-permute-start(s32[1,1]{1,0:T(1,128)} %param.21), channel_id=1, source_target_pairs={{0,4},{4,0},{1,5},{5,1},{2,6},{6,2},{3,7},{7,3},{8,12},{12,8},{9,1... | collective-permute-start | bytes 20 | tf_op jit(solution)/shard_map/ppermute | solution.py:33
  8.9 11.8 %collective-permute-start = (bf16[2,8,4096]{2,1,0:T(8,128)(2,1)S(1)}, bf16[2,8,4096]{2,1,0:T(8,128)(2,1)S(1)}, u32[]{:S(2)}, u32[]{:S(2)}) collective-permute-start(bf16[2,8,4096]{2,1,0:T(8,128)(2,1)S(1)} %copy-done.17), channel_id=1, source_target_pairs={{0,4},{4,0},{1,5},{5,1},{2,6},{6,2},{3,7},{7,3},{8,12},{12,8},{9,1... | collective-permute-start | bytes 393224 | tf_op jit(solution)/shard_map/ppermute | solution.py:33
  9.7 54.4 %collective-permute-start.16 = (bf16[2,224,1024]{2,1,0:T(8,128)(2,1)S(1)}, bf16[2,224,1024]{2,1,0:T(8,128)(2,1)S(1)}, u32[]{:S(2)}, u32[]{:S(2)}) collective-permute-start(bf16[2,224,1024]{2,1,0:T(8,128)(2,1)S(1)} %slice.105.refs_8_), channel_id=1, source_target_pairs={{0,64},{64,0},{1,65},{65,1},{2,66},{66,2},{3,67},{67,3},{4,68},{68... | collective-permute-start | bytes 2752520 | tf_op jit(solution)/shard_map/ppermute | solution.py:305
  31.0 14.2 %collective-permute-start.10 = (bf16[2,8,4224]{2,1,0:T(8,128)(2,1)S(1)}, bf16[2,8,4224]{2,1,0:T(8,128)(2,1)S(1)}, u32[]{:S(2)}, u32[]{:S(2)}) collective-permute-start(bf16[2,8,4224]{2,1,0:T(8,128)(2,1)S(1)} %get-tuple-element.63), channel_id=1, source_target_pairs={{0,8},{8,16},{16,24},{24,0},{1,9},{9,17},{17,25},{25,1},{2,10},{10... | collective-permute-start | bytes 405512 | tf_op jit(solution)/shard_map/ppermute | solution.py:33
  45.4 9.7 %collective-permute-start.13 = (bf16[64,2176]{1,0:T(8,128)(2,1)S(1)}, bf16[64,2176]{1,0:T(8,128)(2,1)S(1)}, u32[]{:S(2)}, u32[]{:S(2)}) collective-permute-start(bf16[64,2176]{1,0:T(8,128)(2,1)S(1)} %slice.104.refs_4_), channel_id=1, source_target_pairs={{0,1},{1,2},{2,3},{3,0},{4,5},{5,6},{6,7},{7,4},{8,9},{9,10},{10,1... | collective-permute-start | bytes 835592 | tf_op jit(solution)/shard_map/ppermute | solution.py:33
  45.5 18.6 %collective-permute-start.12 = (bf16[64,2176]{1,0:T(8,128)(2,1)S(1)}, bf16[64,2176]{1,0:T(8,128)(2,1)S(1)}, u32[]{:S(2)}, u32[]{:S(2)}) collective-permute-start(bf16[64,2176]{1,0:T(8,128)(2,1)S(1)} %slice.104.refs_4_), channel_id=1, source_target_pairs={{0,2},{1,3},{2,0},{3,1},{4,6},{5,7},{6,4},{7,5},{8,10},{9,11},{10,... | collective-permute-start | bytes 835592 | tf_op jit(solution)/shard_map/ppermute | solution.py:33
  47.9 17.0 %collective-permute-start.11 = (bf16[64,2176]{1,0:T(8,128)(2,1)S(1)}, bf16[64,2176]{1,0:T(8,128)(2,1)S(1)}, u32[]{:S(2)}, u32[]{:S(2)}) collective-permute-start(bf16[64,2176]{1,0:T(8,128)(2,1)S(1)} %slice.104.refs_4_), channel_id=1, source_target_pairs={{0,3},{1,0},{2,1},{3,2},{4,7},{5,4},{6,5},{7,6},{8,11},{9,8},{10,9... | collective-permute-start | bytes 835592 | tf_op jit(solution)/shard_map/ppermute | solution.py:33
  55.1 27.9 %collective-permute-start.14 = (bf16[2,224,1024]{2,1,0:T(8,128)(2,1)S(1)}, bf16[2,224,1024]{2,1,0:T(8,128)(2,1)S(1)}, u32[]{:S(2)}, u32[]{:S(2)}) collective-permute-start(bf16[2,224,1024]{2,1,0:T(8,128)(2,1)S(1)} %slice.105.refs_8_), channel_id=1, source_target_pairs={{0,32},{32,0},{1,33},{33,1},{2,34},{34,2},{3,35},{35,3},{4,36},{36... | collective-permute-start | bytes 2752520 | tf_op jit(solution)/shard_map/ppermute | solution.py:302
  64.0 18.9 %collective-permute-start.18 = (bf16[2,224,1024]{2,1,0:T(8,128)(2,1)S(1)}, bf16[2,224,1024]{2,1,0:T(8,128)(2,1)S(1)}, u32[]{:S(2)}, u32[]{:S(2)}) collective-permute-start(bf16[2,224,1024]{2,1,0:T(8,128)(2,1)S(1)} %collective-permute-done.16.refs_12_), channel_id=1, source_target_pairs={{0,32},{32,0},{1,33},{33,1},{2,34},{34,2},{3,35},{35,3},{4,36},{36... | collective-permute-start | bytes 2752520 | tf_op jit(solution)/shard_map/ppermute | solution.py:302
  64.9 18.1 %collective-permute-start.19 = (bf16[1,224,1024]{2,1,0:T(8,128)(2,1)S(1)}, bf16[1,224,1024]{2,1,0:T(8,128)(2,1)S(1)}, u32[]{:S(2)}, u32[]{:S(2)}) collective-permute-start(bf16[1,224,1024]{2,1,0:T(8,128)(2,1)S(1)} %collective-permute-done.17.refs_13_), channel_id=1, source_target_pairs={{0,32},{32,0},{1,33},{33,1},{2,34},{34,2},{3,35},{35,3},{4,36},{36... | collective-permute-start | bytes 1376264 | tf_op jit(solution)/shard_map/ppermute | solution.py:302
  67.7 12.5 %collective-permute-start.5 = (bf16[64,2048]{1,0:T(8,128)(2,1)S(1)}, bf16[64,2048]{1,0:T(8,128)(2,1)S(1)}, u32[]{:S(2)}, u32[]{:S(2)}) collective-permute-start(bf16[64,2048]{1,0:T(8,128)(2,1)S(1)} %get-tuple-element.65.refs_0_), channel_id=1, source_target_pairs={{0,16},{8,24},{16,0},{24,8},{1,17},{9,25},{17,1},{25,9},{2,18},{10... | collective-permute-start | bytes 786440 | tf_op jit(solution)/shard_map/ppermute | solution.py:33
  124.5 38.9 %all-to-all-start.1 = ((bf16[32,8,4096]{2,1,0:T(8,128)(2,1)}), bf16[32,8,4096]{2,1,0:T(8,128)(2,1)S(1)}, u32[]{:S(2)}, u32[]{:S(2)}) async-start(bf16[32,8,4096]{2,1,0:T(8,128)(2,1)} %copy-done.6), calls=%async_computation.1 | async-start | bytes 4194304 | tf_op jit(solution)/shard_map/all_to_all | solution.py:348
  128.9 30.5 %collective-permute-start.22 = (bf16[64,2048]{1,0:T(8,128)(2,1)}, bf16[64,2048]{1,0:T(8,128)(2,1)S(1)}, u32[]{:S(2)}, u32[]{:S(2)}) collective-permute-start(bf16[64,2048]{1,0:T(8,128)(2,1)} %get-tuple-element.64.refs_0_), channel_id=1, source_target_pairs={{0,8},{8,16},{16,24},{24,0},{1,9},{9,17},{17,25},{25,1},{2,10},{10... | collective-permute-start | bytes 786440 | tf_op jit(solution)/shard_map/ppermute | solution.py:33
  130.2 53.4 %collective-permute-start.21 = (bf16[64,2048]{1,0:T(8,128)(2,1)}, bf16[64,2048]{1,0:T(8,128)(2,1)}, u32[]{:S(2)}, u32[]{:S(2)}) collective-permute-start(bf16[64,2048]{1,0:T(8,128)(2,1)} %get-tuple-element.64.refs_0_), channel_id=1, source_target_pairs={{0,16},{8,24},{16,0},{24,8},{1,17},{9,25},{17,1},{25,9},{2,18},{10... | collective-permute-start | bytes 786440 | tf_op jit(solution)/shard_map/ppermute | solution.py:33
  132.7 51.0 %collective-permute-start.20 = (bf16[64,2048]{1,0:T(8,128)(2,1)}, bf16[64,2048]{1,0:T(8,128)(2,1)}, u32[]{:S(2)}, u32[]{:S(2)}) collective-permute-start(bf16[64,2048]{1,0:T(8,128)(2,1)} %get-tuple-element.64.refs_0_), channel_id=1, source_target_pairs={{0,24},{8,0},{16,8},{24,16},{1,25},{9,1},{17,9},{25,17},{2,26},{10... | collective-permute-start | bytes 786440 | tf_op jit(solution)/shard_map/ppermute | solution.py:33
  135.5 48.2 %collective-permute-start.25 = (bf16[64,2048]{1,0:T(8,128)(2,1)}, bf16[64,2048]{1,0:T(8,128)(2,1)}, u32[]{:S(2)}, u32[]{:S(2)}) collective-permute-start(bf16[64,2048]{1,0:T(8,128)(2,1)} %slice.116.refs_4_), channel_id=1, source_target_pairs={{0,1},{1,2},{2,3},{3,0},{4,5},{5,6},{6,7},{7,4},{8,9},{9,10},{10,1... | collective-permute-start | bytes 786440 | tf_op jit(solution)/shard_map/ppermute | solution.py:33
  136.7 47.0 %collective-permute-start.24 = (bf16[64,2048]{1,0:T(8,128)(2,1)}, bf16[64,2048]{1,0:T(8,128)(2,1)}, u32[]{:S(2)}, u32[]{:S(2)}) collective-permute-start(bf16[64,2048]{1,0:T(8,128)(2,1)} %slice.116.refs_4_), channel_id=1, source_target_pairs={{0,2},{1,3},{2,0},{3,1},{4,6},{5,7},{6,4},{7,5},{8,10},{9,11},{10,... | collective-permute-start | bytes 786440 | tf_op jit(solution)/shard_map/ppermute | solution.py:33
  160.2 23.5 %collective-permute-start.23 = (bf16[64,2048]{1,0:T(8,128)(2,1)}, bf16[64,2048]{1,0:T(8,128)(2,1)}, u32[]{:S(2)}, u32[]{:S(2)}) collective-permute-start(bf16[64,2048]{1,0:T(8,128)(2,1)} %slice.116.refs_4_), channel_id=1, source_target_pairs={{0,3},{1,0},{2,1},{3,2},{4,7},{5,4},{6,5},{7,6},{8,11},{9,8},{10,9... | collective-permute-start | bytes 786440 | tf_op jit(solution)/shard_map/ppermute | solution.py:33
  278.1 13.4 %collective-permute-start.29 = (bf16[3,224,1024]{2,1,0:T(8,128)(2,1)S(1)}, bf16[3,224,1024]{2,1,0:T(8,128)(2,1)S(1)}, u32[]{:S(2)}, u32[]{:S(2)}) collective-permute-start(bf16[3,224,1024]{2,1,0:T(8,128)(2,1)S(1)} %bitcast.96), channel_id=1, source_target_pairs={{0,32},{32,0},{1,33},{33,1},{2,34},{34,2},{3,35},{35,3},{4,36},{36... | collective-permute-start | bytes 4128776 | tf_op jit(solution)/shard_map/ppermute | solution.py:302
  278.3 13.2 %collective-permute-start.32 = (bf16[224,1024]{1,0:T(8,128)(2,1)S(1)}, bf16[224,1024]{1,0:T(8,128)(2,1)S(1)}, u32[]{:S(2)}, u32[]{:S(2)}) collective-permute-start(bf16[224,1024]{1,0:T(8,128)(2,1)S(1)} %fusion.2), channel_id=1, source_target_pairs={{0,64},{64,0},{1,65},{65,1},{2,66},{66,2},{3,67},{67,3},{4,68},{68... | collective-permute-start | bytes 1376264 | tf_op jit(solution)/shard_map/ppermute | solution.py:305
  278.8 22.6 %collective-permute-start.31 = (bf16[224,1024]{1,0:T(8,128)(2,1)S(1)}, bf16[224,1024]{1,0:T(8,128)(2,1)S(1)}, u32[]{:S(2)}, u32[]{:S(2)}) collective-permute-start(bf16[224,1024]{1,0:T(8,128)(2,1)S(1)} %fusion.1), channel_id=1, source_target_pairs={{0,64},{64,0},{1,65},{65,1},{2,66},{66,2},{3,67},{67,3},{4,68},{68... | collective-permute-start | bytes 1376264 | tf_op jit(solution)/shard_map/ppermute | solution.py:305
  281.3 29.9 %collective-permute-start.30 = (bf16[224,1024]{1,0:T(8,128)(2,1)S(1)}, bf16[224,1024]{1,0:T(8,128)(2,1)S(1)}, u32[]{:S(2)}, u32[]{:S(2)}) collective-permute-start(bf16[224,1024]{1,0:T(8,128)(2,1)S(1)} %fusion), channel_id=1, source_target_pairs={{0,64},{64,0},{1,65},{65,1},{2,66},{66,2},{3,67},{67,3},{4,68},{68... | collective-permute-start | bytes 1376264 | tf_op jit(solution)/shard_map/ppermute | solution.py:305
  (36 other events, 425.6 us)

commit v5 on v4

--- a/solution.py
+++ b/solution.py
@@ -202,7 +202,7 @@
     for n, p in enumerate(ps):
         ks = [[coef[12 * s + (6 if p == 2 else 0) + j] for j in range(6)] for s in range(steps)]
 
-        @pl.loop(0, rows // step_rows, unroll=2 if (rows // step_rows) % 2 == 0 else 1)
+        @pl.loop(0, rows // step_rows, unroll=7 if (rows // step_rows) % 7 == 0 else 1)
         def _(k, n=n, p=p, ks=ks):
             at = pl.ds(pl.multiple_of(k * step_rows, step_rows), step_rows)
             for low in range(0, quarter, lanes):
@@ -329,8 +329,6 @@
     marked = functools.reduce(jnp.maximum, [jnp.max(p[:, half : half + steps], axis=0) for p in pieces[0][4:]])
     coef = coefficients([marked[s] > 0 for s in range(steps)])
     pos = mine.reshape(1).astype(jnp.int32)
-    first_moment = pltpu.with_memory_space_constraint(first_moment, pltpu.HBM)
-    second_moment = pltpu.with_memory_space_constraint(second_moment, pltpu.HBM)
     at = jnp.stack([lax.axis_index("x"), lax.axis_index("y"), mine]).astype(jnp.int32)
 
     both = [partner(chunk) for chunk in far]
@@ -352,13 +350,9 @@
     arrived = []
     state = (first_moment, second_moment, w_start, parts)
     for p in (2, 0, 1):
-        if p == 2:
-            out = adam(pos, coef, *state, ((p,), (3,)))[0, 0]
-            handed = partner(out)
-            kept = adam(pos, coef, *state, ((p,), (2,)))[0, 0]
-        else:
-            pair = adam(pos, coef, *state, ((p,), (3, 2)))
-            handed, kept = partner(pair[0, 0]), pair[0, 1]
+        out = adam(pos, coef, *state, ((p,), (3,)))[0, 0]
+        handed = partner(out)
+        kept = adam(pos, coef, *state, ((p,), (2,)))[0, 0]
         joint = (kept.astype(f32) + handed.astype(f32)).astype(bf16)
         joint, pos = lax.optimization_barrier((joint, pos))
         arrived.append((p, across(joint)))

time: 313 us -> 311 us (level)
  Pallas kernels: 51.8 us -> 45.3 us
  local copies, waits for them, and re-layouts: 16 us -> 21.6 us
    pallas_call x7 -> x9, Pallas kernels: 38.5 us -> 32 us  [adam(): pl.pallas_call(functools.partial(adam_kernel, steps, ps, r_of, min(512, q...]
    unnamed x61 -> x69, local copies, waits for them, and re-layouts: 12.7 us -> 18.3 us
    ppermute x8, waiting for transfers between devices: 3.49 us -> 0.02 us  [partner(): return lax.ppermute(array, 'co', [(0, 1), (1, 0)])]
  transfers between devices with their start and end apart: 34 -> 34, of which waited for: 16 -> 14; matrix products, arithmetic and copies ran while one was open for 2% -> 2% of each run, Pallas kernels for 8% -> 8%
where the time goes in v5:
time: 311 us; the launch traced here: 310 us
  blocking collectives  95.6 us (31%)
  waiting for transfers between devices  79.2 us (25%)
  starting transfers between devices  60.7 us (20%)
  Pallas kernels  45.3 us (15%)
  local copies, waits for them, and re-layouts  21.6 us (7%)
  other arithmetic  4.66 us (1%)
  between operations  3.23 us (1%)
    all_to_all x2, blocking collectives, round_of(): lax.all_to_all(sums.reshape(-1, tok, width), FSDP, 0, 0, tiled=True)  64.1 us
    ppermute x20, waiting for transfers between devices, around(): lax.ppermute(own, dim, [(i, (i - s) % n) for i in range(n)])  57.2 us
    ppermute x20, starting transfers between devices, around(): lax.ppermute(own, dim, [(i, (i - s) % n) for i in range(n)])  32.7 us
    pallas_call x9, Pallas kernels, adam(): pl.pallas_call(functools.partial(adam_kernel, steps, ps, r_of, min(512, q...  32 us
    all_to_all x1, blocking collectives, round_of(): z = lax.all_to_all(copies, FSDP, 0, 0, tiled=True).reshape(-1, width)  31.5 us
    ppermute x5, waiting for transfers between devices, across(): return lax.ppermute(array, 'zh', [(0, 1), (1, 0)])  22 us
    unnamed x69, local copies, waits for them, and re-layouts  18.3 us
    ppermute x8, starting transfers between devices, partner(): return lax.ppermute(array, 'co', [(0, 1), (1, 0)])  15.3 us
  transfers between devices with their start and end apart: 34, of which 14 were waited for; matrix products, arithmetic and copies ran while one was open for 2% of the time, Pallas kernels for 8%

profile of v5, /device:TPU:1, one launch (start us, length us, event | category | flops | bytes accessed | tf_op | source)
XLA Modules:
  0.0 310.4 jit_solution(6797367263171746829)
XLA Ops:
  2.7 4.5 %collective-permute-start.17 = (bf16[1,224,1024]{2,1,0:T(8,128)(2,1)S(1)}, bf16[1,224,1024]{2,1,0:T(8,128)(2,1)S(1)}, u32[]{:S(2)}, u32[]{:S(2)}) collective-permute-start(bf16[1,224,1024]{2,1,0:T(8,128)(2,1)S(1)} %slice.90.refs_9_), channel_id=1, source_target_pairs={{0,64},{64,0},{1,65},{65,1},{2,66},{66,2},{3,67},{67,3},{4,68},{68... | collective-permute-start | bytes 1376264 | tf_op jit(solution)/shard_map/ppermute | solution.py:305
  10.7 7.2 %collective-permute-done.7 = s32[1,1]{1,0:T(1,128)} collective-permute-done((s32[1,1]{1,0:T(1,128)}, s32[1,1]{1,0:T(1,128)}, u32[]{:S(2)}, u32[]{:S(2)}) %collective-permute-start.7) | collective-permute-done | bytes 36 | tf_op jit(solution)/shard_map/ppermute | solution.py:33
  22.6 3.0 collective-permute-start.2
  26.4 3.6 %collective-permute-done.1 = bf16[2,8,4096]{2,1,0:T(8,128)(2,1)S(1)} collective-permute-done((bf16[2,8,4096]{2,1,0:T(8,128)(2,1)S(1)}, bf16[2,8,4096]{2,1,0:T(8,128)(2,1)S(1)}, u32[]{:S(2)}, u32[]{:S(2)}) %collective-permute-start.1) | collective-permute-done | bytes 131104 | tf_op jit(solution)/shard_map/ppermute | solution.py:33
  32.3 3.1 collective-permute-done.3
  48.4 6.7 %collective-permute-done.13.refs_7_ = bf16[64,2176]{1,0:T(8,128)(2,1)S(1)} collective-permute-done((bf16[64,2176]{1,0:T(8,128)(2,1)S(1)}, bf16[64,2176]{1,0:T(8,128)(2,1)S(1)}, u32[]{:S(2)}, u32[]{:S(2)}) %collective-permute-start.13) | collective-permute-done | bytes 278560 | tf_op jit(solution)/shard_map/ppermute | solution.py:33
  55.1 9.0 %collective-permute-start.14 = (bf16[2,224,1024]{2,1,0:T(8,128)(2,1)S(1)}, bf16[2,224,1024]{2,1,0:T(8,128)(2,1)S(1)}, u32[]{:S(2)}, u32[]{:S(2)}) collective-permute-start(bf16[2,224,1024]{2,1,0:T(8,128)(2,1)S(1)} %slice.89.refs_8_), channel_id=1, source_target_pairs={{0,32},{32,0},{1,33},{33,1},{2,34},{34,2},{3,35},{35,3},{4,36},{36... | collective-permute-start | bytes 2752520 | tf_op jit(solution)/shard_map/ppermute | solution.py:302
  67.7 3.9 %collective-permute-start.5 = (bf16[64,2048]{1,0:T(8,128)(2,1)S(1)}, bf16[64,2048]{1,0:T(8,128)(2,1)S(1)}, u32[]{:S(2)}, u32[]{:S(2)}) collective-permute-start(bf16[64,2048]{1,0:T(8,128)(2,1)S(1)} %get-tuple-element.65.refs_0_), channel_id=1, source_target_pairs={{0,16},{8,24},{16,0},{24,8},{1,17},{9,25},{17,1},{25,9},{2,18},{10... | collective-permute-start | bytes 786440 | tf_op jit(solution)/shard_map/ppermute | solution.py:33
  75.0 5.2 %collective-permute-done.5.refs_2_ = bf16[64,2048]{1,0:T(8,128)(2,1)S(1)} collective-permute-done((bf16[64,2048]{1,0:T(8,128)(2,1)S(1)}, bf16[64,2048]{1,0:T(8,128)(2,1)S(1)}, u32[]{:S(2)}, u32[]{:S(2)}) %collective-permute-start.5) | collective-permute-done | bytes 262176 | tf_op jit(solution)/shard_map/ppermute | solution.py:33
  82.9 3.2 %forward0.1 = (bf16[256,4096]{1,0:T(8,128)(2,1)S(1)}, f32[224,256]{1,0:T(8,128)S(1)}, f32[224,256]{1,0:T(8,128)S(1)}, bf16[224,256]{1,0:T(8,128)(2,1)S(1)}, bf16...) custom-call(s32[3]{0:T(128)S(1)} %pad_add_fusion.at_ref, ...), custom_call_target="tpu_custom_call" | custom-call | flops 1409286144 | bytes 8388608 | tf_op jit(solution)/shard_map/forward0/pallas_call | solution.py:113
  88.6 34.1 %all_to_all.20.parts_ref = bf16[32,8,4096]{2,1,0:T(8,128)(2,1)S(1)} all-to-all(bf16[32,8,4096]{2,1,0:T(8,128)(2,1)S(1)} %bitcast.94), channel_id=1, replica_groups=mesh['zh'=2,'co'=2,'x'=4,'zl'=2,'y'=4] {'x','y','zl'}, dimensions={0} | all-to-all | bytes 4194304 | tf_op jit(solution)/shard_map/all_to_all | solution.py:344
  124.5 4.5 %all-to-all-start.1 = ((bf16[32,8,4096]{2,1,0:T(8,128)(2,1)}), bf16[32,8,4096]{2,1,0:T(8,128)(2,1)S(1)}, u32[]{:S(2)}, u32[]{:S(2)}) async-start(bf16[32,8,4096]{2,1,0:T(8,128)(2,1)} %copy-done.8), calls=%async_computation.1 | async-start | bytes 4194304 | tf_op jit(solution)/shard_map/all_to_all | solution.py:346
  139.1 20.4 %collective-permute-done.22.refs_3_ = bf16[64,2048]{1,0:T(8,128)(2,1)S(1)} collective-permute-done((bf16[64,2048]{1,0:T(8,128)(2,1)}, bf16[64,2048]{1,0:T(8,128)(2,1)S(1)}, u32[]{:S(2)}, u32[]{:S(2)}) %collective-permute-start.22) | collective-permute-done | bytes 262176 | tf_op jit(solution)/shard_map/ppermute | solution.py:33
  160.2 3.2 %collective-permute-start.23 = (bf16[64,2048]{1,0:T(8,128)(2,1)}, bf16[64,2048]{1,0:T(8,128)(2,1)}, u32[]{:S(2)}, u32[]{:S(2)}) collective-permute-start(bf16[64,2048]{1,0:T(8,128)(2,1)} %slice.100.refs_4_), channel_id=1, source_target_pairs={{0,3},{1,0},{2,1},{3,2},{4,7},{5,4},{6,5},{7,6},{8,11},{9,8},{10,9... | collective-permute-start | bytes 786440 | tf_op jit(solution)/shard_map/ppermute | solution.py:33
  176.7 10.4 %shard_map.158.refs_8_.w_ref = bf16[3,4,224,1024]{3,2,1,0:T(8,128)(2,1)S(1)} custom-call(s32[1]{0:T(128)} %bitcast.pos, f32[24]{0:T(128)S(1)} %pad_maximum_fusion.4.coef, bf16[1,3,224,4096]{3,2,1,0:T(8,128)(2,1)S(1)} %copy-done.2, bf16[1,3,224,4096]{3,2,1,0:T(8,128)(2,1)S(1)} %copy-done.3, bf16[3,4,224,1024]{3,2,1,0:T(8,128)(2,1)S(1)} %bitcast.72, ...), custom_call_target="tpu_custom_call" | custom-call | flops 1409286144 | bytes 22020096 | tf_op jit(solution)/shard_map/pallas_call | solution.py:233
  187.2 3.6 %forward1.1 = (bf16[256,4096]{1,0:T(8,128)(2,1)S(1)}, f32[224,256]{1,0:T(8,128)S(1)}, f32[224,256]{1,0:T(8,128)S(1)}, bf16[224,256]{1,0:T(8,128)(2,1)S(1)}, bf16[256,4096]{1,0:T(8,128)(2,1)S(1)}) custom-call(s32[3]{0:T(128)S(1)} %pad_add_fusion.at_ref, bf16[64,2048]{1,0:T(8,128)(2,1)S(1)} %copy-done.9, bf16[64,2048]{1,0:T(8,128)(2,1)} %collective-permute-done.20.refs_1_, ...), custom_call_target="tpu_custom_call" | custom-call | flops 1409286144 | bytes 8388608 | tf_op jit(solution)/shard_map/forward1/pallas_call | solution.py:113
  190.8 30.0 %all_to_all.21.parts_ref = bf16[32,8,4096]{2,1,0:T(8,128)(2,1)S(1)} all-to-all(bf16[32,8,4096]{2,1,0:T(8,128)(2,1)S(1)} %bitcast.95), channel_id=1, replica_groups=mesh['zh'=2,'co'=2,'x'=4,'zl'=2,'y'=4] {'x','y','zl'}, dimensions={0} | all-to-all | bytes 4194304 | tf_op jit(solution)/shard_map/all_to_all | solution.py:344
  221.3 31.5 %all_to_all.22 = bf16[32,8,4096]{2,1,0:T(8,128)(2,1)S(1)} all-to-all(bf16[32,8,4096]{2,1,0:T(8,128)(2,1)S(1)} %own_slopes.3), channel_id=1, replica_groups=mesh['zh'=2,'co'=2,'x'=4,'zl'=2,'y'=4] {'x','y','zl'}, dimensions={0} | all-to-all | bytes 4194304 | tf_op jit(solution)/shard_map/all_to_all | solution.py:346
  256.1 3.5 %collective-permute-start.26 = (bf16[224,1024]{1,0:T(8,128)(2,1)S(1)}, bf16[224,1024]{1,0:T(8,128)(2,1)S(1)}, u32[]{:S(2)}, u32[]{:S(2)}) collective-permute-start(bf16[224,1024]{1,0:T(8,128)(2,1)S(1)} %bitcast.97), channel_id=1, source_target_pairs={{0,32},{32,0},{1,33},{33,1},{2,34},{34,2},{3,35},{35,3},{4,36},{36... | collective-permute-start | bytes 1376264 | tf_op jit(solution)/shard_map/ppermute | solution.py:302
  271.3 4.7 %shard_map.166 = bf16[3,1,224,1024]{3,2,1,0:T(8,128)(2,1)S(1)} custom-call(s32[1]{0:T(128)} %bitcast.pos, f32[24]{0:T(128)S(1)} %pad_maximum_fusion.4.coef, bf16[1,3,224,4096]{3,2,1,0:T(8,128)(2,1)S(1)} %bitcast.74, bf16[1,3,224,4096]{3,2,1,0:T(8,128)(2,1)S(1)} %copy-done.3, bf16[3,4,224,1024]{3,2,1,0:T(8,128)(2,1)S(1)} %bitcast.72, ...), custom_call_target="tpu_custom_call" | custom-call | flops 704643072 | bytes 5505024 | tf_op jit(solution)/shard_map/pallas_call | solution.py:233
  279.6 4.7 %shard_map.165.own_ref = bf16[3,1,224,1024]{3,2,1,0:T(8,128)(2,1)S(1)} custom-call(s32[1]{0:T(128)} %bitcast.pos, f32[24]{0:T(128)S(1)} %pad_maximum_fusion.4.coef, bf16[1,3,224,4096]{3,2,1,0:T(8,128)(2,1)S(1)} %bitcast.74, bf16[1,3,224,4096]{3,2,1,0:T(8,128)(2,1)S(1)} %copy-done.3, bf16[3,4,224,1024]{3,2,1,0:T(8,128)(2,1)S(1)} %bitcast.72, ...), custom_call_target="tpu_custom_call" | custom-call | flops 704643072 | bytes 5505024 | tf_op jit(solution)/shard_map/pallas_call | solution.py:233
  284.3 5.0 %collective-permute-done.32.far_ref = bf16[224,1024]{1,0:T(8,128)(2,1)S(1)} collective-permute-done((bf16[224,1024]{1,0:T(8,128)(2,1)S(1)}, bf16[224,1024]{1,0:T(8,128)(2,1)S(1)}, u32[]{:S(2)}, u32[]{:S(2)}) %collective-permute-start.32) | collective-permute-done | bytes 458784 | tf_op jit(solution)/shard_map/ppermute | solution.py:305
  290.7 8.4 %collective-permute-done.31.far_ref = bf16[224,1024]{1,0:T(8,128)(2,1)S(1)} collective-permute-done((bf16[224,1024]{1,0:T(8,128)(2,1)S(1)}, bf16[224,1024]{1,0:T(8,128)(2,1)S(1)}, u32[]{:S(2)}, u32[]{:S(2)}) %collective-permute-start.31) | collective-permute-done | bytes 458784 | tf_op jit(solution)/shard_map/ppermute | solution.py:305
  300.5 8.5 %collective-permute-done.30.far_ref = bf16[224,1024]{1,0:T(8,128)(2,1)S(1)} collective-permute-done((bf16[224,1024]{1,0:T(8,128)(2,1)S(1)}, bf16[224,1024]{1,0:T(8,128)(2,1)S(1)}, u32[]{:S(2)}, u32[]{:S(2)}) %collective-permute-start.30) | collective-permute-done | bytes 458784 | tf_op jit(solution)/shard_map/ppermute | solution.py:305
  (171 shorter events, 85.2 us)
Async XLA Ops:
  2.7 45.2 %collective-permute-start.17 = (bf16[1,224,1024]{2,1,0:T(8,128)(2,1)S(1)}, bf16[1,224,1024]{2,1,0:T(8,128)(2,1)S(1)}, u32[]{:S(2)}, u32[]{:S(2)}) collective-permute-start(bf16[1,224,1024]{2,1,0:T(8,128)(2,1)S(1)} %slice.90.refs_9_), channel_id=1, source_target_pairs={{0,64},{64,0},{1,65},{65,1},{2,66},{66,2},{3,67},{67,3},{4,68},{68... | collective-permute-start | bytes 1376264 | tf_op jit(solution)/shard_map/ppermute | solution.py:305
  7.2 60.5 %collective-permute-start.15 = (bf16[1,224,1024]{2,1,0:T(8,128)(2,1)S(1)}, bf16[1,224,1024]{2,1,0:T(8,128)(2,1)S(1)}, u32[]{:S(2)}, u32[]{:S(2)}) collective-permute-start(bf16[1,224,1024]{2,1,0:T(8,128)(2,1)S(1)} %slice.90.refs_9_), channel_id=1, source_target_pairs={{0,32},{32,0},{1,33},{33,1},{2,34},{34,2},{3,35},{35,3},{4,36},{36... | collective-permute-start | bytes 1376264 | tf_op jit(solution)/shard_map/ppermute | solution.py:302
  8.2 9.7 %collective-permute-start.7 = (s32[1,1]{1,0:T(1,128)}, s32[1,1]{1,0:T(1,128)}, u32[]{:S(2)}, u32[]{:S(2)}) collective-permute-start(s32[1,1]{1,0:T(1,128)} %param.21), channel_id=1, source_target_pairs={{0,4},{4,0},{1,5},{5,1},{2,6},{6,2},{3,7},{7,3},{8,12},{12,8},{9,1... | collective-permute-start | bytes 20 | tf_op jit(solution)/shard_map/ppermute | solution.py:33
  8.9 11.8 %collective-permute-start = (bf16[2,8,4096]{2,1,0:T(8,128)(2,1)S(1)}, bf16[2,8,4096]{2,1,0:T(8,128)(2,1)S(1)}, u32[]{:S(2)}, u32[]{:S(2)}) collective-permute-start(bf16[2,8,4096]{2,1,0:T(8,128)(2,1)S(1)} %copy-done.19), channel_id=1, source_target_pairs={{0,4},{4,0},{1,5},{5,1},{2,6},{6,2},{3,7},{7,3},{8,12},{12,8},{9,1... | collective-permute-start | bytes 393224 | tf_op jit(solution)/shard_map/ppermute | solution.py:33
  9.7 54.4 %collective-permute-start.16 = (bf16[2,224,1024]{2,1,0:T(8,128)(2,1)S(1)}, bf16[2,224,1024]{2,1,0:T(8,128)(2,1)S(1)}, u32[]{:S(2)}, u32[]{:S(2)}) collective-permute-start(bf16[2,224,1024]{2,1,0:T(8,128)(2,1)S(1)} %slice.89.refs_8_), channel_id=1, source_target_pairs={{0,64},{64,0},{1,65},{65,1},{2,66},{66,2},{3,67},{67,3},{4,68},{68... | collective-permute-start | bytes 2752520 | tf_op jit(solution)/shard_map/ppermute | solution.py:305
  31.0 14.2 %collective-permute-start.10 = (bf16[2,8,4224]{2,1,0:T(8,128)(2,1)S(1)}, bf16[2,8,4224]{2,1,0:T(8,128)(2,1)S(1)}, u32[]{:S(2)}, u32[]{:S(2)}) collective-permute-start(bf16[2,8,4224]{2,1,0:T(8,128)(2,1)S(1)} %get-tuple-element.63), channel_id=1, source_target_pairs={{0,8},{8,16},{16,24},{24,0},{1,9},{9,17},{17,25},{25,1},{2,10},{10... | collective-permute-start | bytes 405512 | tf_op jit(solution)/shard_map/ppermute | solution.py:33
  45.4 9.7 %collective-permute-start.13 = (bf16[64,2176]{1,0:T(8,128)(2,1)S(1)}, bf16[64,2176]{1,0:T(8,128)(2,1)S(1)}, u32[]{:S(2)}, u32[]{:S(2)}) collective-permute-start(bf16[64,2176]{1,0:T(8,128)(2,1)S(1)} %slice.88.refs_4_), channel_id=1, source_target_pairs={{0,1},{1,2},{2,3},{3,0},{4,5},{5,6},{6,7},{7,4},{8,9},{9,10},{10,1... | collective-permute-start | bytes 835592 | tf_op jit(solution)/shard_map/ppermute | solution.py:33
  45.5 18.6 %collective-permute-start.12 = (bf16[64,2176]{1,0:T(8,128)(2,1)S(1)}, bf16[64,2176]{1,0:T(8,128)(2,1)S(1)}, u32[]{:S(2)}, u32[]{:S(2)}) collective-permute-start(bf16[64,2176]{1,0:T(8,128)(2,1)S(1)} %slice.88.refs_4_), channel_id=1, source_target_pairs={{0,2},{1,3},{2,0},{3,1},{4,6},{5,7},{6,4},{7,5},{8,10},{9,11},{10,... | collective-permute-start | bytes 835592 | tf_op jit(solution)/shard_map/ppermute | solution.py:33
  47.9 17.0 %collective-permute-start.11 = (bf16[64,2176]{1,0:T(8,128)(2,1)S(1)}, bf16[64,2176]{1,0:T(8,128)(2,1)S(1)}, u32[]{:S(2)}, u32[]{:S(2)}) collective-permute-start(bf16[64,2176]{1,0:T(8,128)(2,1)S(1)} %slice.88.refs_4_), channel_id=1, source_target_pairs={{0,3},{1,0},{2,1},{3,2},{4,7},{5,4},{6,5},{7,6},{8,11},{9,8},{10,9... | collective-permute-start | bytes 835592 | tf_op jit(solution)/shard_map/ppermute | solution.py:33
  55.1 27.9 %collective-permute-start.14 = (bf16[2,224,1024]{2,1,0:T(8,128)(2,1)S(1)}, bf16[2,224,1024]{2,1,0:T(8,128)(2,1)S(1)}, u32[]{:S(2)}, u32[]{:S(2)}) collective-permute-start(bf16[2,224,1024]{2,1,0:T(8,128)(2,1)S(1)} %slice.89.refs_8_), channel_id=1, source_target_pairs={{0,32},{32,0},{1,33},{33,1},{2,34},{34,2},{3,35},{35,3},{4,36},{36... | collective-permute-start | bytes 2752520 | tf_op jit(solution)/shard_map/ppermute | solution.py:302
  64.0 18.9 %collective-permute-start.18 = (bf16[2,224,1024]{2,1,0:T(8,128)(2,1)S(1)}, bf16[2,224,1024]{2,1,0:T(8,128)(2,1)S(1)}, u32[]{:S(2)}, u32[]{:S(2)}) collective-permute-start(bf16[2,224,1024]{2,1,0:T(8,128)(2,1)S(1)} %collective-permute-done.16.refs_12_), channel_id=1, source_target_pairs={{0,32},{32,0},{1,33},{33,1},{2,34},{34,2},{3,35},{35,3},{4,36},{36... | collective-permute-start | bytes 2752520 | tf_op jit(solution)/shard_map/ppermute | solution.py:302
  64.9 18.0 %collective-permute-start.19 = (bf16[1,224,1024]{2,1,0:T(8,128)(2,1)S(1)}, bf16[1,224,1024]{2,1,0:T(8,128)(2,1)S(1)}, u32[]{:S(2)}, u32[]{:S(2)}) collective-permute-start(bf16[1,224,1024]{2,1,0:T(8,128)(2,1)S(1)} %collective-permute-done.17.refs_13_), channel_id=1, source_target_pairs={{0,32},{32,0},{1,33},{33,1},{2,34},{34,2},{3,35},{35,3},{4,36},{36... | collective-permute-start | bytes 1376264 | tf_op jit(solution)/shard_map/ppermute | solution.py:302
  67.7 12.5 %collective-permute-start.5 = (bf16[64,2048]{1,0:T(8,128)(2,1)S(1)}, bf16[64,2048]{1,0:T(8,128)(2,1)S(1)}, u32[]{:S(2)}, u32[]{:S(2)}) collective-permute-start(bf16[64,2048]{1,0:T(8,128)(2,1)S(1)} %get-tuple-element.65.refs_0_), channel_id=1, source_target_pairs={{0,16},{8,24},{16,0},{24,8},{1,17},{9,25},{17,1},{25,9},{2,18},{10... | collective-permute-start | bytes 786440 | tf_op jit(solution)/shard_map/ppermute | solution.py:33
  124.5 38.9 %all-to-all-start.1 = ((bf16[32,8,4096]{2,1,0:T(8,128)(2,1)}), bf16[32,8,4096]{2,1,0:T(8,128)(2,1)S(1)}, u32[]{:S(2)}, u32[]{:S(2)}) async-start(bf16[32,8,4096]{2,1,0:T(8,128)(2,1)} %copy-done.8), calls=%async_computation.1 | async-start | bytes 4194304 | tf_op jit(solution)/shard_map/all_to_all | solution.py:346
  128.9 30.5 %collective-permute-start.22 = (bf16[64,2048]{1,0:T(8,128)(2,1)}, bf16[64,2048]{1,0:T(8,128)(2,1)S(1)}, u32[]{:S(2)}, u32[]{:S(2)}) collective-permute-start(bf16[64,2048]{1,0:T(8,128)(2,1)} %get-tuple-element.64.refs_0_), channel_id=1, source_target_pairs={{0,8},{8,16},{16,24},{24,0},{1,9},{9,17},{17,25},{25,1},{2,10},{10... | collective-permute-start | bytes 786440 | tf_op jit(solution)/shard_map/ppermute | solution.py:33
  130.2 56.9 %collective-permute-start.21 = (bf16[64,2048]{1,0:T(8,128)(2,1)}, bf16[64,2048]{1,0:T(8,128)(2,1)}, u32[]{:S(2)}, u32[]{:S(2)}) collective-permute-start(bf16[64,2048]{1,0:T(8,128)(2,1)} %get-tuple-element.64.refs_0_), channel_id=1, source_target_pairs={{0,16},{8,24},{16,0},{24,8},{1,17},{9,25},{17,1},{25,9},{2,18},{10... | collective-permute-start | bytes 786440 | tf_op jit(solution)/shard_map/ppermute | solution.py:33
  132.7 54.4 %collective-permute-start.20 = (bf16[64,2048]{1,0:T(8,128)(2,1)}, bf16[64,2048]{1,0:T(8,128)(2,1)}, u32[]{:S(2)}, u32[]{:S(2)}) collective-permute-start(bf16[64,2048]{1,0:T(8,128)(2,1)} %get-tuple-element.64.refs_0_), channel_id=1, source_target_pairs={{0,24},{8,0},{16,8},{24,16},{1,25},{9,1},{17,9},{25,17},{2,26},{10... | collective-permute-start | bytes 786440 | tf_op jit(solution)/shard_map/ppermute | solution.py:33
  135.5 51.6 %collective-permute-start.25 = (bf16[64,2048]{1,0:T(8,128)(2,1)}, bf16[64,2048]{1,0:T(8,128)(2,1)}, u32[]{:S(2)}, u32[]{:S(2)}) collective-permute-start(bf16[64,2048]{1,0:T(8,128)(2,1)} %slice.100.refs_4_), channel_id=1, source_target_pairs={{0,1},{1,2},{2,3},{3,0},{4,5},{5,6},{6,7},{7,4},{8,9},{9,10},{10,1... | collective-permute-start | bytes 786440 | tf_op jit(solution)/shard_map/ppermute | solution.py:33
  136.7 50.5 %collective-permute-start.24 = (bf16[64,2048]{1,0:T(8,128)(2,1)}, bf16[64,2048]{1,0:T(8,128)(2,1)}, u32[]{:S(2)}, u32[]{:S(2)}) collective-permute-start(bf16[64,2048]{1,0:T(8,128)(2,1)} %slice.100.refs_4_), channel_id=1, source_target_pairs={{0,2},{1,3},{2,0},{3,1},{4,6},{5,7},{6,4},{7,5},{8,10},{9,11},{10,... | collective-permute-start | bytes 786440 | tf_op jit(solution)/shard_map/ppermute | solution.py:33
  160.2 27.0 %collective-permute-start.23 = (bf16[64,2048]{1,0:T(8,128)(2,1)}, bf16[64,2048]{1,0:T(8,128)(2,1)}, u32[]{:S(2)}, u32[]{:S(2)}) collective-permute-start(bf16[64,2048]{1,0:T(8,128)(2,1)} %slice.100.refs_4_), channel_id=1, source_target_pairs={{0,3},{1,0},{2,1},{3,2},{4,7},{5,4},{6,5},{7,6},{8,11},{9,8},{10,9... | collective-permute-start | bytes 786440 | tf_op jit(solution)/shard_map/ppermute | solution.py:33
  276.0 13.3 %collective-permute-start.29 = (bf16[3,224,1024]{2,1,0:T(8,128)(2,1)S(1)}, bf16[3,224,1024]{2,1,0:T(8,128)(2,1)S(1)}, u32[]{:S(2)}, u32[]{:S(2)}) collective-permute-start(bf16[3,224,1024]{2,1,0:T(8,128)(2,1)S(1)} %bitcast.96), channel_id=1, source_target_pairs={{0,32},{32,0},{1,33},{33,1},{2,34},{34,2},{3,35},{35,3},{4,36},{36... | collective-permute-start | bytes 4128776 | tf_op jit(solution)/shard_map/ppermute | solution.py:302
  276.1 13.2 %collective-permute-start.32 = (bf16[224,1024]{1,0:T(8,128)(2,1)S(1)}, bf16[224,1024]{1,0:T(8,128)(2,1)S(1)}, u32[]{:S(2)}, u32[]{:S(2)}) collective-permute-start(bf16[224,1024]{1,0:T(8,128)(2,1)S(1)} %fusion.2), channel_id=1, source_target_pairs={{0,64},{64,0},{1,65},{65,1},{2,66},{66,2},{3,67},{67,3},{4,68},{68... | collective-permute-start | bytes 1376264 | tf_op jit(solution)/shard_map/ppermute | solution.py:305
  276.6 22.5 %collective-permute-start.31 = (bf16[224,1024]{1,0:T(8,128)(2,1)S(1)}, bf16[224,1024]{1,0:T(8,128)(2,1)S(1)}, u32[]{:S(2)}, u32[]{:S(2)}) collective-permute-start(bf16[224,1024]{1,0:T(8,128)(2,1)S(1)} %fusion.1), channel_id=1, source_target_pairs={{0,64},{64,0},{1,65},{65,1},{2,66},{66,2},{3,67},{67,3},{4,68},{68... | collective-permute-start | bytes 1376264 | tf_op jit(solution)/shard_map/ppermute | solution.py:305
  279.1 29.9 %collective-permute-start.30 = (bf16[224,1024]{1,0:T(8,128)(2,1)S(1)}, bf16[224,1024]{1,0:T(8,128)(2,1)S(1)}, u32[]{:S(2)}, u32[]{:S(2)}) collective-permute-start(bf16[224,1024]{1,0:T(8,128)(2,1)S(1)} %fusion), channel_id=1, source_target_pairs={{0,64},{64,0},{1,65},{65,1},{2,66},{66,2},{3,67},{67,3},{4,68},{68... | collective-permute-start | bytes 1376264 | tf_op jit(solution)/shard_map/ppermute | solution.py:305
  (40 other events, 477.5 us)
